TPU v7x, 16 devices: a whole 2x2x2 slice. The times are simulated.
16 devices in a mesh: dp: 2 (over z), tp: 8 (over y, x, core).
Axes of the slice: x: 2, y: 2, z: 2, core: 2. Of those that a mesh axis runs over, the one named last changes fastest.
Arguments:
- token_ids: int32 [16384], P('dp'), parts along dimension 0
- positions: int32 [16384], P('dp'), parts along dimension 0
- embed_table: bfloat16 [256000, 2304], P('tp')
- norm_scale: float32 [2304], replicated
- w_query: bfloat16 [2304, 2048], P(None, 'tp')
- w_key: bfloat16 [2304, 1024], replicated
- w_value: bfloat16 [2304, 1024], replicated
Outputs:
- output 1: bfloat16 [16384, 2304], P(('dp', 'tp')), parts along dimension 0
- output 2: bfloat16 [16384, 8, 256], P('dp', 'tp'), parts along dimension 0
- output 3: bfloat16 [16384, 8, 256], P('dp', 'tp'), parts along dimension 0
- output 4: bfloat16 [16384, 8, 256], P('dp', 'tp'), parts along dimension 0
There are 2 independent parts. A program takes and returns all parts, laid end to end along the dimension named above; an argument that names none is the same for every part.
All inputs are finite; a program needn't handle non-finite values.
Results may differ from a plain program's by a relative error of at most 0.0120345.
Values are sent between devices in bfloat16 or wider.
A program may use at most 1 GiB of HBM per device.

v0:
```python
import functools
import math
import jax
import jax.numpy as jnp
from jax import lax
from jax.experimental import pallas as pl
from jax.experimental.pallas import tpu as pltpu
from jax.sharding import PartitionSpec as P

HEAD_DIM = 256
EPSILON = 1e-6
ROPE_BASE = 10000.0
TILE = 128
CHUNKS = 4
SEND_ROWS = 512
CHIPS = 4
MESH_IDS = pl.DeviceIdType.MESH


def rope_tables(positions):
    inv_freq = ROPE_BASE ** (-jnp.arange(0, HEAD_DIM, 2, dtype=jnp.float32) / HEAD_DIM)
    angles = positions.astype(jnp.float32)[:, None] * inv_freq[None, :]
    return jnp.cos(angles), jnp.sin(angles)


def gather_kernel(tiles, width, pair_ids, counts, cols_ref, table_ref, *rest):
    out_ref, pairs, sems = rest[-3:]
    step = pl.program_id(0)
    normalizer = jnp.asarray(math.sqrt(width), dtype=jnp.bfloat16)

    def start(tile, slot):
        @pl.loop(0, TILE, unroll=8)
        def _(row):
            src = pair_ids[tile * TILE + row]

            @pl.when(src >= 0)
            def _():
                pltpu.make_async_copy(table_ref.at[pl.ds(pl.multiple_of(src, 2), 2), :], pairs.at[slot, pl.ds(pl.multiple_of(2 * row, 2), 2), :], sems.at[slot]).start()

    def wait(tile, slot):
        count = counts[tile]
        size = TILE
        while size:
            @pl.when((count // size) % 2 == 1)
            def _():
                pltpu.make_async_copy(table_ref.at[pl.ds(0, 2 * size), :], pairs.at[slot, pl.ds(0, 2 * size), :], sems.at[slot]).wait()

            size //= 2

    @pl.when(step == 0)
    def _():
        pairs[...] = jnp.zeros_like(pairs)
        start(0, 0)
        start(1, 1)

    slot = lax.rem(step, 3)

    @pl.when(step + 2 < tiles)
    def _():
        start(step + 2, lax.rem(step + 2, 3))

    wait(step, slot)
    lanes = lax.broadcasted_iota(jnp.int32, (TILE, 2 * TILE), 1)
    select = jnp.where(lanes == cols_ref[...], normalizer, jnp.zeros((), jnp.bfloat16))
    for piece in range(width // 256):
        cols = pl.ds(piece * 256, 256)
        picked = jnp.dot(select, pairs[slot, :, cols], preferred_element_type=jnp.float32)
        out_ref[:, cols] = picked.astype(jnp.bfloat16)


def gather_rows(pair_ids, counts, cols, table_rows, after):
    count = cols.shape[0]
    width = table_rows.shape[1]
    tiles = count // TILE
    anywhere = pl.BlockSpec(memory_space=pl.ANY)
    grid_spec = pltpu.PrefetchScalarGridSpec(
        num_scalar_prefetch=2,
        grid=(tiles,),
        in_specs=[pl.BlockSpec((TILE, 1), lambda i, *_: (i, 0)), anywhere] + [anywhere] * len(after),
        out_specs=pl.BlockSpec((TILE, width), lambda i, *_: (i, 0)),
        scratch_shapes=[pltpu.VMEM((3, 2 * TILE, width), jnp.bfloat16), pltpu.SemaphoreType.DMA((3,))],
    )
    return pl.pallas_call(
        functools.partial(gather_kernel, tiles, width),
        grid_spec=grid_spec,
        out_shape=jax.ShapeDtypeStruct((count, width), jnp.bfloat16),
        compiler_params=pltpu.CompilerParams(dimension_semantics=("arbitrary",)),
        cost_estimate=pl.CostEstimate(flops=count * 20_000_000, bytes_accessed=count * width * 6, transcendentals=0),
        name="gather_rows",
    )(pair_ids, counts, cols, table_rows, *after)


def heads_kernel(rows, resid_ref, gain_ref, cos_ref, sin_ref, wq_hbm, wk_hbm, wv_hbm, q_out, kv_out,
                 wq, wk, wv, normed, q_stage, kv_stage, w_sem, q_send, q_recv, kv_send, kv_recv,
                 own_recv, fwd_send, fwd_recv, keep_sem):
    group = lax.axis_index("dp")
    me = lax.axis_index("tp")
    core = lax.rem(me, 2)
    chip = me // 2
    partner = me + 1 - 2 * core
    tiles = rows // SEND_ROWS
    half = HEAD_DIM // 2

    loads = [pltpu.make_async_copy(src, dst, w_sem.at[n]) for n, (src, dst) in enumerate(((wk_hbm, wk), (wv_hbm, wv), (wq_hbm, wq)))]
    for load in loads:
        load.start()

    barrier = pltpu.get_barrier_semaphore()
    for step in range(1, 2 * CHIPS):
        pl.semaphore_signal(barrier, inc=1, device_id=(group, lax.rem(me + step, 2 * CHIPS)), device_id_type=MESH_IDS)

    @pl.loop(0, rows // 128)
    def _(part):
        span = pl.ds(pl.multiple_of(part * 128, 128), 128)
        widened = resid_ref[span, :].astype(jnp.float32)
        inv_rms = lax.rsqrt(jnp.mean(widened * widened, axis=-1, keepdims=True) + EPSILON)
        normed[span, :] = (widened * inv_rms * gain_ref[...]).astype(jnp.bfloat16)

    pl.semaphore_wait(barrier, 2 * CHIPS - 1)
    for load in loads:
        load.wait()

    def block(source, tile):
        return pl.ds(pl.multiple_of(source * rows + tile * SEND_ROWS, SEND_ROWS), SEND_ROWS)

    def whole(source):
        return pl.ds(pl.multiple_of(source * rows, rows), rows)

    def remote(src, dst, send, recv, device):
        return pltpu.make_async_remote_copy(src_ref=src, dst_ref=dst, send_sem=send, recv_sem=recv, device_id=(group, device), device_id_type=MESH_IDS)

    def rotated(linear, span, factor):
        front = linear[:, :half]
        back = linear[:, half:]
        cosines = cos_ref[span, :]
        sines = sin_ref[span, :]
        return jnp.concatenate([((front * cosines - back * sines) * factor).astype(jnp.bfloat16), ((back * cosines + front * sines) * factor).astype(jnp.bfloat16)], axis=-1)

    @pl.loop(0, CHIPS * tiles)
    def _(turn):
        offset = lax.rem(turn // tiles + 1, CHIPS)
        tile = lax.rem(turn, tiles)
        there = lax.rem(chip + offset, CHIPS)
        columns = pl.ds(pl.multiple_of(there * HEAD_DIM, HEAD_DIM), HEAD_DIM)
        sent = pl.ds(pl.multiple_of(tile * SEND_ROWS, SEND_ROWS), SEND_ROWS)

        @pl.loop(0, SEND_ROWS // 256)
        def _(part):
            span = pl.ds(pl.multiple_of(tile * SEND_ROWS + part * 256, 256), 256)
            lhs = normed[span, :]

            def linear(weight):
                return jnp.dot(lhs, weight, preferred_element_type=jnp.float32).astype(jnp.bfloat16)

            kv_stage[0, there, span, :] = rotated(linear(wk[:, columns]).astype(jnp.float32), span, 1.0)
            kv_stage[1, there, span, :] = linear(wv[:, columns])
            for side in range(2):
                q_stage[2 * there + side, span, :] = rotated(linear(wq[2 * there + side]).astype(jnp.float32), span, HEAD_DIM ** -0.5)

        @pl.when(offset != 0)
        def _():
            for side in range(2):
                remote(kv_stage.at[side, there, sent, :], kv_out.at[side, block(me, tile), :], kv_send.at[offset, side], kv_recv.at[offset, core, tile], 2 * there + side).start()
            for side in range(2):
                remote(q_stage.at[2 * there + side, sent, :], q_out.at[block(me, tile), :], q_send.at[offset, side], q_recv.at[offset, core], 2 * there + side).start()

    for side in range(2):
        remote(kv_stage.at[side, chip], kv_out.at[side, whole(me), :], kv_send.at[0, side], own_recv.at[side], partner).start()
    remote(q_stage.at[partner], q_out.at[whole(me), :], q_send.at[0, 0], q_recv.at[0, 0], partner).start()
    keeps = [pltpu.make_async_copy(q_stage.at[me], q_out.at[whole(me), :], keep_sem.at[0])]
    for side in range(2):
        keeps.append(pltpu.make_async_copy(kv_stage.at[side, chip], kv_out.at[side, whole(me), :], keep_sem.at[1 + side]))
    for keep in keeps:
        keep.start()

    for tile in range(tiles):
        for offset in range(1, CHIPS):
            for side in range(2):
                source = 2 * lax.rem(chip + CHIPS - offset, CHIPS) + side
                region = kv_out.at[core, block(source, tile), :]
                remote(region, region, kv_send.at[offset, side], kv_recv.at[offset, side, tile], partner).wait_recv()
                remote(region, region, fwd_send.at[offset, side], fwd_recv.at[offset, side], partner).start()

    for keep in keeps:
        keep.wait()
    for offset in range(1, CHIPS):
        there = lax.rem(chip + offset, CHIPS)
        for side in range(2):
            source = 2 * lax.rem(chip + CHIPS - offset, CHIPS) + side
            remote(kv_stage.at[side, there], kv_out.at[side, whole(me), :], kv_send.at[offset, side], own_recv.at[side], partner).wait_send()
            remote(q_stage.at[2 * there + side], q_out.at[whole(source), :], q_send.at[offset, side], q_recv.at[offset, side], partner).wait()
            mine = kv_out.at[core, whole(source), :]
            remote(mine, mine, fwd_send.at[offset, side], fwd_recv.at[offset, side], partner).wait_send()
            other = kv_out.at[1 - core, whole(source), :]
            remote(other, other, fwd_send.at[offset, side], fwd_recv.at[offset, side], partner).wait_recv()
    for side in range(2):
        remote(kv_stage.at[side, chip], kv_out.at[side, whole(partner), :], kv_send.at[0, side], own_recv.at[side], partner).wait()
    remote(q_stage.at[partner], q_out.at[whole(partner), :], q_send.at[0, 0], q_recv.at[0, 0], partner).wait()


def project_heads(residual, gain, cosines, sines, wq_all, w_key, w_value):
    rows, width = residual.shape
    heads = wq_all.shape[0]
    tokens = rows * heads
    tiles = rows // SEND_ROWS
    vmem = pl.BlockSpec(memory_space=pltpu.VMEM)
    anywhere = pl.BlockSpec(memory_space=pl.ANY)
    dma = pltpu.SemaphoreType.DMA
    return pl.pallas_call(
        functools.partial(heads_kernel, rows),
        out_shape=(jax.ShapeDtypeStruct((tokens, HEAD_DIM), jnp.bfloat16), jax.ShapeDtypeStruct((2, tokens, HEAD_DIM), jnp.bfloat16)),
        in_specs=[vmem, vmem, vmem, vmem, anywhere, anywhere, anywhere],
        out_specs=(anywhere, anywhere),
        scratch_shapes=[
            pltpu.VMEM(wq_all.shape, jnp.bfloat16),
            pltpu.VMEM(w_key.shape, jnp.bfloat16),
            pltpu.VMEM(w_value.shape, jnp.bfloat16),
            pltpu.VMEM((rows, width), jnp.bfloat16),
            pltpu.VMEM((heads, rows, HEAD_DIM), jnp.bfloat16),
            pltpu.VMEM((2, CHIPS, rows, HEAD_DIM), jnp.bfloat16),
            dma((3,)),
            dma((CHIPS, 2)), dma((CHIPS, 2)),
            dma((CHIPS, 2)), dma((CHIPS, 2, tiles)),
            dma((2,)),
            dma((CHIPS, 2)), dma((CHIPS, 2)),
            dma((3,)),
        ],
        compiler_params=pltpu.CompilerParams(collective_id=0, has_side_effects=True, vmem_limit_bytes=56 * 1024 * 1024),
        cost_estimate=pl.CostEstimate(flops=2 * rows * width * 4096, bytes_accessed=40_000_000, transcendentals=0),
        name="project_heads",
    )(residual, gain, cosines, sines, wq_all, w_key, w_value)


def solution(mesh):
    group_size = mesh.shape["tp"]

    def exchange(rows, bit):
        return lax.ppermute(rows, "tp", [(i, i ^ bit) for i in range(group_size)])

    def local_body(token_ids, positions, table_rows, norm_scale, w_query, w_key, w_value):
        dev_index = lax.axis_index("tp")
        vocab_rows, _ = table_rows.shape
        wq_all = lax.all_gather(w_query, "tp", axis=0)
        local_ids = token_ids - dev_index * vocab_rows
        inside = (local_ids >= 0) & (local_ids < vocab_rows)
        local_ids = jnp.where(inside, local_ids, -1)
        tokens = token_ids.shape[0]
        block_rows = tokens // group_size
        chunk_rows = block_rows // CHUNKS
        half = chunk_rows // 2

        def arrange(values):
            view = values.reshape(2, 2, 2, CHUNKS, 2, half)
            for axis, bit in ((0, 4), (1, 2), (2, 1)):
                flag = (dev_index // bit) % 2 == 1
                view = jnp.where(flag, jnp.flip(view, axis), view)
            halves = view.transpose(3, 2, 4, 0, 1, 5)
            first = halves[:, :, 0].transpose(0, 1, 3, 2, 4)
            second = halves[:, :, 1]
            return jnp.stack([first, second], axis=2).reshape(CHUNKS, 2, 4 * chunk_rows)

        ids = arrange(local_ids)
        owned = ids >= 0
        pair_ids = jnp.where(owned, (ids // 2) * 2, -1)
        lane = (jnp.arange(4 * chunk_rows, dtype=jnp.int32) % TILE) * 2
        cols = jnp.where(owned, lane + ids % 2, -1)
        counts = jnp.sum(owned.astype(jnp.int32).reshape(CHUNKS, 2, 4 * chunk_rows // TILE, TILE), axis=-1)

        def gather(chunk, side, after):
            return gather_rows(pair_ids[chunk, side], counts[chunk, side], cols[chunk, side][:, None], table_rows, after)

        pieces = []
        after, late, late_next = [], [], []
        for chunk in range(CHUNKS):
            other = gather(chunk, 1, after + late + ([wq_all] if chunk == 2 else []))
            got = exchange(other, 1)
            mine = gather(chunk, 0, [other])
            after, late = [], late_next
            late_next = []
            for part, bits in ((0, (2, 4)), (1, (4, 2))):
                base = part * 4 * half
                keep = [slice(base + k * half, base + (k + 1) * half) for k in range(4)]
                far = slice(base + 2 * half, base + 4 * half)
                sent = mine[far] + got[far]
                back = exchange(sent, bits[0])
                near_send = mine[keep[1]] + got[keep[1]] + back[half:]
                back2 = exchange(near_send, bits[1])
                after.append(sent)
                late_next.append(near_send)
                pieces.append(mine[keep[0]] + got[keep[0]] + back[:half] + back2)
        residual = jnp.concatenate(pieces, axis=0)
        own = lax.dynamic_slice_in_dim(positions, dev_index * block_rows, block_rows)
        cosines, sines = rope_tables(own)
        queries, keys_values = project_heads(residual, (1.0 + norm_scale)[None, :], cosines, sines, wq_all, w_key, w_value)
        return residual, queries[:, None, :], keys_values[0][:, None, :], keys_values[1][:, None, :]

    head_spec = P("dp", "tp", None)
    return jax.shard_map(local_body, mesh=mesh, in_specs=(P("dp"), P("dp"), P("tp", None), P(), P(None, "tp"), P(), P()), out_specs=(P(("dp", "tp"), None), head_spec, head_spec, head_spec), check_vma=False)
```

profile of v0, /device:TPU:0, one launch (start us, length us, event | category | flops | bytes accessed | tf_op | source)
XLA Modules:
  0.0 412.5 jit_solution(286787820098351555)
XLA Ops:
  12.2 15.3 %gather_rows.8.rest_0_ = bf16[1024,2304]{1,0:T(8,128)(2,1)} custom-call(s32[1024]{0:T(1024)} %bitcast.52, s32[8]{0:T(128)} %get-tuple-element.14.counts, s32[1024,1]{1,0:T(8,128)} %copy.34.cols_ref, bf16[32000,2304]{1,0:T(8,128)(2,1)} %table_ref.15), custom_call_target="tpu_custom_call" | custom-call | flops 20480000000 | bytes 14155776 | tf_op jit(solution)/shard_map/gather_rows/pallas_call | solution.py:83
  30.3 15.3 %gather_rows.9 = bf16[1024,2304]{1,0:T(8,128)(2,1)} custom-call(s32[1024]{0:T(1024)} %bitcast.49, s32[8]{0:T(128)} %get-tuple-element.15.counts, s32[1024,1]{1,0:T(8,128)} %copy.35.cols_ref, bf16[32000,2304]{1,0:T(8,128)(2,1)} %table_ref.15, bf16[1024,2304]{1,0:T(8,128)(2,1)} %gather_rows.8.rest_0_), custom_call_target="tpu_custom_call" | custom-call | flops 20480000000 | bytes 14155776 | tf_op jit(solution)/shard_map/gather_rows/pallas_call | solution.py:83
  45.6 4.0 slice_add_fusion.6
  49.6 15.4 %gather_rows.10.rest_0_ = bf16[1024,2304]{1,0:T(8,128)(2,1)} custom-call(s32[1024]{0:T(1024)} %bitcast.48, s32[8]{0:T(128)} %get-tuple-element.12.counts, s32[1024,1]{1,0:T(8,128)} %copy.36.cols_ref, bf16[32000,2304]{1,0:T(8,128)(2,1)} %table_ref.15, bf16[256,2304]{1,0:T(8,128)(2,1)} %get-tuple-element.31.rest_0_, bf16[256,2304]{1,0:T(8,128)(2,1)} %get-tuple-element.30.rest_1_), custom_call_target="tpu_custom_call" | custom-call | flops 20480000000 | bytes 14155776 | tf_op jit(solution)/shard_map/gather_rows/pallas_call | solution.py:83
  67.2 2.8 collective-permute-start.3
  70.1 1.5 collective-permute-start.1
  71.6 15.3 %gather_rows.11 = bf16[1024,2304]{1,0:T(8,128)(2,1)} custom-call(s32[1024]{0:T(1024)} %bitcast.47, s32[8]{0:T(128)} %get-tuple-element.13.counts, s32[1024,1]{1,0:T(8,128)} %copy.37.cols_ref, bf16[32000,2304]{1,0:T(8,128)(2,1)} %table_ref.15, bf16[1024,2304]{1,0:T(8,128)(2,1)} %gather_rows.10.rest_0_), custom_call_target="tpu_custom_call" | custom-call | flops 20480000000 | bytes 14155776 | tf_op jit(solution)/shard_map/gather_rows/pallas_call | solution.py:83
  86.9 9.4 %collective-permute-done.3 = bf16[256,2304]{1,0:T(8,128)(2,1)S(1)} collective-permute-done((bf16[256,2304]{1,0:T(8,128)(2,1)S(1)}, bf16[256,2304]{1,0:T(8,128)(2,1)S(1)}, u32[]{:S(2)}, u32[]{:S(2)}) %collective-permute-start.3) | collective-permute-done | bytes 1179680 | tf_op jit(solution)/shard_map/ppermute | solution.py:238
  96.3 1.6 collective-permute-done.1
  97.8 3.0 slice_add_fusion.32
  100.8 3.3 slice_add_fusion.4
  104.1 15.4 %gather_rows.12.rest_0_ = bf16[1024,2304]{1,0:T(8,128)(2,1)} custom-call(s32[1024]{0:T(1024)} %bitcast.51, s32[8]{0:T(128)} %get-tuple-element.10.counts, s32[1024,1]{1,0:T(8,128)} %copy.38.cols_ref, bf16[32000,2304]{1,0:T(8,128)(2,1)} %table_ref.15, bf16[256,2304]{1,0:T(8,128)(2,1)} %get-tuple-element.27.rest_0_, ...), custom_call_target="tpu_custom_call" | custom-call | flops 20480000000 | bytes 14155776 | tf_op jit(solution)/shard_map/gather_rows/pallas_call | solution.py:83
  120.2 1.5 collective-permute-start.6
  126.9 3.1 multiply_sine_fusion
  129.9 1.4 collective-permute-start.2
  131.9 16.7 %collective-permute-done.8 = bf16[256,2304]{1,0:T(8,128)(2,1)} collective-permute-done((bf16[256,2304]{1,0:T(8,128)(2,1)S(1)}, bf16[256,2304]{1,0:T(8,128)(2,1)}, u32[]{:S(2)}, u32[]{:S(2)}) %collective-permute-start.8) | collective-permute-done | bytes 1179680 | tf_op jit(solution)/shard_map/ppermute | solution.py:238
  149.2 3.1 slice_add_fusion.24
  152.3 15.3 %gather_rows.13 = bf16[1024,2304]{1,0:T(8,128)(2,1)} custom-call(s32[1024]{0:T(1024)} %bitcast.46, s32[8]{0:T(128)} %get-tuple-element.11.counts, s32[1024,1]{1,0:T(8,128)} %copy.39.cols_ref, bf16[32000,2304]{1,0:T(8,128)(2,1)} %table_ref.15, bf16[1024,2304]{1,0:T(8,128)(2,1)} %gather_rows.12.rest_0_), custom_call_target="tpu_custom_call" | custom-call | flops 20480000000 | bytes 14155776 | tf_op jit(solution)/shard_map/gather_rows/pallas_call | solution.py:83
  167.6 4.0 slice_add_fusion.2
  171.6 15.3 %gather_rows.14.rest_0_ = bf16[1024,2304]{1,0:T(8,128)(2,1)} custom-call(s32[1024]{0:T(1024)} %bitcast.50, s32[8]{0:T(128)} %get-tuple-element.9.counts, s32[1024,1]{1,0:T(8,128)} %copy.40.cols_ref, bf16[32000,2304]{1,0:T(8,128)(2,1)} %table_ref.15, bf16[256,2304]{1,0:T(8,128)(2,1)} %get-tuple-element.23.rest_0_, ...), custom_call_target="tpu_custom_call" | custom-call | flops 20480000000 | bytes 14155776 | tf_op jit(solution)/shard_map/gather_rows/pallas_call | solution.py:83
  187.0 2.0 fusion.15
  189.0 1.4 collective-permute-start.7
  190.4 1.7 fusion.13
  192.2 1.5 collective-permute-start.9
  193.7 11.0 %collective-permute-done.7 = bf16[128,2304]{1,0:T(8,128)(2,1)S(1)} collective-permute-done((bf16[128,2304]{1,0:T(8,128)(2,1)S(1)}, bf16[128,2304]{1,0:T(8,128)(2,1)S(1)}, u32[]{:S(2)}, u32[]{:S(2)}) %collective-permute-start.7) | collective-permute-done | bytes 589856 | tf_op jit(solution)/shard_map/ppermute | solution.py:238
  204.7 1.7 fusion.11
  206.4 1.4 collective-permute-start.13
  207.8 1.4 collective-permute-start.11
  209.2 15.3 %gather_rows.15 = bf16[1024,2304]{1,0:T(8,128)(2,1)} custom-call(s32[1024]{0:T(1024)} %bitcast.45, s32[8]{0:T(128)} %get-tuple-element.8.counts, s32[1024,1]{1,0:T(8,128)} %copy.41.cols_ref, bf16[32000,2304]{1,0:T(8,128)(2,1)} %table_ref.15, bf16[1024,2304]{1,0:T(8,128)(2,1)} %gather_rows.14.rest_0_), custom_call_target="tpu_custom_call" | custom-call | flops 20480000000 | bytes 14155776 | tf_op jit(solution)/shard_map/gather_rows/pallas_call | solution.py:83
  224.6 9.4 %collective-permute-done.13 = bf16[256,2304]{1,0:T(8,128)(2,1)} collective-permute-done((bf16[256,2304]{1,0:T(8,128)(2,1)S(1)}, bf16[256,2304]{1,0:T(8,128)(2,1)}, u32[]{:S(2)}, u32[]{:S(2)}) %collective-permute-start.13) | collective-permute-done | bytes 1179680 | tf_op jit(solution)/shard_map/ppermute | solution.py:238
  235.0 2.3 slice_add_fusion.16
  238.4 1.9 slice_add_fusion
  241.3 1.4 collective-permute-start.16
  242.7 2.5 fusion.9
  245.8 7.7 %collective-permute-done.12 = bf16[128,2304]{1,0:T(8,128)(2,1)S(1)} collective-permute-done((bf16[128,2304]{1,0:T(8,128)(2,1)S(1)}, bf16[128,2304]{1,0:T(8,128)(2,1)S(1)}, u32[]{:S(2)}, u32[]{:S(2)}) %collective-permute-start.12) | collective-permute-done | bytes 589856 | tf_op jit(solution)/shard_map/ppermute | solution.py:238
  253.5 2.5 fusion.7
  256.1 20.2 %collective-permute-done.18 = bf16[256,2304]{1,0:T(8,128)(2,1)S(1)} collective-permute-done((bf16[256,2304]{1,0:T(8,128)(2,1)S(1)}, bf16[256,2304]{1,0:T(8,128)(2,1)S(1)}, u32[]{:S(2)}, u32[]{:S(2)}) %collective-permute-start.18) | collective-permute-done | bytes 1179680 | tf_op jit(solution)/shard_map/ppermute | solution.py:238
  276.2 1.4 slice_add_fusion.8
  278.4 1.3 collective-permute-done.14
  279.6 2.6 fusion.5
  282.2 1.4 collective-permute-start.19
  283.6 6.9 %collective-permute-done.17 = bf16[128,2304]{1,0:T(8,128)(2,1)S(1)} collective-permute-done((bf16[128,2304]{1,0:T(8,128)(2,1)S(1)}, bf16[128,2304]{1,0:T(8,128)(2,1)S(1)}, u32[]{:S(2)}, u32[]{:S(2)}) %collective-permute-start.17) | collective-permute-done | bytes 589856 | tf_op jit(solution)/shard_map/ppermute | solution.py:238
  290.5 2.2 fusion.3
  292.7 1.7 collective-permute-done.19
  294.4 2.2 fusion.1.resid_ref
  296.6 99.9 %project_heads.1 = (bf16[8192,256]{1,0:T(8,128)(2,1)}, bf16[2,8192,256]{2,1,0:T(8,128)(2,1)}) custom-call(bf16[1024,2304]{1,0:T(8,128)(2,1)} %fusion.1.resid_ref, f32[1,2304]{1,0:T(1,128)} %broadcast_in_dim.17.gain_ref, f32[1024,128]{1,0:T(8,128)} %get-tuple-element.57.cos_ref, f32[1024,128]{1,0:T(8,128)} %get-tuple-element.56.sin_ref, ...), custom_call_target="tpu_custom_call" | custom-call | flops 19327352832 | bytes 40000000 | tf_op jit(solution)/shard_map/project_heads/pallas_call | solution.py:209
  396.5 6.6 %slice_bitcast_fusion = (bf16[8192,1,256]{2,0,1:T(8,128)(2,1)}, bf16[8192,1,256]{2,0,1:T(8,128)(2,1)}) fusion(bf16[2,8192,256]{2,1,0:T(8,128)(2,1)} %get-tuple-element.7), kind=kLoop, calls=%fused_computation | loop fusion | bytes 16777216 | tf_op jit(solution)/shard_map/broadcast_in_dim;squeeze | solution.py:295
  403.7 2.0 copy.51
  (90 shorter events, 22.1 us)
Async XLA Ops:
  7.2 0.8 copy-start.16
  7.2 96.9 %all-gather.3.cloned.1.call-start = ((), (), s32[]{:S(2)}) async-start(), calls=%async_computation | async-start | bytes 10616832 | tf_op jit(solution)/shard_map/all_gather | solution.py:243
  27.5 18.1 %collective-permute-start = (bf16[1024,2304]{1,0:T(8,128)(2,1)}, bf16[1024,2304]{1,0:T(8,128)(2,1)}, u32[]{:S(2)}, u32[]{:S(2)}) collective-permute-start(bf16[1024,2304]{1,0:T(8,128)(2,1)} %gather_rows.8.rest_0_), channel_id=1, source_target_pairs={{0,1},{1,0},{2,3},{3,2},{4,5},{5,4},{6,7},{7,6},{8,9},{9,8},{10,11... | collective-permute-start | bytes 14155784 | tf_op jit(solution)/shard_map/ppermute | solution.py:238
  49.6 17.6 %copy-start.3 = (bf16[256,2304]{1,0:T(8,128)(2,1)S(1)}, bf16[256,2304]{1,0:T(8,128)(2,1)}, u32[]{:S(2)}) copy-start(bf16[256,2304]{1,0:T(8,128)(2,1)} %get-tuple-element.30.rest_1_) | copy-start | bytes 3538948
  49.6 20.5 %copy-start.2 = (bf16[256,2304]{1,0:T(8,128)(2,1)S(1)}, bf16[256,2304]{1,0:T(8,128)(2,1)}, u32[]{:S(2)}) copy-start(bf16[256,2304]{1,0:T(8,128)(2,1)} %get-tuple-element.31.rest_0_) | copy-start | bytes 3538948
  65.0 35.8 %collective-permute-start.5 = (bf16[1024,2304]{1,0:T(8,128)(2,1)}, bf16[1024,2304]{1,0:T(8,128)(2,1)}, u32[]{:S(2)}, u32[]{:S(2)}) collective-permute-start(bf16[1024,2304]{1,0:T(8,128)(2,1)} %gather_rows.10.rest_0_), channel_id=1, source_target_pairs={{0,1},{1,0},{2,3},{3,2},{4,5},{5,4},{6,7},{7,6},{8,9},{9,8},{10,11... | collective-permute-start | bytes 14155784 | tf_op jit(solution)/shard_map/ppermute | solution.py:238
  67.2 29.0 %collective-permute-start.3 = (bf16[256,2304]{1,0:T(8,128)(2,1)S(1)}, bf16[256,2304]{1,0:T(8,128)(2,1)S(1)}, u32[]{:S(2)}, u32[]{:S(2)}) collective-permute-start(bf16[256,2304]{1,0:T(8,128)(2,1)S(1)} %copy-done.3), channel_id=1, source_target_pairs={{0,4},{1,5},{2,6},{3,7},{4,0},{5,1},{6,2},{7,3},{8,12},{9,13},{10,... | collective-permute-start | bytes 3538952 | tf_op jit(solution)/shard_map/ppermute | solution.py:238
  70.1 27.8 %collective-permute-start.1 = (bf16[256,2304]{1,0:T(8,128)(2,1)S(1)}, bf16[256,2304]{1,0:T(8,128)(2,1)}, u32[]{:S(2)}, u32[]{:S(2)}) collective-permute-start(bf16[256,2304]{1,0:T(8,128)(2,1)S(1)} %copy-done.2), channel_id=1, source_target_pairs={{0,2},{1,3},{2,0},{3,1},{4,6},{5,7},{6,4},{7,5},{8,10},{9,11},{10,... | collective-permute-start | bytes 3538952 | tf_op jit(solution)/shard_map/ppermute | solution.py:238
  86.8 14.0 %copy-start = (bf16[1024,2304]{1,0:T(8,128)(2,1)S(1)}, bf16[1024,2304]{1,0:T(8,128)(2,1)}, u32[]{:S(2)}) copy-start(bf16[1024,2304]{1,0:T(8,128)(2,1)} %gather_rows.11) | copy-start | bytes 14155780
  96.3 4.5 %copy-start.13 = (bf16[256,2304]{1,0:T(8,128)(2,1)}, bf16[256,2304]{1,0:T(8,128)(2,1)S(1)}, u32[]{:S(2)}) copy-start(bf16[256,2304]{1,0:T(8,128)(2,1)S(1)} %collective-permute-done.3) | copy-start | bytes 3538948
  104.1 15.5 %copy-start.6 = (bf16[256,2304]{1,0:T(8,128)(2,1)S(1)}, bf16[256,2304]{1,0:T(8,128)(2,1)}, u32[]{:S(2)}) copy-start(bf16[256,2304]{1,0:T(8,128)(2,1)} %get-tuple-element.26.rest_1_) | copy-start | bytes 3538948
  104.1 16.1 %copy-start.4 = (bf16[256,2304]{1,0:T(8,128)(2,1)S(1)}, bf16[256,2304]{1,0:T(8,128)(2,1)}, u32[]{:S(2)}) copy-start(bf16[256,2304]{1,0:T(8,128)(2,1)} %get-tuple-element.27.rest_0_) | copy-start | bytes 3538948
  104.1 17.6 %copy-start.19 = (s32[1024,1]{0,1:T(1,128)S(1)}, s32[1024,1]{0,1:T(1,128)}, u32[]{:S(2)}) copy-start(s32[1024,1]{0,1:T(1,128)} %get-tuple-element.37) | copy-start | bytes 12292
  104.1 18.7 %copy-start.18 = (s32[1024,1]{0,1:T(1,128)S(1)}, s32[1024,1]{0,1:T(1,128)}, u32[]{:S(2)}) copy-start(s32[1024,1]{0,1:T(1,128)} %get-tuple-element.35) | copy-start | bytes 12292
  104.1 19.7 %copy-start.17 = (s32[1024,1]{0,1:T(1,128)S(1)}, s32[1024,1]{0,1:T(1,128)}, u32[]{:S(2)}) copy-start(s32[1024,1]{0,1:T(1,128)} %get-tuple-element.34) | copy-start | bytes 12292
  119.5 48.1 %collective-permute-start.10 = (bf16[1024,2304]{1,0:T(8,128)(2,1)}, bf16[1024,2304]{1,0:T(8,128)(2,1)}, u32[]{:S(2)}, u32[]{:S(2)}) collective-permute-start(bf16[1024,2304]{1,0:T(8,128)(2,1)} %gather_rows.12.rest_0_), channel_id=1, source_target_pairs={{0,1},{1,0},{2,3},{3,2},{4,5},{5,4},{6,7},{7,6},{8,9},{9,8},{10,11... | collective-permute-start | bytes 14155784 | tf_op jit(solution)/shard_map/ppermute | solution.py:238
  119.6 29.0 %collective-permute-start.8 = (bf16[256,2304]{1,0:T(8,128)(2,1)S(1)}, bf16[256,2304]{1,0:T(8,128)(2,1)}, u32[]{:S(2)}, u32[]{:S(2)}) collective-permute-start(bf16[256,2304]{1,0:T(8,128)(2,1)S(1)} %copy-done.6), channel_id=1, source_target_pairs={{0,4},{1,5},{2,6},{3,7},{4,0},{5,1},{6,2},{7,3},{8,12},{9,13},{10,... | collective-permute-start | bytes 3538952 | tf_op jit(solution)/shard_map/ppermute | solution.py:238
  120.2 28.9 %collective-permute-start.6 = (bf16[256,2304]{1,0:T(8,128)(2,1)S(1)}, bf16[256,2304]{1,0:T(8,128)(2,1)}, u32[]{:S(2)}, u32[]{:S(2)}) collective-permute-start(bf16[256,2304]{1,0:T(8,128)(2,1)S(1)} %copy-done.4), channel_id=1, source_target_pairs={{0,2},{1,3},{2,0},{3,1},{4,6},{5,7},{6,4},{7,5},{8,10},{9,11},{10,... | collective-permute-start | bytes 3538952 | tf_op jit(solution)/shard_map/ppermute | solution.py:238
  122.7 7.2 %copy-start.11 = (bf16[128,2304]{1,0:T(8,128)(2,1)S(1)}, bf16[128,2304]{1,0:T(8,128)(2,1)}, u32[]{:S(2)}) copy-start(bf16[128,2304]{1,0:T(8,128)(2,1)} %get-tuple-element.29.rest_2_) | copy-start | bytes 1769476
  122.7 8.6 %copy-start.9 = (bf16[128,2304]{1,0:T(8,128)(2,1)S(1)}, bf16[128,2304]{1,0:T(8,128)(2,1)}, u32[]{:S(2)}) copy-start(bf16[128,2304]{1,0:T(8,128)(2,1)} %get-tuple-element.28.rest_3_) | copy-start | bytes 1769476
  129.9 57.0 %collective-permute-start.2 = (bf16[128,2304]{1,0:T(8,128)(2,1)S(1)}, bf16[128,2304]{1,0:T(8,128)(2,1)}, u32[]{:S(2)}, u32[]{:S(2)}) collective-permute-start(bf16[128,2304]{1,0:T(8,128)(2,1)S(1)} %copy-done.11), channel_id=1, source_target_pairs={{0,4},{1,5},{2,6},{3,7},{4,0},{5,1},{6,2},{7,3},{8,12},{9,13},{10,... | collective-permute-start | bytes 1769480 | tf_op jit(solution)/shard_map/ppermute | solution.py:238
  131.3 59.1 %collective-permute-start.4 = (bf16[128,2304]{1,0:T(8,128)(2,1)S(1)}, bf16[128,2304]{1,0:T(8,128)(2,1)}, u32[]{:S(2)}, u32[]{:S(2)}) collective-permute-start(bf16[128,2304]{1,0:T(8,128)(2,1)S(1)} %copy-done.9), channel_id=1, source_target_pairs={{0,2},{1,3},{2,0},{3,1},{4,6},{5,7},{6,4},{7,5},{8,10},{9,11},{10,... | collective-permute-start | bytes 1769480 | tf_op jit(solution)/shard_map/ppermute | solution.py:238
  186.9 2.1 copy-start.12
  186.9 3.5 copy-start.14
  186.9 51.1 %collective-permute-start.15 = (bf16[1024,2304]{1,0:T(8,128)(2,1)}, bf16[1024,2304]{1,0:T(8,128)(2,1)}, u32[]{:S(2)}, u32[]{:S(2)}) collective-permute-start(bf16[1024,2304]{1,0:T(8,128)(2,1)} %gather_rows.14.rest_0_), channel_id=1, source_target_pairs={{0,1},{1,0},{2,3},{3,2},{4,5},{5,4},{6,7},{7,6},{8,9},{9,8},{10,11... | collective-permute-start | bytes 14155784 | tf_op jit(solution)/shard_map/ppermute | solution.py:238
  189.0 3.2 copy-start.10
  189.0 15.6 %collective-permute-start.7 = (bf16[128,2304]{1,0:T(8,128)(2,1)S(1)}, bf16[128,2304]{1,0:T(8,128)(2,1)S(1)}, u32[]{:S(2)}, u32[]{:S(2)}) collective-permute-start(bf16[128,2304]{1,0:T(8,128)(2,1)S(1)} %copy-done.12), channel_id=1, source_target_pairs={{0,4},{1,5},{2,6},{3,7},{4,0},{5,1},{6,2},{7,3},{8,12},{9,13},{10,... | collective-permute-start | bytes 1769480 | tf_op jit(solution)/shard_map/ppermute | solution.py:238
  192.2 14.2 %copy-start.7 = (bf16[256,2304]{1,0:T(8,128)(2,1)S(1)}, bf16[256,2304]{1,0:T(8,128)(2,1)}, u32[]{:S(2)}) copy-start(bf16[256,2304]{1,0:T(8,128)(2,1)} %get-tuple-element.22.rest_1_) | copy-start | bytes 3538948
  192.2 15.6 %copy-start.5 = (bf16[256,2304]{1,0:T(8,128)(2,1)S(1)}, bf16[256,2304]{1,0:T(8,128)(2,1)}, u32[]{:S(2)}) copy-start(bf16[256,2304]{1,0:T(8,128)(2,1)} %get-tuple-element.23.rest_0_) | copy-start | bytes 3538948
  192.2 50.5 %collective-permute-start.9 = (bf16[128,2304]{1,0:T(8,128)(2,1)S(1)}, bf16[128,2304]{1,0:T(8,128)(2,1)S(1)}, u32[]{:S(2)}, u32[]{:S(2)}) collective-permute-start(bf16[128,2304]{1,0:T(8,128)(2,1)S(1)} %copy-done.10), channel_id=1, source_target_pairs={{0,2},{1,3},{2,0},{3,1},{4,6},{5,7},{6,4},{7,5},{8,10},{9,11},{10,... | collective-permute-start | bytes 1769480 | tf_op jit(solution)/shard_map/ppermute | solution.py:238
  206.4 2.9 copy-start.15
  206.4 27.5 %collective-permute-start.13 = (bf16[256,2304]{1,0:T(8,128)(2,1)S(1)}, bf16[256,2304]{1,0:T(8,128)(2,1)}, u32[]{:S(2)}, u32[]{:S(2)}) collective-permute-start(bf16[256,2304]{1,0:T(8,128)(2,1)S(1)} %copy-done.7), channel_id=1, source_target_pairs={{0,4},{1,5},{2,6},{3,7},{4,0},{5,1},{6,2},{7,3},{8,12},{9,13},{10,... | collective-permute-start | bytes 3538952 | tf_op jit(solution)/shard_map/ppermute | solution.py:238
  207.8 27.2 %collective-permute-start.11 = (bf16[256,2304]{1,0:T(8,128)(2,1)S(1)}, bf16[256,2304]{1,0:T(8,128)(2,1)}, u32[]{:S(2)}, u32[]{:S(2)}) collective-permute-start(bf16[256,2304]{1,0:T(8,128)(2,1)S(1)} %copy-done.5), channel_id=1, source_target_pairs={{0,2},{1,3},{2,0},{3,1},{4,6},{5,7},{6,4},{7,5},{8,10},{9,11},{10,... | collective-permute-start | bytes 3538952 | tf_op jit(solution)/shard_map/ppermute | solution.py:238
  235.0 3.4 copy-start.1
  237.3 16.2 %collective-permute-start.12 = (bf16[128,2304]{1,0:T(8,128)(2,1)S(1)}, bf16[128,2304]{1,0:T(8,128)(2,1)S(1)}, u32[]{:S(2)}, u32[]{:S(2)}) collective-permute-start(bf16[128,2304]{1,0:T(8,128)(2,1)S(1)} %get-tuple-element.21), channel_id=1, source_target_pairs={{0,4},{1,5},{2,6},{3,7},{4,0},{5,1},{6,2},{7,3},{8,12},{9,13},{10,... | collective-permute-start | bytes 1769480 | tf_op jit(solution)/shard_map/ppermute | solution.py:238
  240.3 35.9 %collective-permute-start.18 = (bf16[256,2304]{1,0:T(8,128)(2,1)S(1)}, bf16[256,2304]{1,0:T(8,128)(2,1)S(1)}, u32[]{:S(2)}, u32[]{:S(2)}) collective-permute-start(bf16[256,2304]{1,0:T(8,128)(2,1)S(1)} %get-tuple-element.18), channel_id=1, source_target_pairs={{0,4},{1,5},{2,6},{3,7},{4,0},{5,1},{6,2},{7,3},{8,12},{9,13},{10,... | collective-permute-start | bytes 3538952 | tf_op jit(solution)/shard_map/ppermute | solution.py:238
  241.3 35.0 %collective-permute-start.16 = (bf16[256,2304]{1,0:T(8,128)(2,1)S(1)}, bf16[256,2304]{1,0:T(8,128)(2,1)S(1)}, u32[]{:S(2)}, u32[]{:S(2)}) collective-permute-start(bf16[256,2304]{1,0:T(8,128)(2,1)S(1)} %get-tuple-element.19), channel_id=1, source_target_pairs={{0,2},{1,3},{2,0},{3,1},{4,6},{5,7},{6,4},{7,5},{8,10},{9,11},{10,... | collective-permute-start | bytes 3538952 | tf_op jit(solution)/shard_map/ppermute | solution.py:238
  245.2 34.4 %collective-permute-start.14 = (bf16[128,2304]{1,0:T(8,128)(2,1)S(1)}, bf16[128,2304]{1,0:T(8,128)(2,1)S(1)}, u32[]{:S(2)}, u32[]{:S(2)}) collective-permute-start(bf16[128,2304]{1,0:T(8,128)(2,1)S(1)} %get-tuple-element.20), channel_id=1, source_target_pairs={{0,2},{1,3},{2,0},{3,1},{4,6},{5,7},{6,4},{7,5},{8,10},{9,11},{10,... | collective-permute-start | bytes 1769480 | tf_op jit(solution)/shard_map/ppermute | solution.py:238
  277.7 12.8 %collective-permute-start.17 = (bf16[128,2304]{1,0:T(8,128)(2,1)S(1)}, bf16[128,2304]{1,0:T(8,128)(2,1)S(1)}, u32[]{:S(2)}, u32[]{:S(2)}) collective-permute-start(bf16[128,2304]{1,0:T(8,128)(2,1)S(1)} %get-tuple-element.17), channel_id=1, source_target_pairs={{0,4},{1,5},{2,6},{3,7},{4,0},{5,1},{6,2},{7,3},{8,12},{9,13},{10,... | collective-permute-start | bytes 1769480 | tf_op jit(solution)/shard_map/ppermute | solution.py:238
  282.2 12.2 %collective-permute-start.19 = (bf16[128,2304]{1,0:T(8,128)(2,1)S(1)}, bf16[128,2304]{1,0:T(8,128)(2,1)S(1)}, u32[]{:S(2)}, u32[]{:S(2)}) collective-permute-start(bf16[128,2304]{1,0:T(8,128)(2,1)S(1)} %get-tuple-element.16), channel_id=1, source_target_pairs={{0,2},{1,3},{2,0},{3,1},{4,6},{5,7},{6,4},{7,5},{8,10},{9,11},{10,... | collective-permute-start | bytes 1769480 | tf_op jit(solution)/shard_map/ppermute | solution.py:238
  396.5 7.2 %copy-start.8 = (bf16[8192,256]{1,0:T(8,128)(2,1)S(1)}, bf16[8192,256]{1,0:T(8,128)(2,1)}, u32[]{:S(2)}) copy-start(bf16[8192,256]{1,0:T(8,128)(2,1)} %get-tuple-element.6) | copy-start | bytes 12582916
Sparse Core Ops, SparseCore 0:
  9.8 58.3 all-gather.2
where the time goes:
time: 420 us; the launch traced here: 413 us
  Pallas kernels  223 us (53%)
  waiting for transfers between devices  88.1 us (21%)
  other arithmetic  45.6 us (11%)
  local copies, waits for them, and re-layouts  20.9 us (5%)
  starting transfers between devices  20.9 us (5%)
  between operations  14.5 us (3%)
    pallas_call x8, Pallas kernels, gather_rows(): pl.pallas_call(functools.partial(gather_kernel, tiles, width), grid_spec=...  123 us
    pallas_call x1, Pallas kernels, project_heads(): pl.pallas_call(functools.partial(heads_kernel, rows), out_shape=(jax.Shap...  99.9 us
    ppermute x20, waiting for transfers between devices, exchange(): return lax.ppermute(rows, 'tp', [(i, i ^ bit) for i in range(group_size)])  87.4 us
    ppermute x20, starting transfers between devices, exchange(): return lax.ppermute(rows, 'tp', [(i, i ^ bit) for i in range(group_size)])  20.9 us
    unnamed x7, other arithmetic  15.2 us
    add x4, other arithmetic, local_body(): sent = mine[far] + got[far]  13.1 us
    add x4, other arithmetic, local_body(): near_send = mine[keep[1]] + got[keep[1]] + back[half:]  9.81 us
    another operation x9, local copies, waits for them, and re-layouts, gather(): cols[chunk, side][:, None]  8.88 us
  transfers between devices with their start and end apart: 21, of which 12 were waited for; matrix products, arithmetic and copies ran while one was open for 13% of the time, Pallas kernels for 26%

commit v1 on v0

--- a/solution.py
+++ b/solution.py
@@ -11,7 +11,9 @@
 EPSILON = 1e-6
 ROPE_BASE = 10000.0
 TILE = 128
-CHUNKS = 4
+CHUNKS = 5
+HEAD_ROWS = 640
+TAIL_ROWS = 640
 SEND_ROWS = 512
 CHIPS = 4
 MESH_IDS = pl.DeviceIdType.MESH
@@ -23,29 +25,34 @@
     return jnp.cos(angles), jnp.sin(angles)
 
 
-def gather_kernel(tiles, width, pair_ids, counts, cols_ref, table_ref, *rest):
+def gather_kernel(base, tiles, width, pair_ids, counts, cols_ref, table_ref, *rest):
     out_ref, pairs, sems = rest[-3:]
     step = pl.program_id(0)
     normalizer = jnp.asarray(math.sqrt(width), dtype=jnp.bfloat16)
 
     def start(tile, slot):
-        @pl.loop(0, TILE, unroll=8)
-        def _(row):
-            src = pair_ids[tile * TILE + row]
-
-            @pl.when(src >= 0)
+        @pl.loop(0, TILE // 8)
+        def _(group):
+            for row in range(8):
+                src = pair_ids[(base + tile) * TILE + group * 8 + row]
+
+                @pl.when(src >= 0)
+                def _():
+                    pltpu.make_async_copy(table_ref.at[pl.ds(pl.multiple_of(src, 2), 2), :], pairs.at[slot, group, pl.ds(2 * row, 2), :], sems.at[slot]).start()
+
+    def wait(tile, slot):
+        count = counts[base + tile]
+        size = TILE // 8
+        while size:
+            @pl.when((count // (8 * size)) % 2 == 1)
             def _():
-                pltpu.make_async_copy(table_ref.at[pl.ds(pl.multiple_of(src, 2), 2), :], pairs.at[slot, pl.ds(pl.multiple_of(2 * row, 2), 2), :], sems.at[slot]).start()
-
-    def wait(tile, slot):
-        count = counts[tile]
-        size = TILE
-        while size:
+                pltpu.make_async_copy(pairs.at[slot, pl.ds(0, size)], pairs.at[slot, pl.ds(0, size)], sems.at[slot]).wait()
+
+            size //= 2
+        for size in (1, 2, 4):
             @pl.when((count // size) % 2 == 1)
             def _():
-                pltpu.make_async_copy(table_ref.at[pl.ds(0, 2 * size), :], pairs.at[slot, pl.ds(0, 2 * size), :], sems.at[slot]).wait()
-
-            size //= 2
+                pltpu.make_async_copy(table_ref.at[pl.ds(0, 2 * size), :], pairs.at[slot, 0, pl.ds(0, 2 * size), :], sems.at[slot]).wait()
 
     @pl.when(step == 0)
     def _():
@@ -60,28 +67,29 @@
         start(step + 2, lax.rem(step + 2, 3))
 
     wait(step, slot)
-    lanes = lax.broadcasted_iota(jnp.int32, (TILE, 2 * TILE), 1)
-    select = jnp.where(lanes == cols_ref[...], normalizer, jnp.zeros((), jnp.bfloat16))
+    lanes = lax.broadcasted_iota(jnp.int32, (TILE, 2 * TILE), 1).astype(jnp.float32)
+    wanted = jnp.broadcast_to(cols_ref[0], (TILE, TILE)).T
+    select = jnp.where(lanes == jnp.concatenate([wanted, wanted], axis=1), normalizer, jnp.zeros((), jnp.bfloat16))
     for piece in range(width // 256):
         cols = pl.ds(piece * 256, 256)
-        picked = jnp.dot(select, pairs[slot, :, cols], preferred_element_type=jnp.float32)
+        picked = jnp.dot(select, pairs[slot, :, :, cols].reshape(2 * TILE, 256), preferred_element_type=jnp.float32)
         out_ref[:, cols] = picked.astype(jnp.bfloat16)
 
 
-def gather_rows(pair_ids, counts, cols, table_rows, after):
-    count = cols.shape[0]
+def gather_rows(base, count, pair_ids, counts, cols, table_rows, after):
     width = table_rows.shape[1]
     tiles = count // TILE
+    base = base // TILE
     anywhere = pl.BlockSpec(memory_space=pl.ANY)
     grid_spec = pltpu.PrefetchScalarGridSpec(
         num_scalar_prefetch=2,
         grid=(tiles,),
-        in_specs=[pl.BlockSpec((TILE, 1), lambda i, *_: (i, 0)), anywhere] + [anywhere] * len(after),
+        in_specs=[pl.BlockSpec((1, 1, TILE), lambda i, *_: (base + i, 0, 0)), anywhere] + [anywhere] * len(after),
         out_specs=pl.BlockSpec((TILE, width), lambda i, *_: (i, 0)),
-        scratch_shapes=[pltpu.VMEM((3, 2 * TILE, width), jnp.bfloat16), pltpu.SemaphoreType.DMA((3,))],
+        scratch_shapes=[pltpu.VMEM((3, TILE // 8, 16, width), jnp.bfloat16), pltpu.SemaphoreType.DMA((3,))],
     )
     return pl.pallas_call(
-        functools.partial(gather_kernel, tiles, width),
+        functools.partial(gather_kernel, base, tiles, width),
         grid_spec=grid_spec,
         out_shape=jax.ShapeDtypeStruct((count, width), jnp.bfloat16),
         compiler_params=pltpu.CompilerParams(dimension_semantics=("arbitrary",)),
@@ -90,8 +98,64 @@
     )(pair_ids, counts, cols, table_rows, *after)
 
 
-def heads_kernel(rows, resid_ref, gain_ref, cos_ref, sin_ref, wq_hbm, wk_hbm, wv_hbm, q_out, kv_out,
-                 wq, wk, wv, normed, q_stage, kv_stage, w_sem, q_send, q_recv, kv_send, kv_recv,
+def finish_kernel(pieces, more, cols_ref, gain_ref, head_ref, extra_ref, *refs):
+    tail_refs, (resid_ref, normed_ref, tail) = refs[:pieces], refs[pieces:]
+    rows, width = resid_ref.shape
+    part = TAIL_ROWS // (pieces // 2)
+    extra_rows = extra_ref.shape[0]
+    normalizer = jnp.asarray(math.sqrt(width), dtype=jnp.bfloat16)
+    for index in range(pieces // 2):
+        tail[pl.ds(index * part, part), :] = tail_refs[2 * index][...] + tail_refs[2 * index + 1][...]
+
+    def one_hot(span, first, count, value):
+        lanes = lax.broadcasted_iota(jnp.int32, (256, count), 1) + first
+        return jnp.where(lanes == cols_ref[span, :], value, jnp.zeros((), jnp.bfloat16))
+
+    @pl.loop(0, rows // 256)
+    def _(block):
+        span = pl.ds(pl.multiple_of(block * 256, 256), 256)
+        from_head = one_hot(span, 0, HEAD_ROWS, normalizer)
+        from_tail = one_hot(span, HEAD_ROWS, TAIL_ROWS, jnp.ones((), jnp.bfloat16))
+        for piece in range(width // 256):
+            cols = pl.ds(piece * 256, 256)
+            picked = jnp.dot(from_head, head_ref[:, cols], preferred_element_type=jnp.float32)
+            picked += jnp.dot(from_tail, tail[:, cols], preferred_element_type=jnp.float32)
+            resid_ref[span, cols] = picked.astype(jnp.bfloat16)
+
+        @pl.when(more[0] > 0)
+        def _():
+            from_extra = one_hot(span, HEAD_ROWS + TAIL_ROWS, extra_rows, jnp.ones((), jnp.bfloat16))
+            for piece in range(width // 256):
+                cols = pl.ds(piece * 256, 256)
+                picked = jnp.dot(from_extra, extra_ref[:, cols], preferred_element_type=jnp.float32)
+                resid_ref[span, cols] = (resid_ref[span, cols].astype(jnp.float32) + picked).astype(jnp.bfloat16)
+
+        for quarter in range(4):
+            rows_here = pl.ds(pl.multiple_of(block * 256 + quarter * 64, 64), 64)
+            widened = resid_ref[rows_here, :].astype(jnp.float32)
+            inv_rms = lax.rsqrt(jnp.mean(widened * widened, axis=-1, keepdims=True) + EPSILON)
+            normed_ref[rows_here, :] = (widened * inv_rms * gain_ref[...]).astype(jnp.bfloat16)
+
+
+def finish_rows(more, cols, gain, head, extra, tail_pieces):
+    rows = cols.shape[0]
+    width = head.shape[1]
+    vmem = pl.BlockSpec(memory_space=pltpu.VMEM)
+    shape = jax.ShapeDtypeStruct((rows, width), jnp.bfloat16)
+    return pl.pallas_call(
+        functools.partial(finish_kernel, len(tail_pieces)),
+        out_shape=(shape, shape),
+        in_specs=[pl.BlockSpec(memory_space=pltpu.SMEM)] + [vmem] * (4 + len(tail_pieces)),
+        out_specs=(vmem, vmem),
+        scratch_shapes=[pltpu.VMEM((TAIL_ROWS, width), jnp.bfloat16)],
+        compiler_params=pltpu.CompilerParams(vmem_limit_bytes=40 * 1024 * 1024),
+        cost_estimate=pl.CostEstimate(flops=2 * rows * width * (HEAD_ROWS + TAIL_ROWS), bytes_accessed=16_000_000, transcendentals=0),
+        name="finish_rows",
+    )(more, cols, gain, head, extra, *tail_pieces)
+
+
+def heads_kernel(rows, normed, cos_ref, sin_ref, wq_hbm, wk_hbm, wv_hbm, q_out, kv_out,
+                 wq, wk, wv, q_stage, kv_stage, w_sem, q_send, q_recv, kv_send, kv_recv,
                  own_recv, fwd_send, fwd_recv, keep_sem):
     group = lax.axis_index("dp")
     me = lax.axis_index("tp")
@@ -108,13 +172,6 @@
     barrier = pltpu.get_barrier_semaphore()
     for step in range(1, 2 * CHIPS):
         pl.semaphore_signal(barrier, inc=1, device_id=(group, lax.rem(me + step, 2 * CHIPS)), device_id_type=MESH_IDS)
-
-    @pl.loop(0, rows // 128)
-    def _(part):
-        span = pl.ds(pl.multiple_of(part * 128, 128), 128)
-        widened = resid_ref[span, :].astype(jnp.float32)
-        inv_rms = lax.rsqrt(jnp.mean(widened * widened, axis=-1, keepdims=True) + EPSILON)
-        normed[span, :] = (widened * inv_rms * gain_ref[...]).astype(jnp.bfloat16)
 
     pl.semaphore_wait(barrier, 2 * CHIPS - 1)
     for load in loads:
@@ -198,8 +255,8 @@
     remote(q_stage.at[partner], q_out.at[whole(partner), :], q_send.at[0, 0], q_recv.at[0, 0], partner).wait()
 
 
-def project_heads(residual, gain, cosines, sines, wq_all, w_key, w_value):
-    rows, width = residual.shape
+def project_heads(normed, cosines, sines, wq_all, w_key, w_value):
+    rows, width = normed.shape
     heads = wq_all.shape[0]
     tokens = rows * heads
     tiles = rows // SEND_ROWS
@@ -209,13 +266,12 @@
     return pl.pallas_call(
         functools.partial(heads_kernel, rows),
         out_shape=(jax.ShapeDtypeStruct((tokens, HEAD_DIM), jnp.bfloat16), jax.ShapeDtypeStruct((2, tokens, HEAD_DIM), jnp.bfloat16)),
-        in_specs=[vmem, vmem, vmem, vmem, anywhere, anywhere, anywhere],
+        in_specs=[vmem, vmem, vmem, anywhere, anywhere, anywhere],
         out_specs=(anywhere, anywhere),
         scratch_shapes=[
             pltpu.VMEM(wq_all.shape, jnp.bfloat16),
             pltpu.VMEM(w_key.shape, jnp.bfloat16),
             pltpu.VMEM(w_value.shape, jnp.bfloat16),
-            pltpu.VMEM((rows, width), jnp.bfloat16),
             pltpu.VMEM((heads, rows, HEAD_DIM), jnp.bfloat16),
             pltpu.VMEM((2, CHIPS, rows, HEAD_DIM), jnp.bfloat16),
             dma((3,)),
@@ -228,7 +284,7 @@
         compiler_params=pltpu.CompilerParams(collective_id=0, has_side_effects=True, vmem_limit_bytes=56 * 1024 * 1024),
         cost_estimate=pl.CostEstimate(flops=2 * rows * width * 4096, bytes_accessed=40_000_000, transcendentals=0),
         name="project_heads",
-    )(residual, gain, cosines, sines, wq_all, w_key, w_value)
+    )(normed, cosines, sines, wq_all, w_key, w_value)
 
 
 def solution(mesh):
@@ -237,17 +293,46 @@
     def exchange(rows, bit):
         return lax.ppermute(rows, "tp", [(i, i ^ bit) for i in range(group_size)])
 
+    def share_head(rows, dev_index):
+        half = rows.shape[0] // 2
+        first, second = rows[:half], rows[half:]
+        first_x = lax.ppermute(first, "tp", [(0, 2)])
+        second_y = lax.ppermute(second, "tp", [(0, 4)])
+        first = jnp.where(dev_index == 2, first_x, first)
+        second = jnp.where(dev_index == 4, second_y, second)
+        first_y = lax.ppermute(first, "tp", [(0, 4), (2, 6)])
+        second_x = lax.ppermute(second, "tp", [(0, 2), (4, 6)])
+        first = jnp.where(dev_index >= 4, first_y, first)
+        second = jnp.where(dev_index % 4 >= 2, second_x, second)
+        both = jnp.concatenate([first, second], axis=0)
+        other = lax.ppermute(both, "tp", [(0, 1), (2, 3), (4, 5), (6, 7)])
+        return jnp.where(dev_index % 2 == 1, other, both)
+
     def local_body(token_ids, positions, table_rows, norm_scale, w_query, w_key, w_value):
         dev_index = lax.axis_index("tp")
-        vocab_rows, _ = table_rows.shape
+        vocab_rows, model_width = table_rows.shape
         wq_all = lax.all_gather(w_query, "tp", axis=0)
-        local_ids = token_ids - dev_index * vocab_rows
-        inside = (local_ids >= 0) & (local_ids < vocab_rows)
-        local_ids = jnp.where(inside, local_ids, -1)
+        head = share_head(table_rows[:HEAD_ROWS], dev_index)
         tokens = token_ids.shape[0]
         block_rows = tokens // group_size
-        chunk_rows = block_rows // CHUNKS
+        extra_rows = block_rows - TAIL_ROWS
+        chunk_rows = TAIL_ROWS // CHUNKS
         half = chunk_rows // 2
+
+        blocks = token_ids.reshape(group_size, block_rows)
+        in_tail = blocks >= HEAD_ROWS
+        earlier = (lax.broadcasted_iota(jnp.int32, (block_rows, block_rows), 0) < lax.broadcasted_iota(jnp.int32, (block_rows, block_rows), 1)).astype(jnp.bfloat16)
+        ranks = jnp.dot(in_tail.astype(jnp.bfloat16), earlier, preferred_element_type=jnp.float32).astype(jnp.int32)
+        ranks = jnp.where(in_tail, ranks, -1)
+
+        def ranked_ids(first, count):
+            wanted = lax.broadcasted_iota(jnp.int32, (group_size, block_rows, count), 2) + first
+            ids = jnp.sum(jnp.where(ranks[:, :, None] == wanted, blocks[:, :, None] + 1, 0), axis=1) - 1
+            local = ids - dev_index * vocab_rows
+            return jnp.where((ids >= 0) & (local >= 0) & (local < vocab_rows), local, -1)
+
+        most = jnp.max(jnp.sum(in_tail.astype(jnp.int32), axis=1))
+        over = (most > TAIL_ROWS).astype(jnp.int32)
 
         def arrange(values):
             view = values.reshape(2, 2, 2, CHUNKS, 2, half)
@@ -259,17 +344,18 @@
             second = halves[:, :, 1]
             return jnp.stack([first, second], axis=2).reshape(CHUNKS, 2, 4 * chunk_rows)
 
-        ids = arrange(local_ids)
+        call_rows = 4 * chunk_rows
+        ids = arrange(ranked_ids(0, TAIL_ROWS)).reshape(-1, TILE)
         owned = ids >= 0
-        pair_ids = jnp.where(owned, (ids // 2) * 2, -1)
-        lane = (jnp.arange(4 * chunk_rows, dtype=jnp.int32) % TILE) * 2
-        cols = jnp.where(owned, lane + ids % 2, -1)
-        counts = jnp.sum(owned.astype(jnp.int32).reshape(CHUNKS, 2, 4 * chunk_rows // TILE, TILE), axis=-1)
+        pair_ids = jnp.where(owned, (ids // 2) * 2, -1).reshape(-1)
+        lane = jnp.arange(TILE, dtype=jnp.int32) * 2
+        cols = jnp.where(owned, lane + ids % 2, -1).astype(jnp.float32)[:, None, :]
+        counts = jnp.sum(owned.astype(jnp.int32), axis=-1)
 
         def gather(chunk, side, after):
-            return gather_rows(pair_ids[chunk, side], counts[chunk, side], cols[chunk, side][:, None], table_rows, after)
-
-        pieces = []
+            return gather_rows((2 * chunk + side) * call_rows, call_rows, pair_ids, counts, cols, table_rows, after)
+
+        pieces, sums = [], []
         after, late, late_next = [], [], []
         for chunk in range(CHUNKS):
             other = gather(chunk, 1, after + late + ([wq_all] if chunk == 2 else []))
@@ -286,12 +372,30 @@
                 near_send = mine[keep[1]] + got[keep[1]] + back[half:]
                 back2 = exchange(near_send, bits[1])
                 after.append(sent)
+                sums.append(sent)
                 late_next.append(near_send)
-                pieces.append(mine[keep[0]] + got[keep[0]] + back[:half] + back2)
-        residual = jnp.concatenate(pieces, axis=0)
+                pieces += [mine[keep[0]] + got[keep[0]] + back[:half], back2]
+
+        def second_exchange(rows):
+            ids = ranked_ids(TAIL_ROWS, extra_rows).reshape(-1)
+            normalizer = jnp.asarray(math.sqrt(model_width), dtype=jnp.bfloat16)
+            picked = jnp.take(rows, jnp.maximum(ids, 0), axis=0, mode="clip") * normalizer
+            partial = jnp.where(ids[:, None] >= 0, picked, jnp.zeros((), jnp.bfloat16))
+            return lax.psum_scatter(partial, "tp", scatter_dimension=0, tiled=True)
+
+        def no_exchange(rows):
+            return jnp.zeros((extra_rows, model_width), jnp.bfloat16)
+
+        over, _ = lax.optimization_barrier((over, sums[2]))
+        more = lax.pmax(over, "dp")
+        asked, _ = lax.optimization_barrier((more, pieces[-5]))
+        extra = lax.cond(asked > 0, second_exchange, no_exchange, table_rows)
+        places = jnp.where(in_tail, HEAD_ROWS + ranks, blocks)
+        own_places = lax.dynamic_index_in_dim(places, dev_index, 0, keepdims=False)
+        residual, normed = finish_rows(more.reshape(1), own_places[:, None], (1.0 + norm_scale)[None, :], head, extra, pieces)
         own = lax.dynamic_slice_in_dim(positions, dev_index * block_rows, block_rows)
         cosines, sines = rope_tables(own)
-        queries, keys_values = project_heads(residual, (1.0 + norm_scale)[None, :], cosines, sines, wq_all, w_key, w_value)
+        queries, keys_values = project_heads(normed, cosines, sines, wq_all, w_key, w_value)
         return residual, queries[:, None, :], keys_values[0][:, None, :], keys_values[1][:, None, :]
 
     head_spec = P("dp", "tp", None)

time: 420 us -> 423 us (level)
  Pallas kernels: 223 us -> 191 us
  starting transfers between devices: 20.9 us -> 37.1 us
  local copies, waits for them, and re-layouts: 20.9 us -> 36.2 us
  blocking collectives: 0 us -> 4.73 us
    pallas_call x8 -> x11, Pallas kernels: 123 us -> 92.5 us  [the longest x10 77.7 us: gather_rows(): pl.pallas_call(functools.partial(gather_kernel, base, tiles, width), grid...]
    ppermute x0 -> x5, starting transfers between devices: none -> 20.5 us  [the longest x1 5.96 us: share_head(): first_x = lax.ppermute(first, 'tp', [(0, 2)])]
    unnamed x42 -> x81, local copies, waits for them, and re-layouts: 3.15 us -> 22.3 us
    unnamed x7 -> x0, other arithmetic: 15.2 us -> none
    select_n x2 -> x6, other arithmetic: 0.15 us -> 8.8 us  [the longest x1 3.73 us: share_head(): first = jnp.where(dev_index == 2, first_x, first)]
    add x0 -> x3, other arithmetic: none -> 8.11 us  [local_body(): pieces += [mine[keep[0]] + got[keep[0]] + back[:half], back2]]
    another operation x9 -> x3, local copies, waits for them, and re-layouts: 8.88 us -> 1.61 us  [gather(): cols[chunk, side][:, None]]
    pmax x0 -> x1, blocking collectives: none -> 4.73 us  [local_body(): more = lax.pmax(over, 'dp')]
  transfers between devices with their start and end apart: 21 -> 31, of which waited for: 12 -> 11; matrix products, arithmetic and copies ran while one was open for 13% -> 13% of each run, Pallas kernels for 26% -> 19%
where the time goes in v1:
time: 423 us; the launch traced here: 416 us
  Pallas kernels  191 us (45%)
  waiting for transfers between devices  85.6 us (20%)
  other arithmetic  45.5 us (11%)
  starting transfers between devices  37.1 us (9%)
  local copies, waits for them, and re-layouts  36.2 us (9%)
  between operations  15.9 us (4%)
  blocking collectives  4.73 us (1%)
    pallas_call x1, Pallas kernels, project_heads(): pl.pallas_call(functools.partial(heads_kernel, rows), out_shape=(jax.Shap...  98 us
    ppermute x25, waiting for transfers between devices, exchange(): return lax.ppermute(rows, 'tp', [(i, i ^ bit) for i in range(group_size)])  84.9 us
    pallas_call x10, Pallas kernels, gather_rows(): pl.pallas_call(functools.partial(gather_kernel, base, tiles, width), grid...  77.7 us
    unnamed x81, local copies, waits for them, and re-layouts  22.3 us
    ppermute x25, starting transfers between devices, exchange(): return lax.ppermute(rows, 'tp', [(i, i ^ bit) for i in range(group_size)])  16.6 us
    pallas_call x1, Pallas kernels, finish_rows(): pl.pallas_call(functools.partial(finish_kernel, len(tail_pieces)), out_sh...  14.9 us
    add x5, other arithmetic, local_body(): sent = mine[far] + got[far]  12.3 us
  transfers between devices with their start and end apart: 31, of which 11 were waited for; matrix products, arithmetic and copies ran while one was open for 13% of the time, Pallas kernels for 19%

profile of v1, /device:TPU:0, one launch (start us, length us, event | category | flops | bytes accessed | tf_op | source)
XLA Modules:
  0.0 416.0 jit_solution(17187470517987821640)
XLA Ops:
  9.2 3.0 select_reduce_fusion.1
  15.4 7.8 %gather_rows.10.rest_0_ = bf16[512,2304]{1,0:T(8,128)(2,1)} custom-call(s32[5120]{0:T(1024)} %fusion.8.pair_ids, s32[40]{0:T(128)} %reduce_sum.41.counts, f32[40,1,128]{2,1,0:T(1,128)} %fusion.9.cols_ref, bf16[32000,2304]{1,0:T(8,128)(2,1)} %table_ref.19), custom_call_target="tpu_custom_call" | custom-call | flops 10240000000 | bytes 7077888 | tf_op jit(solution)/shard_map/gather_rows/pallas_call | solution.py:91
  23.9 7.7 %gather_rows.11 = bf16[512,2304]{1,0:T(8,128)(2,1)} custom-call(s32[5120]{0:T(1024)} %fusion.8.pair_ids, s32[40]{0:T(128)} %reduce_sum.41.counts, f32[40,1,128]{2,1,0:T(1,128)} %fusion.9.cols_ref, bf16[32000,2304]{1,0:T(8,128)(2,1)} %table_ref.19, bf16[512,2304]{1,0:T(8,128)(2,1)} %gather_rows.10.rest_0_), custom_call_target="tpu_custom_call" | custom-call | flops 10240000000 | bytes 7077888 | tf_op jit(solution)/shard_map/gather_rows/pallas_call | solution.py:91
  31.7 3.2 slice_add_fusion.8
  34.9 7.7 %gather_rows.12.rest_0_ = bf16[512,2304]{1,0:T(8,128)(2,1)} custom-call(s32[5120]{0:T(1024)} %fusion.8.pair_ids, s32[40]{0:T(128)} %reduce_sum.41.counts, f32[40,1,128]{2,1,0:T(1,128)} %fusion.9.cols_ref, bf16[32000,2304]{1,0:T(8,128)(2,1)} %table_ref.19, bf16[128,2304]{1,0:T(8,128)(2,1)} %get-tuple-element.80.rest_0_, ...), custom_call_target="tpu_custom_call" | custom-call | flops 10240000000 | bytes 7077888 | tf_op jit(solution)/shard_map/gather_rows/pallas_call | solution.py:91
  42.8 3.6 fusion.14
  46.4 6.0 %collective-permute-start.2 = (bf16[320,2304]{1,0:T(8,128)(2,1)}, bf16[320,2304]{1,0:T(8,128)(2,1)}, u32[]{:S(2)}, u32[]{:S(2)}) collective-permute-start(bf16[320,2304]{1,0:T(8,128)(2,1)} %get-tuple-element.37), channel_id=1, source_target_pairs={{0,2},{8,10}} | collective-permute-start | bytes 4423688 | tf_op jit(solution)/shard_map/ppermute | solution.py:299
  52.3 2.5 collective-permute-start.4
  56.6 7.9 %gather_rows.13 = bf16[512,2304]{1,0:T(8,128)(2,1)} custom-call(s32[5120]{0:T(1024)} %fusion.8.pair_ids, s32[40]{0:T(128)} %reduce_sum.41.counts, f32[40,1,128]{2,1,0:T(1,128)} %fusion.9.cols_ref, bf16[32000,2304]{1,0:T(8,128)(2,1)} %table_ref.19, bf16[512,2304]{1,0:T(8,128)(2,1)} %gather_rows.12.rest_0_), custom_call_target="tpu_custom_call" | custom-call | flops 10240000000 | bytes 7077888 | tf_op jit(solution)/shard_map/gather_rows/pallas_call | solution.py:91
  64.5 33.8 %collective-permute-done.7 = bf16[128,2304]{1,0:T(8,128)(2,1)} collective-permute-done((bf16[128,2304]{1,0:T(8,128)(2,1)}, bf16[128,2304]{1,0:T(8,128)(2,1)}, u32[]{:S(2)}, u32[]{:S(2)}) %collective-permute-start.7) | collective-permute-done | bytes 589856 | tf_op jit(solution)/shard_map/ppermute | solution.py:294
  98.3 2.7 slice_add_fusion.36
  101.0 2.2 slice_add_fusion.6
  103.2 2.5 collective-permute-start.10
  105.7 7.9 %gather_rows.14.rest_0_ = bf16[512,2304]{1,0:T(8,128)(2,1)} custom-call(s32[5120]{0:T(1024)} %fusion.8.pair_ids, s32[40]{0:T(128)} %reduce_sum.41.counts, f32[40,1,128]{2,1,0:T(1,128)} %fusion.9.cols_ref, bf16[32000,2304]{1,0:T(8,128)(2,1)} %table_ref.19, bf16[128,2304]{1,0:T(8,128)(2,1)} %get-tuple-element.78.rest_0_, bf16[128,2304]{1,0:T(8,128)(2,1)} %copy-done.32, ...), custom_call_target="tpu_custom_call" | custom-call | flops 10240000000 | bytes 7077888 | tf_op jit(solution)/shard_map/gather_rows/pallas_call | solution.py:91
  114.4 3.1 multiply_sine_fusion
  117.5 2.8 slice_add_fusion.32
  120.3 7.8 %gather_rows.15 = bf16[512,2304]{1,0:T(8,128)(2,1)} custom-call(s32[5120]{0:T(1024)} %fusion.8.pair_ids, s32[40]{0:T(128)} %reduce_sum.41.counts, f32[40,1,128]{2,1,0:T(1,128)} %fusion.9.cols_ref, bf16[32000,2304]{1,0:T(8,128)(2,1)} %table_ref.19, bf16[512,2304]{1,0:T(8,128)(2,1)} %gather_rows.14.rest_0_), custom_call_target="tpu_custom_call" | custom-call | flops 10240000000 | bytes 7077888 | tf_op jit(solution)/shard_map/gather_rows/pallas_call | solution.py:91
  128.1 2.7 slice_add_fusion.4
  130.8 7.7 %gather_rows.16.rest_0_ = bf16[512,2304]{1,0:T(8,128)(2,1)} custom-call(s32[5120]{0:T(1024)} %fusion.8.pair_ids, s32[40]{0:T(128)} %reduce_sum.41.counts, f32[40,1,128]{2,1,0:T(1,128)} %fusion.9.cols_ref, bf16[32000,2304]{1,0:T(8,128)(2,1)} %table_ref.19, bf16[128,2304]{1,0:T(8,128)(2,1)} %get-tuple-element.76.rest_0_, ...), custom_call_target="tpu_custom_call" | custom-call | flops 10240000000 | bytes 7077888 | tf_op jit(solution)/shard_map/gather_rows/pallas_call | solution.py:91
  139.1 3.7 broadcast_select_fusion.3
  142.8 5.5 %collective-permute-start.5 = (bf16[320,2304]{1,0:T(8,128)(2,1)}, bf16[320,2304]{1,0:T(8,128)(2,1)}, u32[]{:S(2)}, u32[]{:S(2)}) collective-permute-start(bf16[320,2304]{1,0:T(8,128)(2,1)} %get-tuple-element.36), channel_id=1, source_target_pairs={{0,2},{4,6},{8,10},{12,14}} | collective-permute-start | bytes 4423688 | tf_op jit(solution)/shard_map/ppermute | solution.py:304
  148.3 2.6 collective-permute-start.3
  150.9 7.7 %gather_rows.17 = bf16[512,2304]{1,0:T(8,128)(2,1)} custom-call(s32[5120]{0:T(1024)} %fusion.8.pair_ids, s32[40]{0:T(128)} %reduce_sum.41.counts, f32[40,1,128]{2,1,0:T(1,128)} %fusion.9.cols_ref, bf16[32000,2304]{1,0:T(8,128)(2,1)} %table_ref.19, bf16[512,2304]{1,0:T(8,128)(2,1)} %gather_rows.16.rest_0_), custom_call_target="tpu_custom_call" | custom-call | flops 10240000000 | bytes 7077888 | tf_op jit(solution)/shard_map/gather_rows/pallas_call | solution.py:91
  158.7 21.3 %collective-permute-done.19 = bf16[128,2304]{1,0:T(8,128)(2,1)} collective-permute-done((bf16[128,2304]{1,0:T(8,128)(2,1)S(1)}, bf16[128,2304]{1,0:T(8,128)(2,1)}, u32[]{:S(2)}, u32[]{:S(2)}) %collective-permute-start.19) | collective-permute-done | bytes 589856 | tf_op jit(solution)/shard_map/ppermute | solution.py:294
  180.5 2.0 collective-permute-start.16
  182.6 3.0 slice_add_fusion.24
  185.6 2.4 slice_add_fusion.2
  188.1 7.7 %gather_rows.18.rest_0_ = bf16[512,2304]{1,0:T(8,128)(2,1)} custom-call(s32[5120]{0:T(1024)} %fusion.8.pair_ids, s32[40]{0:T(128)} %reduce_sum.41.counts, f32[40,1,128]{2,1,0:T(1,128)} %fusion.9.cols_ref, bf16[32000,2304]{1,0:T(8,128)(2,1)} %table_ref.19, bf16[128,2304]{1,0:T(8,128)(2,1)} %get-tuple-element.67.rest_0_, ...), custom_call_target="tpu_custom_call" | custom-call | flops 10240000000 | bytes 7077888 | tf_op jit(solution)/shard_map/gather_rows/pallas_call | solution.py:91
  197.5 2.1 broadcast_select_fusion.4
  199.5 2.0 pad_maximum_fusion
  201.6 3.9 collective-permute-start.6
  205.5 4.7 %pmax.7 = s32[]{:T(128)} all-reduce(s32[]{:T(128)S(6)} %convert_element_type.32), channel_id=1, replica_groups=mesh['dp'=2,'tp'=8] {'dp'}, use_global_device_ids=true, to_apply=%region_4.5 | all-reduce | flops 1 | bytes 8 | tf_op jit(solution)/shard_map/pmax | solution.py:390
  210.3 2.0 collective-permute-start.13
  212.3 7.7 %gather_rows.19 = bf16[512,2304]{1,0:T(8,128)(2,1)} custom-call(s32[5120]{0:T(1024)} %fusion.8.pair_ids, s32[40]{0:T(128)} %reduce_sum.41.counts, f32[40,1,128]{2,1,0:T(1,128)} %fusion.9.cols_ref, bf16[32000,2304]{1,0:T(8,128)(2,1)} %table_ref.19, bf16[512,2304]{1,0:T(8,128)(2,1)} %gather_rows.18.rest_0_), custom_call_target="tpu_custom_call" | custom-call | flops 10240000000 | bytes 7077888 | tf_op jit(solution)/shard_map/gather_rows/pallas_call | solution.py:91
  223.8 12.6 %collective-permute-done.23 = bf16[128,2304]{1,0:T(8,128)(2,1)S(1)} collective-permute-done((bf16[128,2304]{1,0:T(8,128)(2,1)}, bf16[128,2304]{1,0:T(8,128)(2,1)S(1)}, u32[]{:S(2)}, u32[]{:S(2)}) %collective-permute-start.23) | collective-permute-done | bytes 589856 | tf_op jit(solution)/shard_map/ppermute | solution.py:294
  236.5 2.7 slice_add_fusion.18
  239.1 1.9 collective-permute-start.17
  241.0 5.3 %collective-permute-done.26 = bf16[128,2304]{1,0:T(8,128)(2,1)S(1)} collective-permute-done((bf16[128,2304]{1,0:T(8,128)(2,1)S(1)}, bf16[128,2304]{1,0:T(8,128)(2,1)S(1)}, u32[]{:S(2)}, u32[]{:S(2)}) %collective-permute-start.26) | collective-permute-done | bytes 589856 | tf_op jit(solution)/shard_map/ppermute | solution.py:294
  248.4 2.4 slice_add_fusion.10
  252.9 3.3 collective-permute-done.18.refs_7_
  257.0 2.0 collective-permute-start.27
  259.0 3.6 collective-permute-done.14.refs_15_
  266.8 1.8 collective-permute-done.27.refs_17_
  284.8 14.9 %finish_rows.1 = (bf16[1024,2304]{1,0:T(8,128)(2,1)}, bf16[1024,2304]{1,0:T(8,128)(2,1)S(1)}) custom-call(s32[1]{0:T(128)} %bitcast.6.more, s32[1024,1]{1,0:T(8,128)S(1)} %copy.39.cols_ref, f32[1,2304]{1,0:T(1,128)S(1)} %broadcast_in_dim.71.gain_ref, bf16[640,2304]{1,0:T(8,128)(2,1)S(1)} %broadcast_select_fusion.head_ref, ...), custom_call_target="tpu_custom_call" | custom-call | flops 6039797760 | bytes 16000000 | tf_op jit(solution)/shard_map/finish_rows/pallas_call | solution.py:145
  299.6 2.2 copy-done.20
  301.8 98.0 %project_heads.1 = (bf16[8192,256]{1,0:T(8,128)(2,1)}, bf16[2,8192,256]{2,1,0:T(8,128)(2,1)}) custom-call(bf16[1024,2304]{1,0:T(8,128)(2,1)} %copy-done.20, f32[1024,128]{1,0:T(8,128)} %get-tuple-element.85.cos_ref, f32[1024,128]{1,0:T(8,128)} %get-tuple-element.84.sin_ref, bf16[8,2304,256]{2,1,0:T(8,128)(2,1)} %bitcast.31, bf16[2304,1024]{1,0:T(8,128)(2,1)} %wk_hbm.1, ...), custom_call_target="tpu_custom_call" | custom-call | flops 19327352832 | bytes 40000000 | tf_op jit(solution)/shard_map/project_heads/pallas_call | solution.py:266
  399.9 6.6 %slice_bitcast_fusion = (bf16[8192,1,256]{2,0,1:T(8,128)(2,1)}, bf16[8192,1,256]{2,0,1:T(8,128)(2,1)}) fusion(bf16[2,8192,256]{2,1,0:T(8,128)(2,1)} %get-tuple-element.30), kind=kLoop, calls=%fused_computation.13 | loop fusion | bytes 16777216 | tf_op jit(solution)/shard_map/broadcast_in_dim;squeeze | solution.py:399
  407.1 2.0 copy.48
  (160 shorter events, 41.0 us)
Async XLA Ops:
  7.2 98.5 %all-gather.3.cloned.1.call-start = ((), (), s32[]{:S(2)}) async-start(), calls=%async_computation.2 | async-start | bytes 10616832 | tf_op jit(solution)/shard_map/all_gather | solution.py:314
  9.2 47.0 %copy-start.37 = (s32[8,1024]{1,0:T(8,128)}, s32[8,1024]{1,0:T(8,128)S(1)}, u32[]{:S(2)}) copy-start(s32[8,1024]{1,0:T(8,128)S(1)} %fusion.3) | copy-start | bytes 98308
  23.2 8.5 %collective-permute-start = (bf16[512,2304]{1,0:T(8,128)(2,1)}, bf16[512,2304]{1,0:T(8,128)(2,1)S(1)}, u32[]{:S(2)}, u32[]{:S(2)}) collective-permute-start(bf16[512,2304]{1,0:T(8,128)(2,1)} %gather_rows.10.rest_0_), channel_id=1, source_target_pairs={{0,1},{1,0},{2,3},{3,2},{4,5},{5,4},{6,7},{7,6},{8,9},{9,8},{10,11... | collective-permute-start | bytes 7077896 | tf_op jit(solution)/shard_map/ppermute | solution.py:294
  31.7 11.0 %copy-start.34 = (bf16[512,2304]{1,0:T(8,128)(2,1)}, bf16[512,2304]{1,0:T(8,128)(2,1)S(1)}, u32[]{:S(2)}) copy-start(bf16[512,2304]{1,0:T(8,128)(2,1)S(1)} %collective-permute-done) | copy-start | bytes 7077892
  42.7 13.8 %copy-start.31 = (bf16[128,2304]{1,0:T(8,128)(2,1)S(1)}, bf16[128,2304]{1,0:T(8,128)(2,1)}, u32[]{:S(2)}) copy-start(bf16[128,2304]{1,0:T(8,128)(2,1)} %get-tuple-element.79.rest_1_) | copy-start | bytes 1769476
  42.7 58.3 %collective-permute-start.1 = (bf16[512,2304]{1,0:T(8,128)(2,1)}, bf16[512,2304]{1,0:T(8,128)(2,1)}, u32[]{:S(2)}, u32[]{:S(2)}) collective-permute-start(bf16[512,2304]{1,0:T(8,128)(2,1)} %gather_rows.12.rest_0_), channel_id=1, source_target_pairs={{0,1},{1,0},{2,3},{3,2},{4,5},{5,4},{6,7},{7,6},{8,9},{9,8},{10,11... | collective-permute-start | bytes 7077896 | tf_op jit(solution)/shard_map/ppermute | solution.py:294
  46.4 92.7 %collective-permute-start.2 = (bf16[320,2304]{1,0:T(8,128)(2,1)}, bf16[320,2304]{1,0:T(8,128)(2,1)}, u32[]{:S(2)}, u32[]{:S(2)}) collective-permute-start(bf16[320,2304]{1,0:T(8,128)(2,1)} %get-tuple-element.37), channel_id=1, source_target_pairs={{0,2},{8,10}} | collective-permute-start | bytes 4423688 | tf_op jit(solution)/shard_map/ppermute | solution.py:299
  52.3 86.7 %collective-permute-start.4 = (bf16[320,2304]{1,0:T(8,128)(2,1)}, bf16[320,2304]{1,0:T(8,128)(2,1)}, u32[]{:S(2)}, u32[]{:S(2)}) collective-permute-start(bf16[320,2304]{1,0:T(8,128)(2,1)} %get-tuple-element.38), channel_id=1, source_target_pairs={{0,4},{8,12}} | collective-permute-start | bytes 4423688 | tf_op jit(solution)/shard_map/ppermute | solution.py:300
  56.5 41.8 %copy-start.26 = (bf16[512,2304]{1,0:T(8,128)(2,1)S(1)}, bf16[512,2304]{1,0:T(8,128)(2,1)}, u32[]{:S(2)}) copy-start(bf16[512,2304]{1,0:T(8,128)(2,1)} %gather_rows.11) | copy-start | bytes 7077892
  56.5 41.8 %collective-permute-start.7 = (bf16[128,2304]{1,0:T(8,128)(2,1)}, bf16[128,2304]{1,0:T(8,128)(2,1)}, u32[]{:S(2)}, u32[]{:S(2)}) collective-permute-start(bf16[128,2304]{1,0:T(8,128)(2,1)} %get-tuple-element.80.rest_0_), channel_id=1, source_target_pairs={{0,2},{1,3},{2,0},{3,1},{4,6},{5,7},{6,4},{7,5},{8,10},{9,11},{10,... | collective-permute-start | bytes 1769480 | tf_op jit(solution)/shard_map/ppermute | solution.py:294
  56.5 41.7 %collective-permute-start.8 = (bf16[128,2304]{1,0:T(8,128)(2,1)S(1)}, bf16[128,2304]{1,0:T(8,128)(2,1)}, u32[]{:S(2)}, u32[]{:S(2)}) collective-permute-start(bf16[128,2304]{1,0:T(8,128)(2,1)S(1)} %copy-done.31), channel_id=1, source_target_pairs={{0,4},{1,5},{2,6},{3,7},{4,0},{5,1},{6,2},{7,3},{8,12},{9,13},{10,... | collective-permute-start | bytes 1769480 | tf_op jit(solution)/shard_map/ppermute | solution.py:294
  64.5 36.5 %copy-start.27 = (bf16[512,2304]{1,0:T(8,128)(2,1)S(1)}, bf16[512,2304]{1,0:T(8,128)(2,1)}, u32[]{:S(2)}) copy-start(bf16[512,2304]{1,0:T(8,128)(2,1)} %gather_rows.13) | copy-start | bytes 7077892
  103.2 14.3 %collective-permute-start.10 = (bf16[128,2304]{1,0:T(8,128)(2,1)}, bf16[128,2304]{1,0:T(8,128)(2,1)}, u32[]{:S(2)}, u32[]{:S(2)}) collective-permute-start(bf16[128,2304]{1,0:T(8,128)(2,1)} %get-tuple-element.78.rest_0_), channel_id=1, source_target_pairs={{0,2},{1,3},{2,0},{3,1},{4,6},{5,7},{6,4},{7,5},{8,10},{9,11},{10,... | collective-permute-start | bytes 1769480 | tf_op jit(solution)/shard_map/ppermute | solution.py:294
  105.7 11.8 %collective-permute-start.11 = (bf16[128,2304]{1,0:T(8,128)(2,1)S(1)}, bf16[128,2304]{1,0:T(8,128)(2,1)}, u32[]{:S(2)}, u32[]{:S(2)}) collective-permute-start(bf16[128,2304]{1,0:T(8,128)(2,1)S(1)} %get-tuple-element.77.rest_1_), channel_id=1, source_target_pairs={{0,4},{1,5},{2,6},{3,7},{4,0},{5,1},{6,2},{7,3},{8,12},{9,13},{10,... | collective-permute-start | bytes 1769480 | tf_op jit(solution)/shard_map/ppermute | solution.py:294
  105.7 8.0 %copy-start.39 = (f32[2304]{0:T(1024)S(1)}, f32[2304]{0:T(1024)}, u32[]{:S(2)}) copy-start(f32[2304]{0:T(1024)} %param.12) | copy-start | bytes 27652
  105.7 11.8 %copy-start.28 = (bf16[512,2304]{1,0:T(8,128)(2,1)S(1)}, bf16[512,2304]{1,0:T(8,128)(2,1)}, u32[]{:S(2)}) copy-start(bf16[512,2304]{1,0:T(8,128)(2,1)} %gather_rows.13) | copy-start | bytes 7077892
  113.6 14.4 %collective-permute-start.9 = (bf16[512,2304]{1,0:T(8,128)(2,1)}, bf16[512,2304]{1,0:T(8,128)(2,1)}, u32[]{:S(2)}, u32[]{:S(2)}) collective-permute-start(bf16[512,2304]{1,0:T(8,128)(2,1)} %gather_rows.14.rest_0_), channel_id=1, source_target_pairs={{0,1},{1,0},{2,3},{3,2},{4,5},{5,4},{6,7},{7,6},{8,9},{9,8},{10,11... | collective-permute-start | bytes 7077896 | tf_op jit(solution)/shard_map/ppermute | solution.py:294
  138.5 12.4 %copy-start.33 = (bf16[128,2304]{1,0:T(8,128)(2,1)S(1)}, bf16[128,2304]{1,0:T(8,128)(2,1)}, u32[]{:S(2)}) copy-start(bf16[128,2304]{1,0:T(8,128)(2,1)} %get-tuple-element.76.rest_0_) | copy-start | bytes 1769476
  138.6 47.1 %collective-permute-start.12 = (bf16[512,2304]{1,0:T(8,128)(2,1)}, bf16[512,2304]{1,0:T(8,128)(2,1)}, u32[]{:S(2)}, u32[]{:S(2)}) collective-permute-start(bf16[512,2304]{1,0:T(8,128)(2,1)} %gather_rows.16.rest_0_), channel_id=1, source_target_pairs={{0,1},{1,0},{2,3},{3,2},{4,5},{5,4},{6,7},{7,6},{8,9},{9,8},{10,11... | collective-permute-start | bytes 7077896 | tf_op jit(solution)/shard_map/ppermute | solution.py:294
  142.8 53.1 %collective-permute-start.5 = (bf16[320,2304]{1,0:T(8,128)(2,1)}, bf16[320,2304]{1,0:T(8,128)(2,1)}, u32[]{:S(2)}, u32[]{:S(2)}) collective-permute-start(bf16[320,2304]{1,0:T(8,128)(2,1)} %get-tuple-element.36), channel_id=1, source_target_pairs={{0,2},{4,6},{8,10},{12,14}} | collective-permute-start | bytes 4423688 | tf_op jit(solution)/shard_map/ppermute | solution.py:304
  148.3 49.1 %collective-permute-start.3 = (bf16[320,2304]{1,0:T(8,128)(2,1)}, bf16[320,2304]{1,0:T(8,128)(2,1)}, u32[]{:S(2)}, u32[]{:S(2)}) collective-permute-start(bf16[320,2304]{1,0:T(8,128)(2,1)} %get-tuple-element.35), channel_id=1, source_target_pairs={{0,4},{2,6},{8,12},{10,14}} | collective-permute-start | bytes 4423688 | tf_op jit(solution)/shard_map/ppermute | solution.py:303
  150.9 29.1 %collective-permute-start.19 = (bf16[128,2304]{1,0:T(8,128)(2,1)S(1)}, bf16[128,2304]{1,0:T(8,128)(2,1)}, u32[]{:S(2)}, u32[]{:S(2)}) collective-permute-start(bf16[128,2304]{1,0:T(8,128)(2,1)S(1)} %copy-done.33), channel_id=1, source_target_pairs={{0,2},{1,3},{2,0},{3,1},{4,6},{5,7},{6,4},{7,5},{8,10},{9,11},{10,... | collective-permute-start | bytes 1769480 | tf_op jit(solution)/shard_map/ppermute | solution.py:294
  150.9 29.6 %collective-permute-start.21 = (bf16[128,2304]{1,0:T(8,128)(2,1)}, bf16[128,2304]{1,0:T(8,128)(2,1)}, u32[]{:S(2)}, u32[]{:S(2)}) collective-permute-start(bf16[128,2304]{1,0:T(8,128)(2,1)} %get-tuple-element.75.rest_1_), channel_id=1, source_target_pairs={{0,4},{1,5},{2,6},{3,7},{4,0},{5,1},{6,2},{7,3},{8,12},{9,13},{10,... | collective-permute-start | bytes 1769480 | tf_op jit(solution)/shard_map/ppermute | solution.py:294
  158.7 27.0 %copy-start.25 = (bf16[512,2304]{1,0:T(8,128)(2,1)S(1)}, bf16[512,2304]{1,0:T(8,128)(2,1)}, u32[]{:S(2)}) copy-start(bf16[512,2304]{1,0:T(8,128)(2,1)} %gather_rows.17) | copy-start | bytes 7077892
  180.0 59.1 %collective-permute-start.15 = (bf16[64,2304]{1,0:T(8,128)(2,1)}, bf16[64,2304]{1,0:T(8,128)(2,1)S(1)}, u32[]{:S(2)}, u32[]{:S(2)}) collective-permute-start(bf16[64,2304]{1,0:T(8,128)(2,1)} %get-tuple-element.73.rest_2_), channel_id=1, source_target_pairs={{0,4},{1,5},{2,6},{3,7},{4,0},{5,1},{6,2},{7,3},{8,12},{9,13},{10,... | collective-permute-start | bytes 884744 | tf_op jit(solution)/shard_map/ppermute | solution.py:294
  180.5 70.3 %collective-permute-start.16 = (bf16[64,2304]{1,0:T(8,128)(2,1)}, bf16[64,2304]{1,0:T(8,128)(2,1)S(1)}, u32[]{:S(2)}, u32[]{:S(2)}) collective-permute-start(bf16[64,2304]{1,0:T(8,128)(2,1)} %get-tuple-element.58.rest_3_), channel_id=1, source_target_pairs={{0,2},{1,3},{2,0},{3,1},{4,6},{5,7},{6,4},{7,5},{8,10},{9,11},{10,... | collective-permute-start | bytes 884744 | tf_op jit(solution)/shard_map/ppermute | solution.py:294
  195.8 24.2 %collective-permute-start.25 = (bf16[512,2304]{1,0:T(8,128)(2,1)}, bf16[512,2304]{1,0:T(8,128)(2,1)}, u32[]{:S(2)}, u32[]{:S(2)}) collective-permute-start(bf16[512,2304]{1,0:T(8,128)(2,1)} %gather_rows.18.rest_0_), channel_id=1, source_target_pairs={{0,1},{1,0},{2,3},{3,2},{4,5},{5,4},{6,7},{7,6},{8,9},{9,8},{10,11... | collective-permute-start | bytes 7077896 | tf_op jit(solution)/shard_map/ppermute | solution.py:294
  197.4 4.1 copy-start.21
  201.6 55.4 %collective-permute-start.6 = (bf16[640,2304]{1,0:T(8,128)(2,1)}, bf16[640,2304]{1,0:T(8,128)(2,1)}, u32[]{:S(2)}, u32[]{:S(2)}) collective-permute-start(bf16[640,2304]{1,0:T(8,128)(2,1)} %pad_maximum_fusion), channel_id=1, source_target_pairs={{0,1},{2,3},{4,5},{6,7},{8,9},{10,11},{12,13},{14,15}} | collective-permute-start | bytes 8847368 | tf_op jit(solution)/shard_map/ppermute | solution.py:308
  210.3 12.5 %collective-permute-start.13 = (bf16[128,2304]{1,0:T(8,128)(2,1)}, bf16[128,2304]{1,0:T(8,128)(2,1)}, u32[]{:S(2)}, u32[]{:S(2)}) collective-permute-start(bf16[128,2304]{1,0:T(8,128)(2,1)} %get-tuple-element.68.rest_1_), channel_id=1, source_target_pairs={{0,4},{1,5},{2,6},{3,7},{4,0},{5,1},{6,2},{7,3},{8,12},{9,13},{10,... | collective-permute-start | bytes 1769480 | tf_op jit(solution)/shard_map/ppermute | solution.py:294
  220.0 16.4 %collective-permute-start.23 = (bf16[128,2304]{1,0:T(8,128)(2,1)}, bf16[128,2304]{1,0:T(8,128)(2,1)S(1)}, u32[]{:S(2)}, u32[]{:S(2)}) collective-permute-start(bf16[128,2304]{1,0:T(8,128)(2,1)} %get-tuple-element.67.rest_0_), channel_id=1, source_target_pairs={{0,2},{1,3},{2,0},{3,1},{4,6},{5,7},{6,4},{7,5},{8,10},{9,11},{10,... | collective-permute-start | bytes 1769480 | tf_op jit(solution)/shard_map/ppermute | solution.py:294
  222.8 23.6 %collective-permute-start.26 = (bf16[128,2304]{1,0:T(8,128)(2,1)S(1)}, bf16[128,2304]{1,0:T(8,128)(2,1)S(1)}, u32[]{:S(2)}, u32[]{:S(2)}) collective-permute-start(bf16[128,2304]{1,0:T(8,128)(2,1)S(1)} %get-tuple-element.64), channel_id=1, source_target_pairs={{0,2},{1,3},{2,0},{3,1},{4,6},{5,7},{6,4},{7,5},{8,10},{9,11},{10,... | collective-permute-start | bytes 1769480 | tf_op jit(solution)/shard_map/ppermute | solution.py:294
  236.4 2.7 copy-start.36
  236.4 9.9 %copy-start.35 = (bf16[64,2304]{1,0:T(8,128)(2,1)S(1)}, bf16[64,2304]{1,0:T(8,128)(2,1)}, u32[]{:S(2)}) copy-start(bf16[64,2304]{1,0:T(8,128)(2,1)} %get-tuple-element.54.rest_3_) | copy-start | bytes 884740
  236.4 12.0 %copy-start.29 = (bf16[512,2304]{1,0:T(8,128)(2,1)S(1)}, bf16[512,2304]{1,0:T(8,128)(2,1)}, u32[]{:S(2)}) copy-start(bf16[512,2304]{1,0:T(8,128)(2,1)} %gather_rows.19) | copy-start | bytes 7077892
  236.4 10.4 %collective-permute-start.28 = (bf16[128,2304]{1,0:T(8,128)(2,1)S(1)}, bf16[128,2304]{1,0:T(8,128)(2,1)S(1)}, u32[]{:S(2)}, u32[]{:S(2)}) collective-permute-start(bf16[128,2304]{1,0:T(8,128)(2,1)S(1)} %get-tuple-element.63), channel_id=1, source_target_pairs={{0,4},{1,5},{2,6},{3,7},{4,0},{5,1},{6,2},{7,3},{8,12},{9,13},{10,... | collective-permute-start | bytes 1769480 | tf_op jit(solution)/shard_map/ppermute | solution.py:294
  239.1 11.7 %copy-start.10 = (bf16[64,2304]{1,0:T(8,128)(2,1)}, bf16[64,2304]{1,0:T(8,128)(2,1)S(1)}, u32[]{:S(2)}) copy-start(bf16[64,2304]{1,0:T(8,128)(2,1)S(1)} %collective-permute-done.15.refs_1_) | copy-start | bytes 884740
  239.1 12.4 %collective-permute-start.17 = (bf16[64,2304]{1,0:T(8,128)(2,1)S(1)}, bf16[64,2304]{1,0:T(8,128)(2,1)S(1)}, u32[]{:S(2)}, u32[]{:S(2)}) collective-permute-start(bf16[64,2304]{1,0:T(8,128)(2,1)S(1)} %copy-done.36), channel_id=1, source_target_pairs={{0,4},{1,5},{2,6},{3,7},{4,0},{5,1},{6,2},{7,3},{8,12},{9,13},{10,... | collective-permute-start | bytes 884744 | tf_op jit(solution)/shard_map/ppermute | solution.py:294
  246.4 9.9 %collective-permute-start.18 = (bf16[64,2304]{1,0:T(8,128)(2,1)S(1)}, bf16[64,2304]{1,0:T(8,128)(2,1)S(1)}, u32[]{:S(2)}, u32[]{:S(2)}) collective-permute-start(bf16[64,2304]{1,0:T(8,128)(2,1)S(1)} %copy-done.35), channel_id=1, source_target_pairs={{0,2},{1,3},{2,0},{3,1},{4,6},{5,7},{6,4},{7,5},{8,10},{9,11},{10,... | collective-permute-start | bytes 884744 | tf_op jit(solution)/shard_map/ppermute | solution.py:294
  246.8 16.9 %copy-start.22 = (bf16[320,2304]{1,0:T(8,128)(2,1)S(1)}, bf16[320,2304]{1,0:T(8,128)(2,1)}, u32[]{:S(2)}) copy-start(bf16[320,2304]{1,0:T(8,128)(2,1)} %copy-done.21) | copy-start | bytes 4423684
  246.8 16.9 %copy-start.24 = (bf16[320,2304]{1,0:T(8,128)(2,1)S(1)}, bf16[320,2304]{1,0:T(8,128)(2,1)}, u32[]{:S(2)}) copy-start(bf16[320,2304]{1,0:T(8,128)(2,1)} %copy-done.23) | copy-start | bytes 4423684
  246.8 15.8 %collective-permute-start.14 = (bf16[64,2304]{1,0:T(8,128)(2,1)S(1)}, bf16[64,2304]{1,0:T(8,128)(2,1)S(1)}, u32[]{:S(2)}, u32[]{:S(2)}) collective-permute-start(bf16[64,2304]{1,0:T(8,128)(2,1)S(1)} %get-tuple-element.46), channel_id=1, source_target_pairs={{0,2},{1,3},{2,0},{3,1},{4,6},{5,7},{6,4},{7,5},{8,10},{9,11},{10,... | collective-permute-start | bytes 884744 | tf_op jit(solution)/shard_map/ppermute | solution.py:294
  251.6 15.0 %collective-permute-start.20 = (bf16[64,2304]{1,0:T(8,128)(2,1)}, bf16[64,2304]{1,0:T(8,128)(2,1)}, u32[]{:S(2)}, u32[]{:S(2)}) collective-permute-start(bf16[64,2304]{1,0:T(8,128)(2,1)} %get-tuple-element.70.rest_2_), channel_id=1, source_target_pairs={{0,4},{1,5},{2,6},{3,7},{4,0},{5,1},{6,2},{7,3},{8,12},{9,13},{10,... | collective-permute-start | bytes 884744 | tf_op jit(solution)/shard_map/ppermute | solution.py:294
  252.3 14.5 %collective-permute-start.22 = (bf16[64,2304]{1,0:T(8,128)(2,1)}, bf16[64,2304]{1,0:T(8,128)(2,1)}, u32[]{:S(2)}, u32[]{:S(2)}) collective-permute-start(bf16[64,2304]{1,0:T(8,128)(2,1)} %get-tuple-element.49.rest_3_), channel_id=1, source_target_pairs={{0,2},{1,3},{2,0},{3,1},{4,6},{5,7},{6,4},{7,5},{8,10},{9,11},{10,... | collective-permute-start | bytes 884744 | tf_op jit(solution)/shard_map/ppermute | solution.py:294
  257.0 9.8 %collective-permute-start.24 = (bf16[64,2304]{1,0:T(8,128)(2,1)}, bf16[64,2304]{1,0:T(8,128)(2,1)}, u32[]{:S(2)}, u32[]{:S(2)}) collective-permute-start(bf16[64,2304]{1,0:T(8,128)(2,1)} %get-tuple-element.66), channel_id=1, source_target_pairs={{0,4},{1,5},{2,6},{3,7},{4,0},{5,1},{6,2},{7,3},{8,12},{9,13},{10,... | collective-permute-start | bytes 884744 | tf_op jit(solution)/shard_map/ppermute | solution.py:294
  257.0 11.6 %collective-permute-start.27 = (bf16[64,2304]{1,0:T(8,128)(2,1)}, bf16[64,2304]{1,0:T(8,128)(2,1)}, u32[]{:S(2)}, u32[]{:S(2)}) collective-permute-start(bf16[64,2304]{1,0:T(8,128)(2,1)} %get-tuple-element.62), channel_id=1, source_target_pairs={{0,4},{1,5},{2,6},{3,7},{4,0},{5,1},{6,2},{7,3},{8,12},{9,13},{10,... | collective-permute-start | bytes 884744 | tf_op jit(solution)/shard_map/ppermute | solution.py:294
  263.3 7.0 %collective-permute-start.29 = (bf16[64,2304]{1,0:T(8,128)(2,1)}, bf16[64,2304]{1,0:T(8,128)(2,1)}, u32[]{:S(2)}, u32[]{:S(2)}) collective-permute-start(bf16[64,2304]{1,0:T(8,128)(2,1)} %get-tuple-element.41), channel_id=1, source_target_pairs={{0,2},{1,3},{2,0},{3,1},{4,6},{5,7},{6,4},{7,5},{8,10},{9,11},{10,... | collective-permute-start | bytes 884744 | tf_op jit(solution)/shard_map/ppermute | solution.py:294
  399.9 7.2 %copy-start.30 = (bf16[8192,256]{1,0:T(8,128)(2,1)S(1)}, bf16[8192,256]{1,0:T(8,128)(2,1)}, u32[]{:S(2)}) copy-start(bf16[8192,256]{1,0:T(8,128)(2,1)} %get-tuple-element.29) | copy-start | bytes 12582916
  (23 other events, 25.9 us)
Sparse Core Ops, SparseCore 0:
  9.8 65.8 all-gather.2

commit v2 on v1

--- a/solution.py
+++ b/solution.py
@@ -31,14 +31,21 @@
     normalizer = jnp.asarray(math.sqrt(width), dtype=jnp.bfloat16)
 
     def start(tile, slot):
-        @pl.loop(0, TILE // 8)
+        count = counts[base + tile]
+
+        def copy(group, row):
+            src = pair_ids[(base + tile) * TILE + group * 8 + row]
+            pltpu.make_async_copy(table_ref.at[pl.ds(pl.multiple_of(src, 2), 2), :], pairs.at[slot, group, pl.ds(2 * row, 2), :], sems.at[slot]).start()
+
+        @pl.loop(0, count // 8)
         def _(group):
             for row in range(8):
-                src = pair_ids[(base + tile) * TILE + group * 8 + row]
-
-                @pl.when(src >= 0)
-                def _():
-                    pltpu.make_async_copy(table_ref.at[pl.ds(pl.multiple_of(src, 2), 2), :], pairs.at[slot, group, pl.ds(2 * row, 2), :], sems.at[slot]).start()
+                copy(group, row)
+
+        for row in range(7):
+            @pl.when(row < lax.rem(count, 8))
+            def _():
+                copy(count // 8, row)
 
     def wait(tile, slot):
         count = counts[base + tile]
@@ -98,60 +105,94 @@
     )(pair_ids, counts, cols, table_rows, *after)
 
 
-def finish_kernel(pieces, more, cols_ref, gain_ref, head_ref, extra_ref, *refs):
-    tail_refs, (resid_ref, normed_ref, tail) = refs[:pieces], refs[pieces:]
-    rows, width = resid_ref.shape
+def finish_kernel(pieces, more, cols_ref, gain_ref, head_hbm, extra_hbm, *refs):
+    piece_refs, (resid_hbm, normed_hbm, source, parts, extra, resid, normed, in_sems, out_sems) = refs[:pieces], refs[pieces:]
+    rows, width = resid.shape
     part = TAIL_ROWS // (pieces // 2)
-    extra_rows = extra_ref.shape[0]
+    known = HEAD_ROWS + TAIL_ROWS
     normalizer = jnp.asarray(math.sqrt(width), dtype=jnp.bfloat16)
+    one = jnp.ones((), jnp.bfloat16)
+    zero = jnp.zeros((), jnp.bfloat16)
+    head_copy = pltpu.make_async_copy(head_hbm, source.at[pl.ds(0, HEAD_ROWS), :], in_sems.at[pieces])
+    extra_copy = pltpu.make_async_copy(extra_hbm, extra, in_sems.at[pieces + 1])
+    copies = []
+    for index, ref in enumerate(piece_refs):
+        there = source.at[pl.ds(HEAD_ROWS + index // 2 * part, part), :] if index % 2 == 0 else parts.at[index // 2]
+        copies.append(pltpu.make_async_copy(ref, there, in_sems.at[index]))
+    for copy in copies:
+        copy.start()
+    head_copy.start()
+    extra_copy.start()
     for index in range(pieces // 2):
-        tail[pl.ds(index * part, part), :] = tail_refs[2 * index][...] + tail_refs[2 * index + 1][...]
-
-    def one_hot(span, first, count, value):
-        lanes = lax.broadcasted_iota(jnp.int32, (256, count), 1) + first
-        return jnp.where(lanes == cols_ref[span, :], value, jnp.zeros((), jnp.bfloat16))
+        copies[2 * index].wait()
+        copies[2 * index + 1].wait()
+        span = pl.ds(HEAD_ROWS + index * part, part)
+        source[span, :] = source[span, :] + parts[index]
+    head_copy.wait()
+    extra_copy.wait()
+
+    def results(block):
+        span = pl.ds(pl.multiple_of(block * 256, 256), 256)
+        return (pltpu.make_async_copy(resid.at[span, :], resid_hbm.at[span, :], out_sems.at[0]),
+                pltpu.make_async_copy(normed.at[span, :], normed_hbm.at[span, :], out_sems.at[1]))
 
     @pl.loop(0, rows // 256)
     def _(block):
         span = pl.ds(pl.multiple_of(block * 256, 256), 256)
-        from_head = one_hot(span, 0, HEAD_ROWS, normalizer)
-        from_tail = one_hot(span, HEAD_ROWS, TAIL_ROWS, jnp.ones((), jnp.bfloat16))
+        lanes = lax.broadcasted_iota(jnp.int32, (256, known), 1)
+        value = jnp.where(lax.broadcasted_iota(jnp.int32, (1, known), 1) < HEAD_ROWS, normalizer, one)
+        select = jnp.where(lanes == cols_ref[span, :], jnp.broadcast_to(value, (256, known)), zero)
         for piece in range(width // 256):
             cols = pl.ds(piece * 256, 256)
-            picked = jnp.dot(from_head, head_ref[:, cols], preferred_element_type=jnp.float32)
-            picked += jnp.dot(from_tail, tail[:, cols], preferred_element_type=jnp.float32)
-            resid_ref[span, cols] = picked.astype(jnp.bfloat16)
+            resid[span, cols] = jnp.dot(select, source[:, cols], preferred_element_type=jnp.float32).astype(jnp.bfloat16)
 
         @pl.when(more[0] > 0)
         def _():
-            from_extra = one_hot(span, HEAD_ROWS + TAIL_ROWS, extra_rows, jnp.ones((), jnp.bfloat16))
+            places = lax.broadcasted_iota(jnp.int32, (256, extra.shape[0]), 1) + known
+            from_extra = jnp.where(places == cols_ref[span, :], one, zero)
             for piece in range(width // 256):
                 cols = pl.ds(piece * 256, 256)
-                picked = jnp.dot(from_extra, extra_ref[:, cols], preferred_element_type=jnp.float32)
-                resid_ref[span, cols] = (resid_ref[span, cols].astype(jnp.float32) + picked).astype(jnp.bfloat16)
+                picked = jnp.dot(from_extra, extra[:, cols], preferred_element_type=jnp.float32)
+                resid[span, cols] = (resid[span, cols].astype(jnp.float32) + picked).astype(jnp.bfloat16)
 
         for quarter in range(4):
             rows_here = pl.ds(pl.multiple_of(block * 256 + quarter * 64, 64), 64)
-            widened = resid_ref[rows_here, :].astype(jnp.float32)
+            widened = resid[rows_here, :].astype(jnp.float32)
             inv_rms = lax.rsqrt(jnp.mean(widened * widened, axis=-1, keepdims=True) + EPSILON)
-            normed_ref[rows_here, :] = (widened * inv_rms * gain_ref[...]).astype(jnp.bfloat16)
-
-
-def finish_rows(more, cols, gain, head, extra, tail_pieces):
+            normed[rows_here, :] = (widened * inv_rms * gain_ref[...]).astype(jnp.bfloat16)
+        for result in results(block):
+            result.start()
+
+    @pl.loop(0, rows // 256)
+    def _(block):
+        for result in results(block):
+            result.wait()
+
+
+def finish_rows(more, cols, gain, head, extra, pieces):
     rows = cols.shape[0]
     width = head.shape[1]
     vmem = pl.BlockSpec(memory_space=pltpu.VMEM)
+    hbm = pl.BlockSpec(memory_space=pltpu.HBM)
     shape = jax.ShapeDtypeStruct((rows, width), jnp.bfloat16)
+    dma = pltpu.SemaphoreType.DMA
     return pl.pallas_call(
-        functools.partial(finish_kernel, len(tail_pieces)),
+        functools.partial(finish_kernel, len(pieces)),
         out_shape=(shape, shape),
-        in_specs=[pl.BlockSpec(memory_space=pltpu.SMEM)] + [vmem] * (4 + len(tail_pieces)),
-        out_specs=(vmem, vmem),
-        scratch_shapes=[pltpu.VMEM((TAIL_ROWS, width), jnp.bfloat16)],
+        in_specs=[pl.BlockSpec(memory_space=pltpu.SMEM), vmem, vmem, hbm, hbm] + [hbm] * len(pieces),
+        out_specs=(hbm, hbm),
+        scratch_shapes=[
+            pltpu.VMEM((HEAD_ROWS + TAIL_ROWS, width), jnp.bfloat16),
+            pltpu.VMEM((len(pieces) // 2,) + pieces[0].shape, jnp.bfloat16),
+            pltpu.VMEM(extra.shape, jnp.bfloat16),
+            pltpu.VMEM((rows, width), jnp.bfloat16),
+            pltpu.VMEM((rows, width), jnp.bfloat16),
+            dma((len(pieces) + 2,)), dma((2,)),
+        ],
         compiler_params=pltpu.CompilerParams(vmem_limit_bytes=40 * 1024 * 1024),
         cost_estimate=pl.CostEstimate(flops=2 * rows * width * (HEAD_ROWS + TAIL_ROWS), bytes_accessed=16_000_000, transcendentals=0),
         name="finish_rows",
-    )(more, cols, gain, head, extra, *tail_pieces)
+    )(more, cols, gain, head, extra, *pieces)
 
 
 def heads_kernel(rows, normed, cos_ref, sin_ref, wq_hbm, wk_hbm, wv_hbm, q_out, kv_out,
@@ -347,9 +388,12 @@
         call_rows = 4 * chunk_rows
         ids = arrange(ranked_ids(0, TAIL_ROWS)).reshape(-1, TILE)
         owned = ids >= 0
-        pair_ids = jnp.where(owned, (ids // 2) * 2, -1).reshape(-1)
-        lane = jnp.arange(TILE, dtype=jnp.int32) * 2
-        cols = jnp.where(owned, lane + ids % 2, -1).astype(jnp.float32)[:, None, :]
+        before = (lax.broadcasted_iota(jnp.int32, (TILE, TILE), 0) < lax.broadcasted_iota(jnp.int32, (TILE, TILE), 1)).astype(jnp.bfloat16)
+        slots = jnp.dot(owned.astype(jnp.bfloat16), before, preferred_element_type=jnp.float32).astype(jnp.int32)
+        slots = jnp.where(owned, slots, -1)
+        wanted_slot = lax.broadcasted_iota(jnp.int32, (ids.shape[0], TILE, TILE), 2)
+        pair_ids = jnp.sum(jnp.where(slots[:, :, None] == wanted_slot, (ids // 2)[:, :, None] * 2, 0), axis=1).reshape(-1)
+        cols = jnp.where(owned, 2 * slots + ids % 2, -1).astype(jnp.float32)[:, None, :]
         counts = jnp.sum(owned.astype(jnp.int32), axis=-1)
 
         def gather(chunk, side, after):

time: 423 us -> 414 us (0.979)
  Pallas kernels: 191 us -> 179 us
    pallas_call x10, Pallas kernels: 77.7 us -> 66.5 us  [gather_rows(): pl.pallas_call(functools.partial(gather_kernel, base, tiles, width), grid...]
  transfers between devices with their start and end apart: 31 -> 31, of which waited for: 11 -> 11; matrix products, arithmetic and copies ran while one was open for 13% -> 14% of each run, Pallas kernels for 19% -> 16%
where the time goes in v2:
time: 414 us; the launch traced here: 406 us
  Pallas kernels  179 us (43%)
  waiting for transfers between devices  89.2 us (22%)
  other arithmetic  46.9 us (11%)
  local copies, waits for them, and re-layouts  36 us (9%)
  starting transfers between devices  32.9 us (8%)
  between operations  15.9 us (4%)
  blocking collectives  4.76 us (1%)
    pallas_call x1, Pallas kernels, project_heads(): pl.pallas_call(functools.partial(heads_kernel, rows), out_shape=(jax.Shap...  98.3 us
    ppermute x25, waiting for transfers between devices, exchange(): return lax.ppermute(rows, 'tp', [(i, i ^ bit) for i in range(group_size)])  88.5 us
    pallas_call x10, Pallas kernels, gather_rows(): pl.pallas_call(functools.partial(gather_kernel, base, tiles, width), grid...  66.5 us
    unnamed x81, local copies, waits for them, and re-layouts  22.3 us
    ppermute x25, starting transfers between devices, exchange(): return lax.ppermute(rows, 'tp', [(i, i ^ bit) for i in range(group_size)])  17.8 us
    pallas_call x1, Pallas kernels, finish_rows(): pl.pallas_call(functools.partial(finish_kernel, len(pieces)), out_shape=(...  14.2 us
    add x5, other arithmetic, local_body(): sent = mine[far] + got[far]  12.3 us
  transfers between devices with their start and end apart: 31, of which 11 were waited for; matrix products, arithmetic and copies ran while one was open for 14% of the time, Pallas kernels for 16%

profile of v2, /device:TPU:0, one launch (start us, length us, event | category | flops | bytes accessed | tf_op | source)
XLA Modules:
  0.0 405.8 jit_solution(4599612405020085854)
XLA Ops:
  9.2 3.0 select_reduce_fusion.1
  14.7 2.6 select_reduce_fusion.2
  17.3 6.8 %gather_rows.10.rest_0_ = bf16[512,2304]{1,0:T(8,128)(2,1)} custom-call(s32[5120]{0:T(1024)} %bitcast.35, s32[40]{0:T(128)} %reduce_sum.51.counts, f32[40,1,128]{2,1,0:T(1,128)} %bitcast.45, bf16[32000,2304]{1,0:T(8,128)(2,1)} %table_ref.19), custom_call_target="tpu_custom_call" | custom-call | flops 10240000000 | bytes 7077888 | tf_op jit(solution)/shard_map/gather_rows/pallas_call | solution.py:98
  24.2 6.8 %gather_rows.11 = bf16[512,2304]{1,0:T(8,128)(2,1)} custom-call(s32[5120]{0:T(1024)} %bitcast.36, s32[40]{0:T(128)} %reduce_sum.51.counts, f32[40,1,128]{2,1,0:T(1,128)} %bitcast.46, bf16[32000,2304]{1,0:T(8,128)(2,1)} %table_ref.19, bf16[512,2304]{1,0:T(8,128)(2,1)} %gather_rows.10.rest_0_), custom_call_target="tpu_custom_call" | custom-call | flops 10240000000 | bytes 7077888 | tf_op jit(solution)/shard_map/gather_rows/pallas_call | solution.py:98
  31.1 3.2 slice_add_fusion.8
  34.3 6.7 %gather_rows.12.rest_0_ = bf16[512,2304]{1,0:T(8,128)(2,1)} custom-call(s32[5120]{0:T(1024)} %bitcast.37, s32[40]{0:T(128)} %reduce_sum.51.counts, f32[40,1,128]{2,1,0:T(1,128)} %bitcast.47, bf16[32000,2304]{1,0:T(8,128)(2,1)} %table_ref.19, bf16[128,2304]{1,0:T(8,128)(2,1)} %get-tuple-element.80.rest_0_, bf16[128,2304]{1,0:T(8,128)(2,1)} %get-tuple-element.79.rest_1_), custom_call_target="tpu_custom_call" | custom-call | flops 10240000000 | bytes 7077888 | tf_op jit(solution)/shard_map/gather_rows/pallas_call | solution.py:98
  41.1 3.6 fusion.15
  44.7 3.5 collective-permute-start.2
  48.2 2.5 collective-permute-start.4
  52.4 6.8 %gather_rows.13 = bf16[512,2304]{1,0:T(8,128)(2,1)} custom-call(s32[5120]{0:T(1024)} %bitcast.38, s32[40]{0:T(128)} %reduce_sum.51.counts, f32[40,1,128]{2,1,0:T(1,128)} %bitcast.48, bf16[32000,2304]{1,0:T(8,128)(2,1)} %table_ref.19, bf16[512,2304]{1,0:T(8,128)(2,1)} %gather_rows.12.rest_0_), custom_call_target="tpu_custom_call" | custom-call | flops 10240000000 | bytes 7077888 | tf_op jit(solution)/shard_map/gather_rows/pallas_call | solution.py:98
  59.3 39.2 %collective-permute-done.7 = bf16[128,2304]{1,0:T(8,128)(2,1)} collective-permute-done((bf16[128,2304]{1,0:T(8,128)(2,1)}, bf16[128,2304]{1,0:T(8,128)(2,1)}, u32[]{:S(2)}, u32[]{:S(2)}) %collective-permute-start.7) | collective-permute-done | bytes 589856 | tf_op jit(solution)/shard_map/ppermute | solution.py:335
  98.5 2.7 slice_add_fusion.36
  101.2 2.2 slice_add_fusion.6
  103.4 2.5 collective-permute-start.10
  105.9 6.9 %gather_rows.14.rest_0_ = bf16[512,2304]{1,0:T(8,128)(2,1)} custom-call(s32[5120]{0:T(1024)} %bitcast.39, s32[40]{0:T(128)} %reduce_sum.51.counts, f32[40,1,128]{2,1,0:T(1,128)} %bitcast.49, bf16[32000,2304]{1,0:T(8,128)(2,1)} %table_ref.19, bf16[128,2304]{1,0:T(8,128)(2,1)} %get-tuple-element.78.rest_0_, bf16[128,2304]{1,0:T(8,128)(2,1)} %copy-done.32, ...), custom_call_target="tpu_custom_call" | custom-call | flops 10240000000 | bytes 7077888 | tf_op jit(solution)/shard_map/gather_rows/pallas_call | solution.py:98
  113.6 3.1 multiply_sine_fusion
  116.7 2.8 slice_add_fusion.32
  119.4 6.8 %gather_rows.15 = bf16[512,2304]{1,0:T(8,128)(2,1)} custom-call(s32[5120]{0:T(1024)} %bitcast.40, s32[40]{0:T(128)} %reduce_sum.51.counts, f32[40,1,128]{2,1,0:T(1,128)} %bitcast.50, bf16[32000,2304]{1,0:T(8,128)(2,1)} %table_ref.19, bf16[512,2304]{1,0:T(8,128)(2,1)} %gather_rows.14.rest_0_), custom_call_target="tpu_custom_call" | custom-call | flops 10240000000 | bytes 7077888 | tf_op jit(solution)/shard_map/gather_rows/pallas_call | solution.py:98
  126.2 2.7 slice_add_fusion.4
  128.9 6.8 %gather_rows.16.rest_0_ = bf16[512,2304]{1,0:T(8,128)(2,1)} custom-call(s32[5120]{0:T(1024)} %bitcast.41, s32[40]{0:T(128)} %reduce_sum.51.counts, f32[40,1,128]{2,1,0:T(1,128)} %bitcast.51, bf16[32000,2304]{1,0:T(8,128)(2,1)} %table_ref.19, bf16[128,2304]{1,0:T(8,128)(2,1)} %get-tuple-element.76.rest_0_, bf16[128,2304]{1,0:T(8,128)(2,1)} %get-tuple-element.75.rest_1_, ...), custom_call_target="tpu_custom_call" | custom-call | flops 10240000000 | bytes 7077888 | tf_op jit(solution)/shard_map/gather_rows/pallas_call | solution.py:98
  135.9 3.8 broadcast_select_fusion.3
  139.6 2.7 collective-permute-start.5
  142.4 2.4 collective-permute-start.3
  144.8 6.7 %gather_rows.17 = bf16[512,2304]{1,0:T(8,128)(2,1)} custom-call(s32[5120]{0:T(1024)} %bitcast.42, s32[40]{0:T(128)} %reduce_sum.51.counts, f32[40,1,128]{2,1,0:T(1,128)} %bitcast.52, bf16[32000,2304]{1,0:T(8,128)(2,1)} %table_ref.19, bf16[512,2304]{1,0:T(8,128)(2,1)} %gather_rows.16.rest_0_), custom_call_target="tpu_custom_call" | custom-call | flops 10240000000 | bytes 7077888 | tf_op jit(solution)/shard_map/gather_rows/pallas_call | solution.py:98
  151.5 22.6 %collective-permute-done.19 = bf16[128,2304]{1,0:T(8,128)(2,1)} collective-permute-done((bf16[128,2304]{1,0:T(8,128)(2,1)S(1)}, bf16[128,2304]{1,0:T(8,128)(2,1)}, u32[]{:S(2)}, u32[]{:S(2)}) %collective-permute-start.19) | collective-permute-done | bytes 589856 | tf_op jit(solution)/shard_map/ppermute | solution.py:335
  174.1 1.9 collective-permute-done.21
  176.6 3.0 slice_add_fusion.24
  179.7 2.5 slice_add_fusion.2
  182.1 6.0 %gather_rows.18.rest_0_ = bf16[512,2304]{1,0:T(8,128)(2,1)} custom-call(s32[5120]{0:T(1024)} %bitcast.43, s32[40]{0:T(128)} %reduce_sum.51.counts, f32[40,1,128]{2,1,0:T(1,128)} %bitcast.53, bf16[32000,2304]{1,0:T(8,128)(2,1)} %table_ref.19, bf16[128,2304]{1,0:T(8,128)(2,1)} %get-tuple-element.67.rest_0_, bf16[128,2304]{1,0:T(8,128)(2,1)} %get-tuple-element.68.rest_1_, ...), custom_call_target="tpu_custom_call" | custom-call | flops 10240000000 | bytes 7077888 | tf_op jit(solution)/shard_map/gather_rows/pallas_call | solution.py:98
  189.8 2.1 broadcast_select_fusion.4
  191.8 2.0 pad_maximum_fusion
  193.9 3.9 collective-permute-start.6
  197.8 4.8 %pmax.7 = s32[]{:T(128)} all-reduce(s32[]{:T(128)S(6)} %convert_element_type.30), channel_id=1, replica_groups=mesh['dp'=2,'tp'=8] {'dp'}, use_global_device_ids=true, to_apply=%region_5.6 | all-reduce | flops 1 | bytes 8 | tf_op jit(solution)/shard_map/pmax | solution.py:434
  204.3 6.1 %gather_rows.19 = bf16[512,2304]{1,0:T(8,128)(2,1)} custom-call(s32[5120]{0:T(1024)} %bitcast.44, s32[40]{0:T(128)} %reduce_sum.51.counts, f32[40,1,128]{2,1,0:T(1,128)} %bitcast.54, bf16[32000,2304]{1,0:T(8,128)(2,1)} %table_ref.19, bf16[512,2304]{1,0:T(8,128)(2,1)} %gather_rows.18.rest_0_), custom_call_target="tpu_custom_call" | custom-call | flops 10240000000 | bytes 7077888 | tf_op jit(solution)/shard_map/gather_rows/pallas_call | solution.py:98
  214.9 1.8 collective-permute-start.26
  216.6 10.2 %collective-permute-done.23 = bf16[128,2304]{1,0:T(8,128)(2,1)S(1)} collective-permute-done((bf16[128,2304]{1,0:T(8,128)(2,1)}, bf16[128,2304]{1,0:T(8,128)(2,1)S(1)}, u32[]{:S(2)}, u32[]{:S(2)}) %collective-permute-start.23) | collective-permute-done | bytes 589856 | tf_op jit(solution)/shard_map/ppermute | solution.py:335
  226.9 2.6 slice_add_fusion.18
  229.5 1.9 collective-permute-start.17
  231.4 5.2 %collective-permute-done.26 = bf16[128,2304]{1,0:T(8,128)(2,1)S(1)} collective-permute-done((bf16[128,2304]{1,0:T(8,128)(2,1)S(1)}, bf16[128,2304]{1,0:T(8,128)(2,1)S(1)}, u32[]{:S(2)}, u32[]{:S(2)}) %collective-permute-start.26) | collective-permute-done | bytes 589856 | tf_op jit(solution)/shard_map/ppermute | solution.py:335
  238.7 2.6 slice_add_fusion.10
  244.3 2.2 collective-permute-done.18.refs_7_
  247.2 2.0 collective-permute-start.27
  249.2 3.6 collective-permute-done.14.refs_15_
  275.0 14.2 %finish_rows.1 = (bf16[1024,2304]{1,0:T(8,128)(2,1)}, bf16[1024,2304]{1,0:T(8,128)(2,1)S(1)}) custom-call(s32[1]{0:T(128)} %bitcast.8.more, s32[1024,1]{1,0:T(8,128)S(1)} %copy.35.cols_ref, f32[1,2304]{1,0:T(1,128)S(1)} %broadcast_in_dim.89.gain_ref, bf16[640,2304]{1,0:T(8,128)(2,1)S(1)} %broadcast_select_fusion.head_hbm, ...), custom_call_target="tpu_custom_call" | custom-call | flops 6039797760 | bytes 16000000 | tf_op jit(solution)/shard_map/finish_rows/pallas_call | solution.py:179
  289.2 2.2 copy-done.20
  291.4 98.3 %project_heads.1 = (bf16[8192,256]{1,0:T(8,128)(2,1)}, bf16[2,8192,256]{2,1,0:T(8,128)(2,1)}) custom-call(bf16[1024,2304]{1,0:T(8,128)(2,1)} %copy-done.20, f32[1024,128]{1,0:T(8,128)} %get-tuple-element.87.cos_ref, f32[1024,128]{1,0:T(8,128)} %get-tuple-element.86.sin_ref, bf16[8,2304,256]{2,1,0:T(8,128)(2,1)} %bitcast.33, bf16[2304,1024]{1,0:T(8,128)(2,1)} %wk_hbm.1, ...), custom_call_target="tpu_custom_call" | custom-call | flops 19327352832 | bytes 40000000 | tf_op jit(solution)/shard_map/project_heads/pallas_call | solution.py:307
  389.8 6.6 %slice_bitcast_fusion = (bf16[8192,1,256]{2,0,1:T(8,128)(2,1)}, bf16[8192,1,256]{2,0,1:T(8,128)(2,1)}) fusion(bf16[2,8192,256]{2,1,0:T(8,128)(2,1)} %get-tuple-element.30), kind=kLoop, calls=%fused_computation.13 | loop fusion | bytes 16777216 | tf_op jit(solution)/shard_map/broadcast_in_dim;squeeze | solution.py:443
  397.0 2.0 copy.44
  (158 shorter events, 44.2 us)
Async XLA Ops:
  7.2 98.7 %all-gather.3.cloned.1.call-start = ((), (), s32[]{:S(2)}) async-start(), calls=%async_computation.2 | async-start | bytes 10616832 | tf_op jit(solution)/shard_map/all_gather | solution.py:355
  9.2 42.9 %copy-start.37 = (s32[8,1024]{1,0:T(8,128)}, s32[8,1024]{1,0:T(8,128)S(1)}, u32[]{:S(2)}) copy-start(s32[8,1024]{1,0:T(8,128)S(1)} %fusion.3) | copy-start | bytes 98308
  24.2 6.9 %collective-permute-start = (bf16[512,2304]{1,0:T(8,128)(2,1)}, bf16[512,2304]{1,0:T(8,128)(2,1)S(1)}, u32[]{:S(2)}, u32[]{:S(2)}) collective-permute-start(bf16[512,2304]{1,0:T(8,128)(2,1)} %gather_rows.10.rest_0_), channel_id=1, source_target_pairs={{0,1},{1,0},{2,3},{3,2},{4,5},{5,4},{6,7},{7,6},{8,9},{9,8},{10,11... | collective-permute-start | bytes 7077896 | tf_op jit(solution)/shard_map/ppermute | solution.py:335
  31.0 10.0 %copy-start.34 = (bf16[512,2304]{1,0:T(8,128)(2,1)}, bf16[512,2304]{1,0:T(8,128)(2,1)S(1)}, u32[]{:S(2)}) copy-start(bf16[512,2304]{1,0:T(8,128)(2,1)S(1)} %collective-permute-done) | copy-start | bytes 7077892
  41.0 11.3 %copy-start.31 = (bf16[128,2304]{1,0:T(8,128)(2,1)S(1)}, bf16[128,2304]{1,0:T(8,128)(2,1)}, u32[]{:S(2)}) copy-start(bf16[128,2304]{1,0:T(8,128)(2,1)} %get-tuple-element.79.rest_1_) | copy-start | bytes 1769476
  41.0 60.1 %collective-permute-start.1 = (bf16[512,2304]{1,0:T(8,128)(2,1)}, bf16[512,2304]{1,0:T(8,128)(2,1)}, u32[]{:S(2)}, u32[]{:S(2)}) collective-permute-start(bf16[512,2304]{1,0:T(8,128)(2,1)} %gather_rows.12.rest_0_), channel_id=1, source_target_pairs={{0,1},{1,0},{2,3},{3,2},{4,5},{5,4},{6,7},{7,6},{8,9},{9,8},{10,11... | collective-permute-start | bytes 7077896 | tf_op jit(solution)/shard_map/ppermute | solution.py:335
  44.7 91.1 %collective-permute-start.2 = (bf16[320,2304]{1,0:T(8,128)(2,1)}, bf16[320,2304]{1,0:T(8,128)(2,1)}, u32[]{:S(2)}, u32[]{:S(2)}) collective-permute-start(bf16[320,2304]{1,0:T(8,128)(2,1)} %get-tuple-element.37), channel_id=1, source_target_pairs={{0,2},{8,10}} | collective-permute-start | bytes 4423688 | tf_op jit(solution)/shard_map/ppermute | solution.py:340
  48.2 87.6 %collective-permute-start.4 = (bf16[320,2304]{1,0:T(8,128)(2,1)}, bf16[320,2304]{1,0:T(8,128)(2,1)}, u32[]{:S(2)}, u32[]{:S(2)}) collective-permute-start(bf16[320,2304]{1,0:T(8,128)(2,1)} %get-tuple-element.38), channel_id=1, source_target_pairs={{0,4},{8,12}} | collective-permute-start | bytes 4423688 | tf_op jit(solution)/shard_map/ppermute | solution.py:341
  52.3 46.1 %copy-start.26 = (bf16[512,2304]{1,0:T(8,128)(2,1)S(1)}, bf16[512,2304]{1,0:T(8,128)(2,1)}, u32[]{:S(2)}) copy-start(bf16[512,2304]{1,0:T(8,128)(2,1)} %gather_rows.11) | copy-start | bytes 7077892
  52.3 46.1 %collective-permute-start.7 = (bf16[128,2304]{1,0:T(8,128)(2,1)}, bf16[128,2304]{1,0:T(8,128)(2,1)}, u32[]{:S(2)}, u32[]{:S(2)}) collective-permute-start(bf16[128,2304]{1,0:T(8,128)(2,1)} %get-tuple-element.80.rest_0_), channel_id=1, source_target_pairs={{0,2},{1,3},{2,0},{3,1},{4,6},{5,7},{6,4},{7,5},{8,10},{9,11},{10,... | collective-permute-start | bytes 1769480 | tf_op jit(solution)/shard_map/ppermute | solution.py:335
  52.4 46.1 %collective-permute-start.8 = (bf16[128,2304]{1,0:T(8,128)(2,1)S(1)}, bf16[128,2304]{1,0:T(8,128)(2,1)}, u32[]{:S(2)}, u32[]{:S(2)}) collective-permute-start(bf16[128,2304]{1,0:T(8,128)(2,1)S(1)} %copy-done.31), channel_id=1, source_target_pairs={{0,4},{1,5},{2,6},{3,7},{4,0},{5,1},{6,2},{7,3},{8,12},{9,13},{10,... | collective-permute-start | bytes 1769480 | tf_op jit(solution)/shard_map/ppermute | solution.py:335
  59.3 41.9 %copy-start.27 = (bf16[512,2304]{1,0:T(8,128)(2,1)S(1)}, bf16[512,2304]{1,0:T(8,128)(2,1)}, u32[]{:S(2)}) copy-start(bf16[512,2304]{1,0:T(8,128)(2,1)} %gather_rows.13) | copy-start | bytes 7077892
  103.4 13.3 %collective-permute-start.10 = (bf16[128,2304]{1,0:T(8,128)(2,1)}, bf16[128,2304]{1,0:T(8,128)(2,1)}, u32[]{:S(2)}, u32[]{:S(2)}) collective-permute-start(bf16[128,2304]{1,0:T(8,128)(2,1)} %get-tuple-element.78.rest_0_), channel_id=1, source_target_pairs={{0,2},{1,3},{2,0},{3,1},{4,6},{5,7},{6,4},{7,5},{8,10},{9,11},{10,... | collective-permute-start | bytes 1769480 | tf_op jit(solution)/shard_map/ppermute | solution.py:335
  105.8 10.8 %collective-permute-start.11 = (bf16[128,2304]{1,0:T(8,128)(2,1)S(1)}, bf16[128,2304]{1,0:T(8,128)(2,1)}, u32[]{:S(2)}, u32[]{:S(2)}) collective-permute-start(bf16[128,2304]{1,0:T(8,128)(2,1)S(1)} %get-tuple-element.77.rest_1_), channel_id=1, source_target_pairs={{0,4},{1,5},{2,6},{3,7},{4,0},{5,1},{6,2},{7,3},{8,12},{9,13},{10,... | collective-permute-start | bytes 1769480 | tf_op jit(solution)/shard_map/ppermute | solution.py:335
  105.9 7.0 %copy-start.39 = (f32[2304]{0:T(1024)S(1)}, f32[2304]{0:T(1024)}, u32[]{:S(2)}) copy-start(f32[2304]{0:T(1024)} %param.12) | copy-start | bytes 27652
  105.9 10.8 %copy-start.28 = (bf16[512,2304]{1,0:T(8,128)(2,1)S(1)}, bf16[512,2304]{1,0:T(8,128)(2,1)}, u32[]{:S(2)}) copy-start(bf16[512,2304]{1,0:T(8,128)(2,1)} %gather_rows.13) | copy-start | bytes 7077892
  112.8 13.4 %collective-permute-start.9 = (bf16[512,2304]{1,0:T(8,128)(2,1)}, bf16[512,2304]{1,0:T(8,128)(2,1)}, u32[]{:S(2)}, u32[]{:S(2)}) collective-permute-start(bf16[512,2304]{1,0:T(8,128)(2,1)} %gather_rows.14.rest_0_), channel_id=1, source_target_pairs={{0,1},{1,0},{2,3},{3,2},{4,5},{5,4},{6,7},{7,6},{8,9},{9,8},{10,11... | collective-permute-start | bytes 7077896 | tf_op jit(solution)/shard_map/ppermute | solution.py:335
  135.8 9.0 %copy-start.33 = (bf16[128,2304]{1,0:T(8,128)(2,1)S(1)}, bf16[128,2304]{1,0:T(8,128)(2,1)}, u32[]{:S(2)}) copy-start(bf16[128,2304]{1,0:T(8,128)(2,1)} %get-tuple-element.76.rest_0_) | copy-start | bytes 1769476
  135.8 43.9 %collective-permute-start.12 = (bf16[512,2304]{1,0:T(8,128)(2,1)}, bf16[512,2304]{1,0:T(8,128)(2,1)}, u32[]{:S(2)}, u32[]{:S(2)}) collective-permute-start(bf16[512,2304]{1,0:T(8,128)(2,1)} %gather_rows.16.rest_0_), channel_id=1, source_target_pairs={{0,1},{1,0},{2,3},{3,2},{4,5},{5,4},{6,7},{7,6},{8,9},{9,8},{10,11... | collective-permute-start | bytes 7077896 | tf_op jit(solution)/shard_map/ppermute | solution.py:335
  139.6 48.5 %collective-permute-start.5 = (bf16[320,2304]{1,0:T(8,128)(2,1)}, bf16[320,2304]{1,0:T(8,128)(2,1)}, u32[]{:S(2)}, u32[]{:S(2)}) collective-permute-start(bf16[320,2304]{1,0:T(8,128)(2,1)} %get-tuple-element.36), channel_id=1, source_target_pairs={{0,2},{4,6},{8,10},{12,14}} | collective-permute-start | bytes 4423688 | tf_op jit(solution)/shard_map/ppermute | solution.py:345
  142.4 47.4 %collective-permute-start.3 = (bf16[320,2304]{1,0:T(8,128)(2,1)}, bf16[320,2304]{1,0:T(8,128)(2,1)}, u32[]{:S(2)}, u32[]{:S(2)}) collective-permute-start(bf16[320,2304]{1,0:T(8,128)(2,1)} %get-tuple-element.35), channel_id=1, source_target_pairs={{0,4},{2,6},{8,12},{10,14}} | collective-permute-start | bytes 4423688 | tf_op jit(solution)/shard_map/ppermute | solution.py:344
  144.8 29.3 %collective-permute-start.19 = (bf16[128,2304]{1,0:T(8,128)(2,1)S(1)}, bf16[128,2304]{1,0:T(8,128)(2,1)}, u32[]{:S(2)}, u32[]{:S(2)}) collective-permute-start(bf16[128,2304]{1,0:T(8,128)(2,1)S(1)} %copy-done.33), channel_id=1, source_target_pairs={{0,2},{1,3},{2,0},{3,1},{4,6},{5,7},{6,4},{7,5},{8,10},{9,11},{10,... | collective-permute-start | bytes 1769480 | tf_op jit(solution)/shard_map/ppermute | solution.py:335
  144.8 31.2 %collective-permute-start.21 = (bf16[128,2304]{1,0:T(8,128)(2,1)}, bf16[128,2304]{1,0:T(8,128)(2,1)}, u32[]{:S(2)}, u32[]{:S(2)}) collective-permute-start(bf16[128,2304]{1,0:T(8,128)(2,1)} %get-tuple-element.75.rest_1_), channel_id=1, source_target_pairs={{0,4},{1,5},{2,6},{3,7},{4,0},{5,1},{6,2},{7,3},{8,12},{9,13},{10,... | collective-permute-start | bytes 1769480 | tf_op jit(solution)/shard_map/ppermute | solution.py:335
  151.5 28.2 %copy-start.25 = (bf16[512,2304]{1,0:T(8,128)(2,1)S(1)}, bf16[512,2304]{1,0:T(8,128)(2,1)}, u32[]{:S(2)}) copy-start(bf16[512,2304]{1,0:T(8,128)(2,1)} %gather_rows.17) | copy-start | bytes 7077892
  174.1 55.5 %collective-permute-start.15 = (bf16[64,2304]{1,0:T(8,128)(2,1)}, bf16[64,2304]{1,0:T(8,128)(2,1)S(1)}, u32[]{:S(2)}, u32[]{:S(2)}) collective-permute-start(bf16[64,2304]{1,0:T(8,128)(2,1)} %get-tuple-element.73.rest_2_), channel_id=1, source_target_pairs={{0,4},{1,5},{2,6},{3,7},{4,0},{5,1},{6,2},{7,3},{8,12},{9,13},{10,... | collective-permute-start | bytes 884744 | tf_op jit(solution)/shard_map/ppermute | solution.py:335
  176.0 65.2 %collective-permute-start.16 = (bf16[64,2304]{1,0:T(8,128)(2,1)}, bf16[64,2304]{1,0:T(8,128)(2,1)S(1)}, u32[]{:S(2)}, u32[]{:S(2)}) collective-permute-start(bf16[64,2304]{1,0:T(8,128)(2,1)} %get-tuple-element.58.rest_3_), channel_id=1, source_target_pairs={{0,2},{1,3},{2,0},{3,1},{4,6},{5,7},{6,4},{7,5},{8,10},{9,11},{10,... | collective-permute-start | bytes 884744 | tf_op jit(solution)/shard_map/ppermute | solution.py:335
  188.1 22.3 %collective-permute-start.25 = (bf16[512,2304]{1,0:T(8,128)(2,1)}, bf16[512,2304]{1,0:T(8,128)(2,1)}, u32[]{:S(2)}, u32[]{:S(2)}) collective-permute-start(bf16[512,2304]{1,0:T(8,128)(2,1)} %gather_rows.18.rest_0_), channel_id=1, source_target_pairs={{0,1},{1,0},{2,3},{3,2},{4,5},{5,4},{6,7},{7,6},{8,9},{9,8},{10,11... | collective-permute-start | bytes 7077896 | tf_op jit(solution)/shard_map/ppermute | solution.py:335
  189.7 4.1 %copy-start.21 = (bf16[320,2304]{1,0:T(8,128)(2,1)}, bf16[320,2304]{1,0:T(8,128)(2,1)S(1)}, u32[]{:S(2)}) copy-start(bf16[320,2304]{1,0:T(8,128)(2,1)S(1)} %broadcast_select_fusion.2) | copy-start | bytes 4423684
  193.9 53.3 %collective-permute-start.6 = (bf16[640,2304]{1,0:T(8,128)(2,1)}, bf16[640,2304]{1,0:T(8,128)(2,1)}, u32[]{:S(2)}, u32[]{:S(2)}) collective-permute-start(bf16[640,2304]{1,0:T(8,128)(2,1)} %pad_maximum_fusion), channel_id=1, source_target_pairs={{0,1},{2,3},{4,5},{6,7},{8,9},{10,11},{12,13},{14,15}} | collective-permute-start | bytes 8847368 | tf_op jit(solution)/shard_map/ppermute | solution.py:349
  202.6 12.3 %collective-permute-start.13 = (bf16[128,2304]{1,0:T(8,128)(2,1)}, bf16[128,2304]{1,0:T(8,128)(2,1)}, u32[]{:S(2)}, u32[]{:S(2)}) collective-permute-start(bf16[128,2304]{1,0:T(8,128)(2,1)} %get-tuple-element.68.rest_1_), channel_id=1, source_target_pairs={{0,4},{1,5},{2,6},{3,7},{4,0},{5,1},{6,2},{7,3},{8,12},{9,13},{10,... | collective-permute-start | bytes 1769480 | tf_op jit(solution)/shard_map/ppermute | solution.py:335
  210.4 16.4 %collective-permute-start.23 = (bf16[128,2304]{1,0:T(8,128)(2,1)}, bf16[128,2304]{1,0:T(8,128)(2,1)S(1)}, u32[]{:S(2)}, u32[]{:S(2)}) collective-permute-start(bf16[128,2304]{1,0:T(8,128)(2,1)} %get-tuple-element.67.rest_0_), channel_id=1, source_target_pairs={{0,2},{1,3},{2,0},{3,1},{4,6},{5,7},{6,4},{7,5},{8,10},{9,11},{10,... | collective-permute-start | bytes 1769480 | tf_op jit(solution)/shard_map/ppermute | solution.py:335
  214.9 21.8 %collective-permute-start.26 = (bf16[128,2304]{1,0:T(8,128)(2,1)S(1)}, bf16[128,2304]{1,0:T(8,128)(2,1)S(1)}, u32[]{:S(2)}, u32[]{:S(2)}) collective-permute-start(bf16[128,2304]{1,0:T(8,128)(2,1)S(1)} %get-tuple-element.64), channel_id=1, source_target_pairs={{0,2},{1,3},{2,0},{3,1},{4,6},{5,7},{6,4},{7,5},{8,10},{9,11},{10,... | collective-permute-start | bytes 1769480 | tf_op jit(solution)/shard_map/ppermute | solution.py:335
  226.9 9.8 %copy-start.35 = (bf16[64,2304]{1,0:T(8,128)(2,1)S(1)}, bf16[64,2304]{1,0:T(8,128)(2,1)}, u32[]{:S(2)}) copy-start(bf16[64,2304]{1,0:T(8,128)(2,1)} %get-tuple-element.54.rest_3_) | copy-start | bytes 884740
  226.9 11.8 %copy-start.29 = (bf16[512,2304]{1,0:T(8,128)(2,1)S(1)}, bf16[512,2304]{1,0:T(8,128)(2,1)}, u32[]{:S(2)}) copy-start(bf16[512,2304]{1,0:T(8,128)(2,1)} %gather_rows.19) | copy-start | bytes 7077892
  226.9 11.5 %collective-permute-start.28 = (bf16[128,2304]{1,0:T(8,128)(2,1)S(1)}, bf16[128,2304]{1,0:T(8,128)(2,1)S(1)}, u32[]{:S(2)}, u32[]{:S(2)}) collective-permute-start(bf16[128,2304]{1,0:T(8,128)(2,1)S(1)} %get-tuple-element.63), channel_id=1, source_target_pairs={{0,4},{1,5},{2,6},{3,7},{4,0},{5,1},{6,2},{7,3},{8,12},{9,13},{10,... | collective-permute-start | bytes 1769480 | tf_op jit(solution)/shard_map/ppermute | solution.py:335
  229.5 11.7 %copy-start.10 = (bf16[64,2304]{1,0:T(8,128)(2,1)}, bf16[64,2304]{1,0:T(8,128)(2,1)S(1)}, u32[]{:S(2)}) copy-start(bf16[64,2304]{1,0:T(8,128)(2,1)S(1)} %collective-permute-done.15.refs_1_) | copy-start | bytes 884740
  229.5 12.5 %collective-permute-start.17 = (bf16[64,2304]{1,0:T(8,128)(2,1)S(1)}, bf16[64,2304]{1,0:T(8,128)(2,1)S(1)}, u32[]{:S(2)}, u32[]{:S(2)}) collective-permute-start(bf16[64,2304]{1,0:T(8,128)(2,1)S(1)} %copy-done.36), channel_id=1, source_target_pairs={{0,4},{1,5},{2,6},{3,7},{4,0},{5,1},{6,2},{7,3},{8,12},{9,13},{10,... | collective-permute-start | bytes 884744 | tf_op jit(solution)/shard_map/ppermute | solution.py:335
  236.6 9.9 %collective-permute-start.18 = (bf16[64,2304]{1,0:T(8,128)(2,1)S(1)}, bf16[64,2304]{1,0:T(8,128)(2,1)S(1)}, u32[]{:S(2)}, u32[]{:S(2)}) collective-permute-start(bf16[64,2304]{1,0:T(8,128)(2,1)S(1)} %copy-done.35), channel_id=1, source_target_pairs={{0,2},{1,3},{2,0},{3,1},{4,6},{5,7},{6,4},{7,5},{8,10},{9,11},{10,... | collective-permute-start | bytes 884744 | tf_op jit(solution)/shard_map/ppermute | solution.py:335
  238.4 16.9 %copy-start.22 = (bf16[320,2304]{1,0:T(8,128)(2,1)S(1)}, bf16[320,2304]{1,0:T(8,128)(2,1)}, u32[]{:S(2)}) copy-start(bf16[320,2304]{1,0:T(8,128)(2,1)} %copy-done.21) | copy-start | bytes 4423684
  238.4 16.9 %copy-start.24 = (bf16[320,2304]{1,0:T(8,128)(2,1)S(1)}, bf16[320,2304]{1,0:T(8,128)(2,1)}, u32[]{:S(2)}) copy-start(bf16[320,2304]{1,0:T(8,128)(2,1)} %copy-done.23) | copy-start | bytes 4423684
  238.4 14.5 %collective-permute-start.14 = (bf16[64,2304]{1,0:T(8,128)(2,1)S(1)}, bf16[64,2304]{1,0:T(8,128)(2,1)S(1)}, u32[]{:S(2)}, u32[]{:S(2)}) collective-permute-start(bf16[64,2304]{1,0:T(8,128)(2,1)S(1)} %get-tuple-element.46), channel_id=1, source_target_pairs={{0,2},{1,3},{2,0},{3,1},{4,6},{5,7},{6,4},{7,5},{8,10},{9,11},{10,... | collective-permute-start | bytes 884744 | tf_op jit(solution)/shard_map/ppermute | solution.py:335
  242.0 16.1 %collective-permute-start.20 = (bf16[64,2304]{1,0:T(8,128)(2,1)}, bf16[64,2304]{1,0:T(8,128)(2,1)}, u32[]{:S(2)}, u32[]{:S(2)}) collective-permute-start(bf16[64,2304]{1,0:T(8,128)(2,1)} %get-tuple-element.70.rest_2_), channel_id=1, source_target_pairs={{0,4},{1,5},{2,6},{3,7},{4,0},{5,1},{6,2},{7,3},{8,12},{9,13},{10,... | collective-permute-start | bytes 884744 | tf_op jit(solution)/shard_map/ppermute | solution.py:335
  242.7 15.4 %collective-permute-start.22 = (bf16[64,2304]{1,0:T(8,128)(2,1)}, bf16[64,2304]{1,0:T(8,128)(2,1)}, u32[]{:S(2)}, u32[]{:S(2)}) collective-permute-start(bf16[64,2304]{1,0:T(8,128)(2,1)} %get-tuple-element.49.rest_3_), channel_id=1, source_target_pairs={{0,2},{1,3},{2,0},{3,1},{4,6},{5,7},{6,4},{7,5},{8,10},{9,11},{10,... | collective-permute-start | bytes 884744 | tf_op jit(solution)/shard_map/ppermute | solution.py:335
  247.2 10.9 %collective-permute-start.24 = (bf16[64,2304]{1,0:T(8,128)(2,1)}, bf16[64,2304]{1,0:T(8,128)(2,1)}, u32[]{:S(2)}, u32[]{:S(2)}) collective-permute-start(bf16[64,2304]{1,0:T(8,128)(2,1)} %get-tuple-element.66), channel_id=1, source_target_pairs={{0,4},{1,5},{2,6},{3,7},{4,0},{5,1},{6,2},{7,3},{8,12},{9,13},{10,... | collective-permute-start | bytes 884744 | tf_op jit(solution)/shard_map/ppermute | solution.py:335
  247.2 11.8 %collective-permute-start.27 = (bf16[64,2304]{1,0:T(8,128)(2,1)}, bf16[64,2304]{1,0:T(8,128)(2,1)}, u32[]{:S(2)}, u32[]{:S(2)}) collective-permute-start(bf16[64,2304]{1,0:T(8,128)(2,1)} %get-tuple-element.62), channel_id=1, source_target_pairs={{0,4},{1,5},{2,6},{3,7},{4,0},{5,1},{6,2},{7,3},{8,12},{9,13},{10,... | collective-permute-start | bytes 884744 | tf_op jit(solution)/shard_map/ppermute | solution.py:335
  253.5 3.1 copy-start.38
  253.5 7.0 %collective-permute-start.29 = (bf16[64,2304]{1,0:T(8,128)(2,1)}, bf16[64,2304]{1,0:T(8,128)(2,1)}, u32[]{:S(2)}, u32[]{:S(2)}) collective-permute-start(bf16[64,2304]{1,0:T(8,128)(2,1)} %get-tuple-element.41), channel_id=1, source_target_pairs={{0,2},{1,3},{2,0},{3,1},{4,6},{5,7},{6,4},{7,5},{8,10},{9,11},{10,... | collective-permute-start | bytes 884744 | tf_op jit(solution)/shard_map/ppermute | solution.py:335
  389.8 7.2 %copy-start.30 = (bf16[8192,256]{1,0:T(8,128)(2,1)S(1)}, bf16[8192,256]{1,0:T(8,128)(2,1)}, u32[]{:S(2)}) copy-start(bf16[8192,256]{1,0:T(8,128)(2,1)} %get-tuple-element.29) | copy-start | bytes 12582916
  (23 other events, 26.7 us)
Sparse Core Ops, SparseCore 0:
  9.8 69.6 all-gather.2

commit v3 on v2

--- a/solution.py
+++ b/solution.py
@@ -11,7 +11,7 @@
 EPSILON = 1e-6
 ROPE_BASE = 10000.0
 TILE = 128
-CHUNKS = 5
+CHUNKS = 2
 HEAD_ROWS = 640
 TAIL_ROWS = 640
 SEND_ROWS = 512
@@ -75,7 +75,7 @@
 
     wait(step, slot)
     lanes = lax.broadcasted_iota(jnp.int32, (TILE, 2 * TILE), 1).astype(jnp.float32)
-    wanted = jnp.broadcast_to(cols_ref[0], (TILE, TILE)).T
+    wanted = jnp.broadcast_to(cols_ref[base + step], (TILE, TILE)).T
     select = jnp.where(lanes == jnp.concatenate([wanted, wanted], axis=1), normalizer, jnp.zeros((), jnp.bfloat16))
     for piece in range(width // 256):
         cols = pl.ds(piece * 256, 256)
@@ -91,7 +91,7 @@
     grid_spec = pltpu.PrefetchScalarGridSpec(
         num_scalar_prefetch=2,
         grid=(tiles,),
-        in_specs=[pl.BlockSpec((1, 1, TILE), lambda i, *_: (base + i, 0, 0)), anywhere] + [anywhere] * len(after),
+        in_specs=[pl.BlockSpec(cols.shape, lambda i, *_: (0, 0, 0)), anywhere] + [anywhere] * len(after),
         out_specs=pl.BlockSpec((TILE, width), lambda i, *_: (i, 0)),
         scratch_shapes=[pltpu.VMEM((3, TILE // 8, 16, width), jnp.bfloat16), pltpu.SemaphoreType.DMA((3,))],
     )
@@ -173,7 +173,7 @@
     rows = cols.shape[0]
     width = head.shape[1]
     vmem = pl.BlockSpec(memory_space=pltpu.VMEM)
-    hbm = pl.BlockSpec(memory_space=pltpu.HBM)
+    hbm = pl.BlockSpec(memory_space=pl.ANY)
     shape = jax.ShapeDtypeStruct((rows, width), jnp.bfloat16)
     dma = pltpu.SemaphoreType.DMA
     return pl.pallas_call(
@@ -195,8 +195,8 @@
     )(more, cols, gain, head, extra, *pieces)
 
 
-def heads_kernel(rows, normed, cos_ref, sin_ref, wq_hbm, wk_hbm, wv_hbm, q_out, kv_out,
-                 wq, wk, wv, q_stage, kv_stage, w_sem, q_send, q_recv, kv_send, kv_recv,
+def heads_kernel(rows, normed_hbm, cos_ref, sin_ref, wq_hbm, wk_hbm, wv_hbm, q_out, kv_out,
+                 wq, wk, wv, normed, q_stage, kv_stage, w_sem, q_send, q_recv, kv_send, kv_recv,
                  own_recv, fwd_send, fwd_recv, keep_sem):
     group = lax.axis_index("dp")
     me = lax.axis_index("tp")
@@ -206,7 +206,7 @@
     tiles = rows // SEND_ROWS
     half = HEAD_DIM // 2
 
-    loads = [pltpu.make_async_copy(src, dst, w_sem.at[n]) for n, (src, dst) in enumerate(((wk_hbm, wk), (wv_hbm, wv), (wq_hbm, wq)))]
+    loads = [pltpu.make_async_copy(src, dst, w_sem.at[n]) for n, (src, dst) in enumerate(((normed_hbm, normed), (wk_hbm, wk), (wv_hbm, wv), (wq_hbm, wq)))]
     for load in loads:
         load.start()
 
@@ -307,15 +307,16 @@
     return pl.pallas_call(
         functools.partial(heads_kernel, rows),
         out_shape=(jax.ShapeDtypeStruct((tokens, HEAD_DIM), jnp.bfloat16), jax.ShapeDtypeStruct((2, tokens, HEAD_DIM), jnp.bfloat16)),
-        in_specs=[vmem, vmem, vmem, anywhere, anywhere, anywhere],
+        in_specs=[anywhere, vmem, vmem, anywhere, anywhere, anywhere],
         out_specs=(anywhere, anywhere),
         scratch_shapes=[
             pltpu.VMEM(wq_all.shape, jnp.bfloat16),
             pltpu.VMEM(w_key.shape, jnp.bfloat16),
             pltpu.VMEM(w_value.shape, jnp.bfloat16),
+            pltpu.VMEM((rows, width), jnp.bfloat16),
             pltpu.VMEM((heads, rows, HEAD_DIM), jnp.bfloat16),
             pltpu.VMEM((2, CHIPS, rows, HEAD_DIM), jnp.bfloat16),
-            dma((3,)),
+            dma((4,)),
             dma((CHIPS, 2)), dma((CHIPS, 2)),
             dma((CHIPS, 2)), dma((CHIPS, 2, tiles)),
             dma((2,)),
@@ -334,26 +335,32 @@
     def exchange(rows, bit):
         return lax.ppermute(rows, "tp", [(i, i ^ bit) for i in range(group_size)])
 
-    def share_head(rows, dev_index):
+    def pass_head(values, pairs, after=None):
+        got = lax.ppermute(values, "tp", pairs)
+        if after is not None:
+            got, _ = lax.optimization_barrier((got, after))
+        return jnp.where(lax.axis_index("tp") == pairs[0][1], got, values)
+
+    def share_head(rows):
         half = rows.shape[0] // 2
-        first, second = rows[:half], rows[half:]
-        first_x = lax.ppermute(first, "tp", [(0, 2)])
-        second_y = lax.ppermute(second, "tp", [(0, 4)])
-        first = jnp.where(dev_index == 2, first_x, first)
-        second = jnp.where(dev_index == 4, second_y, second)
-        first_y = lax.ppermute(first, "tp", [(0, 4), (2, 6)])
-        second_x = lax.ppermute(second, "tp", [(0, 2), (4, 6)])
-        first = jnp.where(dev_index >= 4, first_y, first)
-        second = jnp.where(dev_index % 4 >= 2, second_x, second)
+        first = pass_head(rows[:half], [(0, 2)])
+        second = pass_head(rows[half:], [(0, 4)])
+        first = pass_head(first, [(2, 6)])
+        second = pass_head(second, [(4, 6)])
+        return first, second
+
+    def share_head_back(first, second, after):
+        first = pass_head(first, [(6, 4)], after)
+        second = pass_head(second, [(6, 2)], after)
         both = jnp.concatenate([first, second], axis=0)
         other = lax.ppermute(both, "tp", [(0, 1), (2, 3), (4, 5), (6, 7)])
-        return jnp.where(dev_index % 2 == 1, other, both)
+        return jnp.where(lax.axis_index("tp") % 2 == 1, other, both)
 
     def local_body(token_ids, positions, table_rows, norm_scale, w_query, w_key, w_value):
         dev_index = lax.axis_index("tp")
         vocab_rows, model_width = table_rows.shape
         wq_all = lax.all_gather(w_query, "tp", axis=0)
-        head = share_head(table_rows[:HEAD_ROWS], dev_index)
+        head_halves = share_head(table_rows[:HEAD_ROWS])
         tokens = token_ids.shape[0]
         block_rows = tokens // group_size
         extra_rows = block_rows - TAIL_ROWS
@@ -402,7 +409,7 @@
         pieces, sums = [], []
         after, late, late_next = [], [], []
         for chunk in range(CHUNKS):
-            other = gather(chunk, 1, after + late + ([wq_all] if chunk == 2 else []))
+            other = gather(chunk, 1, after + late + ([wq_all] if chunk == 1 else []))
             got = exchange(other, 1)
             mine = gather(chunk, 0, [other])
             after, late = [], late_next
@@ -420,6 +427,8 @@
                 late_next.append(near_send)
                 pieces += [mine[keep[0]] + got[keep[0]] + back[:half], back2]
 
+        head = share_head_back(*head_halves, pieces[2])
+
         def second_exchange(rows):
             ids = ranked_ids(TAIL_ROWS, extra_rows).reshape(-1)
             normalizer = jnp.asarray(math.sqrt(model_width), dtype=jnp.bfloat16)

time: 414 us -> 363 us (0.88)
  waiting for transfers between devices: 89.2 us -> 43.6 us
  starting transfers between devices: 32.9 us -> 67.9 us
  Pallas kernels: 179 us -> 161 us
  local copies, waits for them, and re-layouts: 36 us -> 23.9 us
  other arithmetic: 46.9 us -> 38.3 us
    ppermute x25 -> x10, waiting for transfers between devices: 88.5 us -> 30.9 us  [exchange(): return lax.ppermute(rows, 'tp', [(i, i ^ bit) for i in range(group_size)])]
    ppermute x25 -> x10, starting transfers between devices: 17.8 us -> 49.8 us  [exchange(): return lax.ppermute(rows, 'tp', [(i, i ^ bit) for i in range(group_size)])]
    pallas_call x10 -> x4, Pallas kernels: 66.5 us -> 48.4 us  [gather_rows(): pl.pallas_call(functools.partial(gather_kernel, base, tiles, width), grid...]
    ppermute x5 -> x7, waiting for transfers between devices: 0.01 us -> 12 us  [the longest x6 12 us: pass_head(): got = lax.ppermute(values, 'tp', pairs)]
    unnamed x81 -> x46, local copies, waits for them, and re-layouts: 22.3 us -> 12.2 us
    add x3 -> x0, other arithmetic: 8.11 us -> none  [local_body(): pieces += [mine[keep[0]] + got[keep[0]] + back[:half], back2]]
    add x5 -> x2, other arithmetic: 12.3 us -> 6.87 us  [local_body(): sent = mine[far] + got[far]]
    add x2, other arithmetic: 5.6 us -> 10.5 us  [local_body(): near_send = mine[keep[1]] + got[keep[1]] + back[half:]]
  transfers between devices with their start and end apart: 31 -> 18, of which waited for: 11 -> 7; matrix products, arithmetic and copies ran while one was open for 14% -> 13% of each run, Pallas kernels for 16% -> 14%
where the time goes in v3:
time: 363 us; the launch traced here: 357 us
  Pallas kernels  161 us (44%)
  starting transfers between devices  67.9 us (19%)
  waiting for transfers between devices  43.6 us (12%)
  other arithmetic  38.3 us (11%)
  local copies, waits for them, and re-layouts  23.9 us (7%)
  between operations  15.8 us (4%)
  blocking collectives  4.84 us (1%)
    pallas_call x1, Pallas kernels, project_heads(): pl.pallas_call(functools.partial(heads_kernel, rows), out_shape=(jax.Shap...  98.1 us
    ppermute x10, starting transfers between devices, exchange(): return lax.ppermute(rows, 'tp', [(i, i ^ bit) for i in range(group_size)])  49.8 us
    pallas_call x4, Pallas kernels, gather_rows(): pl.pallas_call(functools.partial(gather_kernel, base, tiles, width), grid...  48.4 us
    ppermute x10, waiting for transfers between devices, exchange(): return lax.ppermute(rows, 'tp', [(i, i ^ bit) for i in range(group_size)])  30.9 us
    ppermute x6, starting transfers between devices, pass_head(): got = lax.ppermute(values, 'tp', pairs)  15.2 us
    pallas_call x1, Pallas kernels, finish_rows(): pl.pallas_call(functools.partial(finish_kernel, len(pieces)), out_shape=(...  14.4 us
    unnamed x46, local copies, waits for them, and re-layouts  12.2 us
    ppermute x6, waiting for transfers between devices, pass_head(): got = lax.ppermute(values, 'tp', pairs)  12 us
  transfers between devices with their start and end apart: 18, of which 7 were waited for; matrix products, arithmetic and copies ran while one was open for 13% of the time, Pallas kernels for 14%

profile of v3, /device:TPU:0, one launch (start us, length us, event | category | flops | bytes accessed | tf_op | source)
XLA Modules:
  0.0 356.9 jit_solution(1618370507491328844)
XLA Ops:
  7.9 3.1 fusion.13
  11.0 5.2 %collective-permute-start.2 = (bf16[320,2304]{1,0:T(8,128)(2,1)}, bf16[320,2304]{1,0:T(8,128)(2,1)S(1)}, u32[]{:S(2)}, u32[]{:S(2)}) collective-permute-start(bf16[320,2304]{1,0:T(8,128)(2,1)} %get-tuple-element.39), channel_id=1, source_target_pairs={{0,2},{8,10}} | collective-permute-start | bytes 4423688 | tf_op jit(solution)/shard_map/ppermute | solution.py:339
  16.2 2.5 collective-permute-start.6
  20.4 3.0 select_reduce_fusion.1
  24.0 1.4 fusion.9
  25.4 2.6 select_reduce_fusion.2
  28.0 12.6 %gather_rows.4.rest_0_ = bf16[1280,2304]{1,0:T(8,128)(2,1)} custom-call(s32[5120]{0:T(1024)} %bitcast.35, s32[40]{0:T(128)} %get-tuple-element.63.counts, f32[40,1,128]{2,1,0:T(1,128)} %bitcast.39, bf16[32000,2304]{1,0:T(8,128)(2,1)} %table_ref.7), custom_call_target="tpu_custom_call" | custom-call | flops 25600000000 | bytes 17694720 | tf_op jit(solution)/shard_map/gather_rows/pallas_call | solution.py:98
  40.6 9.6 %collective-permute-done.2 = bf16[320,2304]{1,0:T(8,128)(2,1)S(1)} collective-permute-done((bf16[320,2304]{1,0:T(8,128)(2,1)}, bf16[320,2304]{1,0:T(8,128)(2,1)S(1)}, u32[]{:S(2)}, u32[]{:S(2)}) %collective-permute-start.2) | collective-permute-done | bytes 1474592 | tf_op jit(solution)/shard_map/ppermute | solution.py:339
  51.4 2.4 collective-permute-done.6
  53.7 2.1 broadcast_select_fusion.2
  55.8 1.9 collective-permute-start.3
  57.7 1.9 collective-permute-start.7
  59.6 12.7 %gather_rows.5 = bf16[1280,2304]{1,0:T(8,128)(2,1)} custom-call(s32[5120]{0:T(1024)} %bitcast.36, s32[40]{0:T(128)} %get-tuple-element.63.counts, f32[40,1,128]{2,1,0:T(1,128)} %bitcast.40, bf16[32000,2304]{1,0:T(8,128)(2,1)} %table_ref.7, bf16[1280,2304]{1,0:T(8,128)(2,1)} %gather_rows.4.rest_0_), custom_call_target="tpu_custom_call" | custom-call | flops 25600000000 | bytes 17694720 | tf_op jit(solution)/shard_map/gather_rows/pallas_call | solution.py:98
  72.3 1.3 broadcast_select_fusion.4
  73.6 2.0 collective-permute-start.4
  75.6 1.3 broadcast_select_fusion.3
  76.9 1.8 collective-permute-start.8
  78.7 2.3 slice_add_fusion.2
  81.0 24.8 %collective-permute-start.5 = (bf16[320,2304]{1,0:T(8,128)(2,1)S(1)}, bf16[320,2304]{1,0:T(8,128)(2,1)}, u32[]{:S(2)}, u32[]{:S(2)}) collective-permute-start(bf16[320,2304]{1,0:T(8,128)(2,1)S(1)} %get-tuple-element.55.rest_1_), channel_id=1, source_target_pairs={{0,4},{1,5},{2,6},{3,7},{4,0},{5,1},{6,2},{7,3},{8,12},{9,13},{10,... | collective-permute-start | bytes 4423688 | tf_op jit(solution)/shard_map/ppermute | solution.py:336
  105.8 10.4 %collective-permute-start.11 = (bf16[320,2304]{1,0:T(8,128)(2,1)S(1)}, bf16[320,2304]{1,0:T(8,128)(2,1)}, u32[]{:S(2)}, u32[]{:S(2)}) collective-permute-start(bf16[320,2304]{1,0:T(8,128)(2,1)S(1)} %get-tuple-element.56.rest_0_), channel_id=1, source_target_pairs={{0,2},{1,3},{2,0},{3,1},{4,6},{5,7},{6,4},{7,5},{8,10},{9,11},{10,... | collective-permute-start | bytes 4423688 | tf_op jit(solution)/shard_map/ppermute | solution.py:336
  116.2 11.6 %gather_rows.6.rest_0_ = bf16[1280,2304]{1,0:T(8,128)(2,1)} custom-call(s32[5120]{0:T(1024)} %bitcast.37, s32[40]{0:T(128)} %get-tuple-element.63.counts, f32[40,1,128]{2,1,0:T(1,128)} %bitcast.41, bf16[32000,2304]{1,0:T(8,128)(2,1)} %table_ref.7, bf16[320,2304]{1,0:T(8,128)(2,1)} %copy-done.10, bf16[320,2304]{1,0:T(8,128)(2,1)} %copy-done.11, ...), custom_call_target="tpu_custom_call" | custom-call | flops 25600000000 | bytes 17694720 | tf_op jit(solution)/shard_map/gather_rows/pallas_call | solution.py:98
  127.8 5.8 %collective-permute-done.11 = bf16[320,2304]{1,0:T(8,128)(2,1)} collective-permute-done((bf16[320,2304]{1,0:T(8,128)(2,1)S(1)}, bf16[320,2304]{1,0:T(8,128)(2,1)}, u32[]{:S(2)}, u32[]{:S(2)}) %collective-permute-start.11) | collective-permute-done | bytes 1474592 | tf_op jit(solution)/shard_map/ppermute | solution.py:336
  133.7 5.3 %slice_add_fusion.12 = (bf16[160,2304]{1,0:T(8,128)(2,1)}, bf16[160,2304]{1,0:T(8,128)(2,1)}, bf16[160,2304]{1,0:T(8,128)(2,1)}, bf16[160,2304]{1,0:T(8,128)(2,1)}) fusion(bf16[320,2304]{1,0:T(8,128)(2,1)} %collective-permute-done.11, bf16[1280,2304]{1,0:T(8,128)(2,1)} %collective-permute-done, bf16[1280,2304]{1,0:T(8,128)(2,1)} %gather_rows.5, ...), kind=kLoop, calls=%fused_computation.45 | loop fusion | flops 2949120 | bytes 11796480 | tf_op jit(solution)/shard_map/add | solution.py:423
  138.9 1.5 broadcast_select_fusion.1
  140.5 2.1 broadcast_select_fusion.6
  143.9 2.9 collective-permute-start.9
  146.8 11.6 %gather_rows.7 = bf16[1280,2304]{1,0:T(8,128)(2,1)} custom-call(s32[5120]{0:T(1024)} %bitcast.38, s32[40]{0:T(128)} %get-tuple-element.63.counts, f32[40,1,128]{2,1,0:T(1,128)} %bitcast.42, bf16[32000,2304]{1,0:T(8,128)(2,1)} %table_ref.7, bf16[1280,2304]{1,0:T(8,128)(2,1)} %gather_rows.6.rest_0_), custom_call_target="tpu_custom_call" | custom-call | flops 25600000000 | bytes 17694720 | tf_op jit(solution)/shard_map/gather_rows/pallas_call | solution.py:98
  158.4 4.6 %slice_add_fusion = (bf16[320,2304]{1,0:T(8,128)(2,1)}, bf16[320,2304]{1,0:T(8,128)(2,1)}) fusion(bf16[1280,2304]{1,0:T(8,128)(2,1)} %collective-permute-done.1, bf16[1280,2304]{1,0:T(8,128)(2,1)} %gather_rows.7), kind=kLoop, calls=%fused_computation.21 | loop fusion | flops 1474560 | bytes 8847360 | tf_op jit(solution)/shard_map/add | solution.py:421
  163.0 5.2 %collective-permute-start.15 = (bf16[320,2304]{1,0:T(8,128)(2,1)}, bf16[320,2304]{1,0:T(8,128)(2,1)}, u32[]{:S(2)}, u32[]{:S(2)}) collective-permute-start(bf16[320,2304]{1,0:T(8,128)(2,1)} %get-tuple-element.51), channel_id=1, source_target_pairs={{0,4},{1,5},{2,6},{3,7},{4,0},{5,1},{6,2},{7,3},{8,12},{9,13},{10,... | collective-permute-start | bytes 4423688 | tf_op jit(solution)/shard_map/ppermute | solution.py:336
  168.2 5.2 %collective-permute-start.13 = (bf16[320,2304]{1,0:T(8,128)(2,1)}, bf16[320,2304]{1,0:T(8,128)(2,1)}, u32[]{:S(2)}, u32[]{:S(2)}) collective-permute-start(bf16[320,2304]{1,0:T(8,128)(2,1)} %get-tuple-element.52), channel_id=1, source_target_pairs={{0,2},{1,3},{2,0},{3,1},{4,6},{5,7},{6,4},{7,5},{8,10},{9,11},{10,... | collective-permute-start | bytes 4423688 | tf_op jit(solution)/shard_map/ppermute | solution.py:336
  176.5 3.0 multiply_sine_fusion
  179.5 2.0 collective-permute-start.12
  181.5 20.1 %collective-permute-done.15 = bf16[320,2304]{1,0:T(8,128)(2,1)} collective-permute-done((bf16[320,2304]{1,0:T(8,128)(2,1)}, bf16[320,2304]{1,0:T(8,128)(2,1)}, u32[]{:S(2)}, u32[]{:S(2)}) %collective-permute-start.15) | collective-permute-done | bytes 1474592 | tf_op jit(solution)/shard_map/ppermute | solution.py:336
  201.6 2.7 collective-permute-done.13
  204.3 5.2 %slice_add_fusion.4 = (bf16[160,2304]{1,0:T(8,128)(2,1)}, bf16[160,2304]{1,0:T(8,128)(2,1)}, bf16[160,2304]{1,0:T(8,128)(2,1)}, bf16[160,2304]{1,0:T(8,128)(2,1)}) fusion(bf16[320,2304]{1,0:T(8,128)(2,1)} %collective-permute-done.15, bf16[1280,2304]{1,0:T(8,128)(2,1)} %collective-permute-done.1, bf16[1280,2304]{1,0:T(8,128)(2,1)} %gather_rows.7, ...), kind=kLoop, calls=%fused_computation.37 | loop fusion | flops 2949120 | bytes 11796480 | tf_op jit(solution)/shard_map/add | solution.py:423
  209.9 1.7 collective-permute-start.14
  212.5 4.8 %pmax.7 = s32[]{:T(128)} all-reduce(s32[]{:T(128)S(6)} %convert_element_type.29), channel_id=1, replica_groups=mesh['dp'=2,'tp'=8] {'dp'}, use_global_device_ids=true, to_apply=%region_5.6 | all-reduce | flops 1 | bytes 8 | tf_op jit(solution)/shard_map/pmax | solution.py:443
  217.9 1.4 conditional.1
  218.0 1.4 broadcast.217
  219.4 2.0 collective-permute-done.16.refs_7_
  221.7 1.1 copy-done
  222.8 1.1 copy-done.1
  223.9 1.1 copy-done.2
  226.2 14.4 %finish_rows.1 = (bf16[1024,2304]{1,0:T(8,128)(2,1)}, bf16[1024,2304]{1,0:T(8,128)(2,1)S(1)}) custom-call(s32[1]{0:T(128)} %bitcast.7.more, s32[1024,1]{1,0:T(8,128)S(1)} %copy.17.cols_ref, f32[1,2304]{1,0:T(1,128)S(1)} %broadcast_in_dim.89.gain_ref, bf16[640,2304]{1,0:T(8,128)(2,1)S(1)} %broadcast_select_fusion.head_hbm, ...), custom_call_target="tpu_custom_call" | custom-call | flops 6039797760 | bytes 16000000 | tf_op jit(solution)/shard_map/finish_rows/pallas_call | solution.py:179
  240.5 2.2 copy-done.4
  242.7 98.1 %project_heads.1 = (bf16[8192,256]{1,0:T(8,128)(2,1)}, bf16[2,8192,256]{2,1,0:T(8,128)(2,1)}) custom-call(bf16[1024,2304]{1,0:T(8,128)(2,1)} %copy-done.4, f32[1024,128]{1,0:T(8,128)} %get-tuple-element.66.cos_ref, f32[1024,128]{1,0:T(8,128)} %get-tuple-element.65.sin_ref, bf16[8,2304,256]{2,1,0:T(8,128)(2,1)} %bitcast.33, bf16[2304,1024]{1,0:T(8,128)(2,1)} %wk_hbm.1, ...), custom_call_target="tpu_custom_call" | custom-call | flops 19327352832 | bytes 40000000 | tf_op jit(solution)/shard_map/project_heads/pallas_call | solution.py:307
  340.9 6.6 %slice_bitcast_fusion = (bf16[8192,1,256]{2,0,1:T(8,128)(2,1)}, bf16[8192,1,256]{2,0,1:T(8,128)(2,1)}) fusion(bf16[2,8192,256]{2,1,0:T(8,128)(2,1)} %get-tuple-element.34), kind=kLoop, calls=%fused_computation.13 | loop fusion | bytes 16777216 | tf_op jit(solution)/shard_map/broadcast_in_dim;squeeze | solution.py:452
  348.0 2.0 copy.26
  (84 shorter events, 11.0 us)
Async XLA Ops:
  7.2 109.0 %all-gather.3.cloned.1.call-start = ((), (), s32[]{:S(2)}) async-start(), calls=%async_computation.2 | async-start | bytes 10616832 | tf_op jit(solution)/shard_map/all_gather | solution.py:362
  7.9 10.8 %copy-start.17 = (s32[8192]{0:T(1024)S(1)}, s32[8192]{0:T(1024)}, u32[]{:S(2)}) copy-start(s32[8192]{0:T(1024)} %param.9) | copy-start | bytes 98308
  11.0 39.2 %collective-permute-start.2 = (bf16[320,2304]{1,0:T(8,128)(2,1)}, bf16[320,2304]{1,0:T(8,128)(2,1)S(1)}, u32[]{:S(2)}, u32[]{:S(2)}) collective-permute-start(bf16[320,2304]{1,0:T(8,128)(2,1)} %get-tuple-element.39), channel_id=1, source_target_pairs={{0,2},{8,10}} | collective-permute-start | bytes 4423688 | tf_op jit(solution)/shard_map/ppermute | solution.py:339
  16.2 37.5 %collective-permute-start.6 = (bf16[320,2304]{1,0:T(8,128)(2,1)S(1)}, bf16[320,2304]{1,0:T(8,128)(2,1)}, u32[]{:S(2)}, u32[]{:S(2)}) collective-permute-start(bf16[320,2304]{1,0:T(8,128)(2,1)S(1)} %get-tuple-element.40), channel_id=1, source_target_pairs={{0,4},{8,12}} | collective-permute-start | bytes 4423688 | tf_op jit(solution)/shard_map/ppermute | solution.py:339
  18.7 1.0 copy-start.16
  19.5 3.9 %copy-start.18 = (pred[8,1024]{1,0:T(8,128)(4,1)}, pred[8,1024]{1,0:T(8,128)(4,1)S(1)}, u32[]{:S(2)}) copy-start(pred[8,1024]{1,0:T(8,128)(4,1)S(1)} %get-tuple-element.36) | copy-start | bytes 24580
  19.8 0.6 copy-start.14
  40.6 38.1 %collective-permute-start = (bf16[1280,2304]{1,0:T(8,128)(2,1)}, bf16[1280,2304]{1,0:T(8,128)(2,1)}, u32[]{:S(2)}, u32[]{:S(2)}) collective-permute-start(bf16[1280,2304]{1,0:T(8,128)(2,1)} %gather_rows.4.rest_0_), channel_id=1, source_target_pairs={{0,1},{1,0},{2,3},{3,2},{4,5},{5,4},{6,7},{7,6},{8,9},{9,8},{10,11... | collective-permute-start | bytes 17694728 | tf_op jit(solution)/shard_map/ppermute | solution.py:336
  50.3 1.1 copy-start.13
  55.8 16.4 %collective-permute-start.3 = (bf16[320,2304]{1,0:T(8,128)(2,1)S(1)}, bf16[320,2304]{1,0:T(8,128)(2,1)}, u32[]{:S(2)}, u32[]{:S(2)}) collective-permute-start(bf16[320,2304]{1,0:T(8,128)(2,1)S(1)} %get-tuple-element.37), channel_id=1, source_target_pairs={{2,6},{10,14}} | collective-permute-start | bytes 4423688 | tf_op jit(solution)/shard_map/ppermute | solution.py:339
  57.7 17.9 %collective-permute-start.7 = (bf16[320,2304]{1,0:T(8,128)(2,1)S(1)}, bf16[320,2304]{1,0:T(8,128)(2,1)}, u32[]{:S(2)}, u32[]{:S(2)}) collective-permute-start(bf16[320,2304]{1,0:T(8,128)(2,1)S(1)} %get-tuple-element.38), channel_id=1, source_target_pairs={{4,6},{12,14}} | collective-permute-start | bytes 4423688 | tf_op jit(solution)/shard_map/ppermute | solution.py:339
  72.3 6.4 %copy-start.5 = (bf16[1280,2304]{1,0:T(8,128)(2,1)S(1)}, bf16[1280,2304]{1,0:T(8,128)(2,1)}, u32[]{:S(2)}) copy-start(bf16[1280,2304]{1,0:T(8,128)(2,1)} %gather_rows.5) | copy-start | bytes 17694724
  73.6 65.3 %collective-permute-start.4 = (bf16[320,2304]{1,0:T(8,128)(2,1)}, bf16[320,2304]{1,0:T(8,128)(2,1)}, u32[]{:S(2)}, u32[]{:S(2)}) collective-permute-start(bf16[320,2304]{1,0:T(8,128)(2,1)} %broadcast_select_fusion.4), channel_id=1, source_target_pairs={{6,4},{14,12}} | collective-permute-start | bytes 4423688 | tf_op jit(solution)/shard_map/ppermute | solution.py:339
  76.9 62.1 %collective-permute-start.8 = (bf16[320,2304]{1,0:T(8,128)(2,1)}, bf16[320,2304]{1,0:T(8,128)(2,1)}, u32[]{:S(2)}, u32[]{:S(2)}) collective-permute-start(bf16[320,2304]{1,0:T(8,128)(2,1)} %broadcast_select_fusion.3), channel_id=1, source_target_pairs={{6,2},{14,10}} | collective-permute-start | bytes 4423688 | tf_op jit(solution)/shard_map/ppermute | solution.py:339
  80.9 35.3 %copy-start.10 = (bf16[320,2304]{1,0:T(8,128)(2,1)}, bf16[320,2304]{1,0:T(8,128)(2,1)S(1)}, u32[]{:S(2)}) copy-start(bf16[320,2304]{1,0:T(8,128)(2,1)S(1)} %get-tuple-element.56.rest_0_) | copy-start | bytes 4423684
  81.0 35.3 %copy-start.11 = (bf16[320,2304]{1,0:T(8,128)(2,1)}, bf16[320,2304]{1,0:T(8,128)(2,1)S(1)}, u32[]{:S(2)}) copy-start(bf16[320,2304]{1,0:T(8,128)(2,1)S(1)} %get-tuple-element.55.rest_1_) | copy-start | bytes 4423684
  81.0 46.9 %collective-permute-start.5 = (bf16[320,2304]{1,0:T(8,128)(2,1)S(1)}, bf16[320,2304]{1,0:T(8,128)(2,1)}, u32[]{:S(2)}, u32[]{:S(2)}) collective-permute-start(bf16[320,2304]{1,0:T(8,128)(2,1)S(1)} %get-tuple-element.55.rest_1_), channel_id=1, source_target_pairs={{0,4},{1,5},{2,6},{3,7},{4,0},{5,1},{6,2},{7,3},{8,12},{9,13},{10,... | collective-permute-start | bytes 4423688 | tf_op jit(solution)/shard_map/ppermute | solution.py:336
  105.8 27.8 %collective-permute-start.11 = (bf16[320,2304]{1,0:T(8,128)(2,1)S(1)}, bf16[320,2304]{1,0:T(8,128)(2,1)}, u32[]{:S(2)}, u32[]{:S(2)}) collective-permute-start(bf16[320,2304]{1,0:T(8,128)(2,1)S(1)} %get-tuple-element.56.rest_0_), channel_id=1, source_target_pairs={{0,2},{1,3},{2,0},{3,1},{4,6},{5,7},{6,4},{7,5},{8,10},{9,11},{10,... | collective-permute-start | bytes 4423688 | tf_op jit(solution)/shard_map/ppermute | solution.py:336
  127.8 30.6 %collective-permute-start.1 = (bf16[1280,2304]{1,0:T(8,128)(2,1)}, bf16[1280,2304]{1,0:T(8,128)(2,1)}, u32[]{:S(2)}, u32[]{:S(2)}) collective-permute-start(bf16[1280,2304]{1,0:T(8,128)(2,1)} %gather_rows.6.rest_0_), channel_id=1, source_target_pairs={{0,1},{1,0},{2,3},{3,2},{4,5},{5,4},{6,7},{7,6},{8,9},{9,8},{10,11... | collective-permute-start | bytes 17694728 | tf_op jit(solution)/shard_map/ppermute | solution.py:336
  140.5 3.4 copy-start.6
  142.6 1.1 copy-start.8
  143.9 67.8 %collective-permute-start.9 = (bf16[640,2304]{1,0:T(8,128)(2,1)S(1)}, bf16[640,2304]{1,0:T(8,128)(2,1)}, u32[]{:S(2)}, u32[]{:S(2)}) collective-permute-start(bf16[640,2304]{1,0:T(8,128)(2,1)S(1)} %pad_maximum_fusion), channel_id=1, source_target_pairs={{0,1},{2,3},{4,5},{6,7},{8,9},{10,11},{12,13},{14,15}} | collective-permute-start | bytes 8847368 | tf_op jit(solution)/shard_map/ppermute | solution.py:356
  158.4 15.0 %copy-start.20 = (f32[2304]{0:T(1024)S(1)}, f32[2304]{0:T(1024)}, u32[]{:S(2)}) copy-start(f32[2304]{0:T(1024)} %param.12) | copy-start | bytes 27652
  158.4 15.0 %copy-start.21 = (s32[8]{0:T(128)S(1)}, s32[8]{0:T(128)}, u32[]{:S(2)}) copy-start(s32[8]{0:T(128)} %get-tuple-element.35) | copy-start | bytes 100
  158.4 16.3 %copy-start.15 = (s32[8,1024]{1,0:T(8,128)S(1)}, s32[8,1024]{1,0:T(8,128)}, u32[]{:S(2)}) copy-start(s32[8,1024]{1,0:T(8,128)} %copy-done.14) | copy-start | bytes 98308
  158.4 16.3 %copy-start.19 = (pred[8,1024]{1,0:T(8,128)(4,1)S(1)}, pred[8,1024]{1,0:T(8,128)(4,1)}, u32[]{:S(2)}) copy-start(pred[8,1024]{1,0:T(8,128)(4,1)} %copy-done.18) | copy-start | bytes 24580
  163.0 38.6 %collective-permute-start.15 = (bf16[320,2304]{1,0:T(8,128)(2,1)}, bf16[320,2304]{1,0:T(8,128)(2,1)}, u32[]{:S(2)}, u32[]{:S(2)}) collective-permute-start(bf16[320,2304]{1,0:T(8,128)(2,1)} %get-tuple-element.51), channel_id=1, source_target_pairs={{0,4},{1,5},{2,6},{3,7},{4,0},{5,1},{6,2},{7,3},{8,12},{9,13},{10,... | collective-permute-start | bytes 4423688 | tf_op jit(solution)/shard_map/ppermute | solution.py:336
  168.2 36.2 %collective-permute-start.13 = (bf16[320,2304]{1,0:T(8,128)(2,1)}, bf16[320,2304]{1,0:T(8,128)(2,1)}, u32[]{:S(2)}, u32[]{:S(2)}) collective-permute-start(bf16[320,2304]{1,0:T(8,128)(2,1)} %get-tuple-element.52), channel_id=1, source_target_pairs={{0,2},{1,3},{2,0},{3,1},{4,6},{5,7},{6,4},{7,5},{8,10},{9,11},{10,... | collective-permute-start | bytes 4423688 | tf_op jit(solution)/shard_map/ppermute | solution.py:336
  179.5 39.9 %collective-permute-start.12 = (bf16[160,2304]{1,0:T(8,128)(2,1)}, bf16[160,2304]{1,0:T(8,128)(2,1)}, u32[]{:S(2)}, u32[]{:S(2)}) collective-permute-start(bf16[160,2304]{1,0:T(8,128)(2,1)} %get-tuple-element.45), channel_id=1, source_target_pairs={{0,4},{1,5},{2,6},{3,7},{4,0},{5,1},{6,2},{7,3},{8,12},{9,13},{10,... | collective-permute-start | bytes 2211848 | tf_op jit(solution)/shard_map/ppermute | solution.py:336
  181.5 30.1 %copy-start.7 = (bf16[320,2304]{1,0:T(8,128)(2,1)S(1)}, bf16[320,2304]{1,0:T(8,128)(2,1)}, u32[]{:S(2)}) copy-start(bf16[320,2304]{1,0:T(8,128)(2,1)} %copy-done.6) | copy-start | bytes 4423684
  181.5 30.1 %copy-start.9 = (bf16[320,2304]{1,0:T(8,128)(2,1)S(1)}, bf16[320,2304]{1,0:T(8,128)(2,1)}, u32[]{:S(2)}) copy-start(bf16[320,2304]{1,0:T(8,128)(2,1)} %copy-done.8) | copy-start | bytes 4423684
  181.5 35.8 %collective-permute-start.10 = (bf16[160,2304]{1,0:T(8,128)(2,1)}, bf16[160,2304]{1,0:T(8,128)(2,1)}, u32[]{:S(2)}, u32[]{:S(2)}) collective-permute-start(bf16[160,2304]{1,0:T(8,128)(2,1)} %get-tuple-element.54), channel_id=1, source_target_pairs={{0,2},{1,3},{2,0},{3,1},{4,6},{5,7},{6,4},{7,5},{8,10},{9,11},{10,... | collective-permute-start | bytes 2211848 | tf_op jit(solution)/shard_map/ppermute | solution.py:336
  209.6 11.8 %collective-permute-start.16 = (bf16[160,2304]{1,0:T(8,128)(2,1)}, bf16[160,2304]{1,0:T(8,128)(2,1)}, u32[]{:S(2)}, u32[]{:S(2)}) collective-permute-start(bf16[160,2304]{1,0:T(8,128)(2,1)} %get-tuple-element.41), channel_id=1, source_target_pairs={{0,2},{1,3},{2,0},{3,1},{4,6},{5,7},{6,4},{7,5},{8,10},{9,11},{10,... | collective-permute-start | bytes 2211848 | tf_op jit(solution)/shard_map/ppermute | solution.py:336
  209.9 11.8 %collective-permute-start.14 = (bf16[160,2304]{1,0:T(8,128)(2,1)}, bf16[160,2304]{1,0:T(8,128)(2,1)}, u32[]{:S(2)}, u32[]{:S(2)}) collective-permute-start(bf16[160,2304]{1,0:T(8,128)(2,1)} %get-tuple-element.50), channel_id=1, source_target_pairs={{0,4},{1,5},{2,6},{3,7},{4,0},{5,1},{6,2},{7,3},{8,12},{9,13},{10,... | collective-permute-start | bytes 2211848 | tf_op jit(solution)/shard_map/ppermute | solution.py:336
  221.7 1.1 copy-start
  222.8 1.1 copy-start.1
  223.9 1.1 copy-start.2
  225.0 1.1 copy-start.3
  240.5 2.2 copy-start.4
  340.8 7.2 %copy-start.12 = (bf16[8192,256]{1,0:T(8,128)(2,1)S(1)}, bf16[8192,256]{1,0:T(8,128)(2,1)}, u32[]{:S(2)}) copy-start(bf16[8192,256]{1,0:T(8,128)(2,1)} %get-tuple-element.33) | copy-start | bytes 12582916
Sparse Core Ops, SparseCore 0:
  9.8 65.1 all-gather.2

commit v4 on v3

--- a/solution.py
+++ b/solution.py
@@ -108,7 +108,7 @@
 def finish_kernel(pieces, more, cols_ref, gain_ref, head_hbm, extra_hbm, *refs):
     piece_refs, (resid_hbm, normed_hbm, source, parts, extra, resid, normed, in_sems, out_sems) = refs[:pieces], refs[pieces:]
     rows, width = resid.shape
-    part = TAIL_ROWS // (pieces // 2)
+    part = TAIL_ROWS // (pieces // 3)
     known = HEAD_ROWS + TAIL_ROWS
     normalizer = jnp.asarray(math.sqrt(width), dtype=jnp.bfloat16)
     one = jnp.ones((), jnp.bfloat16)
@@ -117,53 +117,53 @@
     extra_copy = pltpu.make_async_copy(extra_hbm, extra, in_sems.at[pieces + 1])
     copies = []
     for index, ref in enumerate(piece_refs):
-        there = source.at[pl.ds(HEAD_ROWS + index // 2 * part, part), :] if index % 2 == 0 else parts.at[index // 2]
-        copies.append(pltpu.make_async_copy(ref, there, in_sems.at[index]))
+        there = source.at[pl.ds(HEAD_ROWS + index // 3 * part, part), :] if index % 3 == 0 else parts.at[index // 3, index % 3 - 1]
+        copies.append(pltpu.make_async_copy(ref.at[pl.ds(0, part), :], there, in_sems.at[index]))
+    head_copy.start()
+    extra_copy.start()
     for copy in copies:
         copy.start()
-    head_copy.start()
-    extra_copy.start()
-    for index in range(pieces // 2):
-        copies[2 * index].wait()
-        copies[2 * index + 1].wait()
+    for copy in copies:
+        copy.wait()
+    for index in range(pieces // 3):
         span = pl.ds(HEAD_ROWS + index * part, part)
-        source[span, :] = source[span, :] + parts[index]
+        source[span, :] = source[span, :] + parts[index, 0] + parts[index, 1]
     head_copy.wait()
     extra_copy.wait()
 
     def results(block):
-        span = pl.ds(pl.multiple_of(block * 256, 256), 256)
+        span = pl.ds(pl.multiple_of(block * 512, 512), 512)
         return (pltpu.make_async_copy(resid.at[span, :], resid_hbm.at[span, :], out_sems.at[0]),
                 pltpu.make_async_copy(normed.at[span, :], normed_hbm.at[span, :], out_sems.at[1]))
 
-    @pl.loop(0, rows // 256)
+    @pl.loop(0, rows // 512)
     def _(block):
-        span = pl.ds(pl.multiple_of(block * 256, 256), 256)
-        lanes = lax.broadcasted_iota(jnp.int32, (256, known), 1)
+        span = pl.ds(pl.multiple_of(block * 512, 512), 512)
+        lanes = lax.broadcasted_iota(jnp.int32, (512, known), 1)
         value = jnp.where(lax.broadcasted_iota(jnp.int32, (1, known), 1) < HEAD_ROWS, normalizer, one)
-        select = jnp.where(lanes == cols_ref[span, :], jnp.broadcast_to(value, (256, known)), zero)
+        select = jnp.where(lanes == cols_ref[span, :], jnp.broadcast_to(value, (512, known)), zero)
         for piece in range(width // 256):
             cols = pl.ds(piece * 256, 256)
             resid[span, cols] = jnp.dot(select, source[:, cols], preferred_element_type=jnp.float32).astype(jnp.bfloat16)
 
         @pl.when(more[0] > 0)
         def _():
-            places = lax.broadcasted_iota(jnp.int32, (256, extra.shape[0]), 1) + known
+            places = lax.broadcasted_iota(jnp.int32, (512, extra.shape[0]), 1) + known
             from_extra = jnp.where(places == cols_ref[span, :], one, zero)
             for piece in range(width // 256):
                 cols = pl.ds(piece * 256, 256)
                 picked = jnp.dot(from_extra, extra[:, cols], preferred_element_type=jnp.float32)
                 resid[span, cols] = (resid[span, cols].astype(jnp.float32) + picked).astype(jnp.bfloat16)
 
-        for quarter in range(4):
-            rows_here = pl.ds(pl.multiple_of(block * 256 + quarter * 64, 64), 64)
+        for quarter in range(8):
+            rows_here = pl.ds(pl.multiple_of(block * 512 + quarter * 64, 64), 64)
             widened = resid[rows_here, :].astype(jnp.float32)
             inv_rms = lax.rsqrt(jnp.mean(widened * widened, axis=-1, keepdims=True) + EPSILON)
             normed[rows_here, :] = (widened * inv_rms * gain_ref[...]).astype(jnp.bfloat16)
         for result in results(block):
             result.start()
 
-    @pl.loop(0, rows // 256)
+    @pl.loop(0, rows // 512)
     def _(block):
         for result in results(block):
             result.wait()
@@ -183,19 +183,19 @@
         out_specs=(hbm, hbm),
         scratch_shapes=[
             pltpu.VMEM((HEAD_ROWS + TAIL_ROWS, width), jnp.bfloat16),
-            pltpu.VMEM((len(pieces) // 2,) + pieces[0].shape, jnp.bfloat16),
+            pltpu.VMEM((len(pieces) // 3, 2) + pieces[0].shape, jnp.bfloat16),
             pltpu.VMEM(extra.shape, jnp.bfloat16),
             pltpu.VMEM((rows, width), jnp.bfloat16),
             pltpu.VMEM((rows, width), jnp.bfloat16),
             dma((len(pieces) + 2,)), dma((2,)),
         ],
-        compiler_params=pltpu.CompilerParams(vmem_limit_bytes=40 * 1024 * 1024),
+        compiler_params=pltpu.CompilerParams(vmem_limit_bytes=67_043_328),
         cost_estimate=pl.CostEstimate(flops=2 * rows * width * (HEAD_ROWS + TAIL_ROWS), bytes_accessed=16_000_000, transcendentals=0),
         name="finish_rows",
     )(more, cols, gain, head, extra, *pieces)
 
 
-def heads_kernel(rows, normed_hbm, cos_ref, sin_ref, wq_hbm, wk_hbm, wv_hbm, q_out, kv_out,
+def heads_kernel(rows, normed_hbm, cos_ref, sin_ref, wq_hbm, wk_hbm, wv_hbm, q_out, k_out, v_out,
                  wq, wk, wv, normed, q_stage, kv_stage, w_sem, q_send, q_recv, kv_send, kv_recv,
                  own_recv, fwd_send, fwd_recv, keep_sem):
     group = lax.axis_index("dp")
@@ -203,6 +203,7 @@
     core = lax.rem(me, 2)
     chip = me // 2
     partner = me + 1 - 2 * core
+    kv_outs = (k_out, v_out)
     tiles = rows // SEND_ROWS
     half = HEAD_DIM // 2
 
@@ -258,26 +259,39 @@
         @pl.when(offset != 0)
         def _():
             for side in range(2):
-                remote(kv_stage.at[side, there, sent, :], kv_out.at[side, block(me, tile), :], kv_send.at[offset, side], kv_recv.at[offset, core, tile], 2 * there + side).start()
+                remote(kv_stage.at[side, there, sent, :], kv_outs[side].at[block(me, tile), :], kv_send.at[offset, side], kv_recv.at[offset, core, tile], 2 * there + side).start()
             for side in range(2):
                 remote(q_stage.at[2 * there + side, sent, :], q_out.at[block(me, tile), :], q_send.at[offset, side], q_recv.at[offset, core], 2 * there + side).start()
 
     for side in range(2):
-        remote(kv_stage.at[side, chip], kv_out.at[side, whole(me), :], kv_send.at[0, side], own_recv.at[side], partner).start()
+        remote(kv_stage.at[side, chip], kv_outs[side].at[whole(me), :], kv_send.at[0, side], own_recv.at[side], partner).start()
     remote(q_stage.at[partner], q_out.at[whole(me), :], q_send.at[0, 0], q_recv.at[0, 0], partner).start()
     keeps = [pltpu.make_async_copy(q_stage.at[me], q_out.at[whole(me), :], keep_sem.at[0])]
     for side in range(2):
-        keeps.append(pltpu.make_async_copy(kv_stage.at[side, chip], kv_out.at[side, whole(me), :], keep_sem.at[1 + side]))
+        keeps.append(pltpu.make_async_copy(kv_stage.at[side, chip], kv_outs[side].at[whole(me), :], keep_sem.at[1 + side]))
     for keep in keeps:
         keep.start()
 
-    for tile in range(tiles):
+    def forward(mine_out, other_out):
+        for tile in range(tiles):
+            for offset in range(1, CHIPS):
+                for side in range(2):
+                    source = 2 * lax.rem(chip + CHIPS - offset, CHIPS) + side
+                    region = mine_out.at[block(source, tile), :]
+                    remote(region, region, kv_send.at[offset, side], kv_recv.at[offset, side, tile], partner).wait_recv()
+                    remote(region, region, fwd_send.at[offset, side], fwd_recv.at[offset, side], partner).start()
         for offset in range(1, CHIPS):
             for side in range(2):
                 source = 2 * lax.rem(chip + CHIPS - offset, CHIPS) + side
-                region = kv_out.at[core, block(source, tile), :]
-                remote(region, region, kv_send.at[offset, side], kv_recv.at[offset, side, tile], partner).wait_recv()
-                remote(region, region, fwd_send.at[offset, side], fwd_recv.at[offset, side], partner).start()
+                mine = mine_out.at[whole(source), :]
+                remote(mine, mine, fwd_send.at[offset, side], fwd_recv.at[offset, side], partner).wait_send()
+                other = other_out.at[whole(source), :]
+                remote(other, other, fwd_send.at[offset, side], fwd_recv.at[offset, side], partner).wait_recv()
+
+    for kind in range(2):
+        @pl.when(core == kind)
+        def _():
+            forward(kv_outs[kind], kv_outs[1 - kind])
 
     for keep in keeps:
         keep.wait()
@@ -285,14 +299,10 @@
         there = lax.rem(chip + offset, CHIPS)
         for side in range(2):
             source = 2 * lax.rem(chip + CHIPS - offset, CHIPS) + side
-            remote(kv_stage.at[side, there], kv_out.at[side, whole(me), :], kv_send.at[offset, side], own_recv.at[side], partner).wait_send()
+            remote(kv_stage.at[side, there], kv_outs[side].at[whole(me), :], kv_send.at[offset, side], own_recv.at[side], partner).wait_send()
             remote(q_stage.at[2 * there + side], q_out.at[whole(source), :], q_send.at[offset, side], q_recv.at[offset, side], partner).wait()
-            mine = kv_out.at[core, whole(source), :]
-            remote(mine, mine, fwd_send.at[offset, side], fwd_recv.at[offset, side], partner).wait_send()
-            other = kv_out.at[1 - core, whole(source), :]
-            remote(other, other, fwd_send.at[offset, side], fwd_recv.at[offset, side], partner).wait_recv()
     for side in range(2):
-        remote(kv_stage.at[side, chip], kv_out.at[side, whole(partner), :], kv_send.at[0, side], own_recv.at[side], partner).wait()
+        remote(kv_stage.at[side, chip], kv_outs[side].at[whole(partner), :], kv_send.at[0, side], own_recv.at[side], partner).wait()
     remote(q_stage.at[partner], q_out.at[whole(partner), :], q_send.at[0, 0], q_recv.at[0, 0], partner).wait()
 
 
@@ -306,9 +316,9 @@
     dma = pltpu.SemaphoreType.DMA
     return pl.pallas_call(
         functools.partial(heads_kernel, rows),
-        out_shape=(jax.ShapeDtypeStruct((tokens, HEAD_DIM), jnp.bfloat16), jax.ShapeDtypeStruct((2, tokens, HEAD_DIM), jnp.bfloat16)),
+        out_shape=(jax.ShapeDtypeStruct((tokens, HEAD_DIM), jnp.bfloat16),) * 3,
         in_specs=[anywhere, vmem, vmem, anywhere, anywhere, anywhere],
-        out_specs=(anywhere, anywhere),
+        out_specs=(anywhere,) * 3,
         scratch_shapes=[
             pltpu.VMEM(wq_all.shape, jnp.bfloat16),
             pltpu.VMEM(w_key.shape, jnp.bfloat16),
@@ -323,7 +333,7 @@
             dma((CHIPS, 2)), dma((CHIPS, 2)),
             dma((3,)),
         ],
-        compiler_params=pltpu.CompilerParams(collective_id=0, has_side_effects=True, vmem_limit_bytes=56 * 1024 * 1024),
+        compiler_params=pltpu.CompilerParams(collective_id=0, has_side_effects=True, vmem_limit_bytes=67_043_328),
         cost_estimate=pl.CostEstimate(flops=2 * rows * width * 4096, bytes_accessed=40_000_000, transcendentals=0),
         name="project_heads",
     )(normed, cosines, sines, wq_all, w_key, w_value)
@@ -406,28 +416,29 @@
         def gather(chunk, side, after):
             return gather_rows((2 * chunk + side) * call_rows, call_rows, pair_ids, counts, cols, table_rows, after)
 
-        pieces, sums = [], []
+        pieces = []
         after, late, late_next = [], [], []
         for chunk in range(CHUNKS):
-            other = gather(chunk, 1, after + late + ([wq_all] if chunk == 1 else []))
+            other = gather(chunk, 1, after + late)
             got = exchange(other, 1)
-            mine = gather(chunk, 0, [other])
+            mine = gather(chunk, 0, [other] + ([wq_all] if chunk == CHUNKS - 1 else []))
             after, late = [], late_next
             late_next = []
+            spans = []
+            for part in range(2):
+                first_row = part * 4 * half
+                spans += [slice(first_row, first_row + half), slice(first_row + half, first_row + 2 * half), slice(first_row + 2 * half, first_row + 4 * half)]
+            both = lax.optimization_barrier([mine[span] + got[span] for span in spans])
             for part, bits in ((0, (2, 4)), (1, (4, 2))):
-                base = part * 4 * half
-                keep = [slice(base + k * half, base + (k + 1) * half) for k in range(4)]
-                far = slice(base + 2 * half, base + 4 * half)
-                sent = mine[far] + got[far]
+                kept, near, sent = both[3 * part:3 * part + 3]
                 back = exchange(sent, bits[0])
-                near_send = mine[keep[1]] + got[keep[1]] + back[half:]
+                near_send = near + back[half:]
                 back2 = exchange(near_send, bits[1])
                 after.append(sent)
-                sums.append(sent)
                 late_next.append(near_send)
-                pieces += [mine[keep[0]] + got[keep[0]] + back[:half], back2]
-
-        head = share_head_back(*head_halves, pieces[2])
+                pieces += [kept, back, back2]
+
+        head = share_head_back(*head_halves, pieces[5])
 
         def second_exchange(rows):
             ids = ranked_ids(TAIL_ROWS, extra_rows).reshape(-1)
@@ -439,17 +450,17 @@
         def no_exchange(rows):
             return jnp.zeros((extra_rows, model_width), jnp.bfloat16)
 
-        over, _ = lax.optimization_barrier((over, sums[2]))
+        over, _ = lax.optimization_barrier((over, pieces[2]))
         more = lax.pmax(over, "dp")
-        asked, _ = lax.optimization_barrier((more, pieces[-5]))
+        asked, _ = lax.optimization_barrier((more, pieces[5]))
         extra = lax.cond(asked > 0, second_exchange, no_exchange, table_rows)
         places = jnp.where(in_tail, HEAD_ROWS + ranks, blocks)
         own_places = lax.dynamic_index_in_dim(places, dev_index, 0, keepdims=False)
         residual, normed = finish_rows(more.reshape(1), own_places[:, None], (1.0 + norm_scale)[None, :], head, extra, pieces)
         own = lax.dynamic_slice_in_dim(positions, dev_index * block_rows, block_rows)
         cosines, sines = rope_tables(own)
-        queries, keys_values = project_heads(normed, cosines, sines, wq_all, w_key, w_value)
-        return residual, queries[:, None, :], keys_values[0][:, None, :], keys_values[1][:, None, :]
+        outs = project_heads(normed, cosines, sines, wq_all, w_key, w_value)
+        return (residual,) + tuple(out[:, None, :] for out in outs)
 
     head_spec = P("dp", "tp", None)
     return jax.shard_map(local_body, mesh=mesh, in_specs=(P("dp"), P("dp"), P("tp", None), P(), P(None, "tp"), P(), P()), out_specs=(P(("dp", "tp"), None), head_spec, head_spec, head_spec), check_vma=False)

time: 363 us -> 388 us (1.069)
  waiting for transfers between devices: 43.6 us -> 68.3 us
  starting transfers between devices: 67.9 us -> 62.2 us
  other arithmetic: 38.3 us -> 43.8 us
    ppermute x10, waiting for transfers between devices: 30.9 us -> 56 us  [exchange(): return lax.ppermute(rows, 'tp', [(i, i ^ bit) for i in range(group_size)])]
    another operation x2 -> x1, local copies, waits for them, and re-layouts: 8.01 us -> 1.41 us  [the longest x1 6.6 us: local_body(): keys_values[1][:, None, :]]
    ppermute x10, starting transfers between devices: 49.8 us -> 44.2 us  [exchange(): return lax.ppermute(rows, 'tp', [(i, i ^ bit) for i in range(group_size)])]
    add x4 -> x8, other arithmetic: 17.4 us -> 21.4 us  [the longest x4 15.3 us: local_body(): both = lax.optimization_barrier([mine[span] + got[span] for span in spans])]
  transfers between devices with their start and end apart: 18 -> 18, of which waited for: 7 -> 7; matrix products, arithmetic and copies ran while one was open for 13% -> 14% of each run, Pallas kernels for 14% -> 13%
where the time goes in v4:
time: 388 us; the launch traced here: 381 us
  Pallas kernels  163 us (42%)
  waiting for transfers between devices  68.3 us (18%)
  starting transfers between devices  62.2 us (16%)
  other arithmetic  43.8 us (11%)
  local copies, waits for them, and re-layouts  21.7 us (6%)
  between operations  15.8 us (4%)
  blocking collectives  4.84 us (1%)
    pallas_call x1, Pallas kernels, project_heads(): pl.pallas_call(functools.partial(heads_kernel, rows), out_shape=(jax.Shap...  97.2 us
    ppermute x10, waiting for transfers between devices, exchange(): return lax.ppermute(rows, 'tp', [(i, i ^ bit) for i in range(group_size)])  56 us
    pallas_call x4, Pallas kernels, gather_rows(): pl.pallas_call(functools.partial(gather_kernel, base, tiles, width), grid...  48.5 us
    ppermute x10, starting transfers between devices, exchange(): return lax.ppermute(rows, 'tp', [(i, i ^ bit) for i in range(group_size)])  44.2 us
    pallas_call x1, Pallas kernels, finish_rows(): pl.pallas_call(functools.partial(finish_kernel, len(pieces)), out_shape=(...  17 us
    add x4, other arithmetic, local_body(): both = lax.optimization_barrier([mine[span] + got[span] for span in spans])  15.3 us
    unnamed x46, local copies, waits for them, and re-layouts  15.2 us
    ppermute x6, starting transfers between devices, pass_head(): got = lax.ppermute(values, 'tp', pairs)  15.1 us
  transfers between devices with their start and end apart: 18, of which 7 were waited for; matrix products, arithmetic and copies ran while one was open for 14% of the time, Pallas kernels for 13%

profile of v4, /device:TPU:0, one launch (start us, length us, event | category | flops | bytes accessed | tf_op | source)
XLA Modules:
  0.0 381.1 jit_solution(10162859570828366181)
XLA Ops:
  7.9 3.1 fusion.13
  11.0 5.2 %collective-permute-start.3 = (bf16[320,2304]{1,0:T(8,128)(2,1)}, bf16[320,2304]{1,0:T(8,128)(2,1)S(1)}, u32[]{:S(2)}, u32[]{:S(2)}) collective-permute-start(bf16[320,2304]{1,0:T(8,128)(2,1)} %get-tuple-element.65), channel_id=1, source_target_pairs={{0,2},{8,10}} | collective-permute-start | bytes 4423688 | tf_op jit(solution)/shard_map/ppermute | solution.py:349
  16.2 2.5 collective-permute-start.8
  20.7 3.0 select_reduce_fusion.1
  24.2 1.4 fusion.9
  25.7 2.6 select_reduce_fusion.2
  28.3 12.6 %gather_rows.4.rest_0_ = bf16[1280,2304]{1,0:T(8,128)(2,1)} custom-call(s32[5120]{0:T(1024)} %bitcast.35, s32[40]{0:T(128)} %get-tuple-element.83.counts, f32[40,1,128]{2,1,0:T(1,128)} %bitcast.39, bf16[32000,2304]{1,0:T(8,128)(2,1)} %table_ref.7), custom_call_target="tpu_custom_call" | custom-call | flops 25600000000 | bytes 17694720 | tf_op jit(solution)/shard_map/gather_rows/pallas_call | solution.py:98
  40.9 9.3 %collective-permute-done.3 = bf16[320,2304]{1,0:T(8,128)(2,1)S(1)} collective-permute-done((bf16[320,2304]{1,0:T(8,128)(2,1)}, bf16[320,2304]{1,0:T(8,128)(2,1)S(1)}, u32[]{:S(2)}, u32[]{:S(2)}) %collective-permute-start.3) | collective-permute-done | bytes 1474592 | tf_op jit(solution)/shard_map/ppermute | solution.py:349
  51.4 2.4 collective-permute-done.8
  53.7 2.1 broadcast_select_fusion.2
  55.8 1.9 collective-permute-start.4
  57.7 1.8 collective-permute-start.9
  59.5 12.6 %gather_rows.5 = bf16[1280,2304]{1,0:T(8,128)(2,1)} custom-call(s32[5120]{0:T(1024)} %bitcast.36, s32[40]{0:T(128)} %get-tuple-element.83.counts, f32[40,1,128]{2,1,0:T(1,128)} %bitcast.40, bf16[32000,2304]{1,0:T(8,128)(2,1)} %table_ref.7, bf16[1280,2304]{1,0:T(8,128)(2,1)} %gather_rows.4.rest_0_), custom_call_target="tpu_custom_call" | custom-call | flops 25600000000 | bytes 17694720 | tf_op jit(solution)/shard_map/gather_rows/pallas_call | solution.py:98
  72.2 1.3 broadcast_select_fusion.4
  73.4 2.0 collective-permute-start.5
  75.6 1.8 collective-permute-start.10
  77.4 3.5 slice_add_fusion.12
  80.9 3.4 slice_add_fusion.2
  84.3 11.0 %collective-permute-start.6 = (bf16[320,2304]{1,0:T(8,128)(2,1)S(1)}, bf16[320,2304]{1,0:T(8,128)(2,1)}, u32[]{:S(2)}, u32[]{:S(2)}) collective-permute-start(bf16[320,2304]{1,0:T(8,128)(2,1)S(1)} %get-tuple-element.44.rest_1_), channel_id=1, source_target_pairs={{0,4},{1,5},{2,6},{3,7},{4,0},{5,1},{6,2},{7,3},{8,12},{9,13},{10,... | collective-permute-start | bytes 4423688 | tf_op jit(solution)/shard_map/ppermute | solution.py:346
  95.3 11.6 %gather_rows.6.rest_0_ = bf16[1280,2304]{1,0:T(8,128)(2,1)} custom-call(s32[5120]{0:T(1024)} %bitcast.37, s32[40]{0:T(128)} %get-tuple-element.83.counts, f32[40,1,128]{2,1,0:T(1,128)} %bitcast.41, bf16[32000,2304]{1,0:T(8,128)(2,1)} %table_ref.7, bf16[320,2304]{1,0:T(8,128)(2,1)} %get-tuple-element.41.rest_0_, bf16[320,2304]{1,0:T(8,128)(2,1)} %copy-done.2), custom_call_target="tpu_custom_call" | custom-call | flops 25600000000 | bytes 17694720 | tf_op jit(solution)/shard_map/gather_rows/pallas_call | solution.py:98
  107.0 5.7 %collective-permute-done.6.refs_4_ = bf16[320,2304]{1,0:T(8,128)(2,1)} collective-permute-done((bf16[320,2304]{1,0:T(8,128)(2,1)S(1)}, bf16[320,2304]{1,0:T(8,128)(2,1)}, u32[]{:S(2)}, u32[]{:S(2)}) %collective-permute-start.6) | collective-permute-done | bytes 1474592 | tf_op jit(solution)/shard_map/ppermute | solution.py:346
  112.8 1.4 slice_add_fusion.10
  114.2 30.9 %collective-permute-start.7 = (bf16[160,2304]{1,0:T(8,128)(2,1)S(1)}, bf16[160,2304]{1,0:T(8,128)(2,1)S(1)}, u32[]{:S(2)}, u32[]{:S(2)}) collective-permute-start(bf16[160,2304]{1,0:T(8,128)(2,1)S(1)} %slice_add_fusion.10), channel_id=1, source_target_pairs={{0,2},{1,3},{2,0},{3,1},{4,6},{5,7},{6,4},{7,5},{8,10},{9,11},{10,... | collective-permute-start | bytes 2211848 | tf_op jit(solution)/shard_map/ppermute | solution.py:346
  145.2 17.2 %collective-permute-done.7.refs_5_ = bf16[160,2304]{1,0:T(8,128)(2,1)S(1)} collective-permute-done((bf16[160,2304]{1,0:T(8,128)(2,1)S(1)}, bf16[160,2304]{1,0:T(8,128)(2,1)S(1)}, u32[]{:S(2)}, u32[]{:S(2)}) %collective-permute-start.7) | collective-permute-done | bytes 737312 | tf_op jit(solution)/shard_map/ppermute | solution.py:346
  163.2 1.5 broadcast_select_fusion.6
  164.8 1.5 broadcast_select_fusion.1
  166.3 1.8 pad_maximum_fusion
  168.1 2.9 collective-permute-start.11
  171.0 11.6 %gather_rows.7 = bf16[1280,2304]{1,0:T(8,128)(2,1)} custom-call(s32[5120]{0:T(1024)} %bitcast.38, s32[40]{0:T(128)} %get-tuple-element.83.counts, f32[40,1,128]{2,1,0:T(1,128)} %bitcast.42, bf16[32000,2304]{1,0:T(8,128)(2,1)} %table_ref.7, bf16[1280,2304]{1,0:T(8,128)(2,1)} %gather_rows.6.rest_0_, bf16[8,2304,256]{2,1,0:T(8,128)(2,1)} %bitcast.30), custom_call_target="tpu_custom_call" | custom-call | flops 25600000000 | bytes 17694720 | tf_op jit(solution)/shard_map/gather_rows/pallas_call | solution.py:98
  182.6 4.4 %slice_add_fusion.6 = (bf16[160,2304]{1,0:T(8,128)(2,1)}, bf16[160,2304]{1,0:T(8,128)(2,1)}, bf16[160,2304]{1,0:T(8,128)(2,1)}, bf16[160,2304]{1,0:T(8,128)(2,1)}) fusion(bf16[1280,2304]{1,0:T(8,128)(2,1)} %collective-permute-done.12, bf16[1280,2304]{1,0:T(8,128)(2,1)} %gather_rows.7), kind=kLoop, calls=%fused_computation.37 | loop fusion | flops 1474560 | bytes 8847360 | tf_op jit(solution)/shard_map/add | solution.py:431
  188.1 3.9 %slice_add_fusion = (bf16[320,2304]{1,0:T(8,128)(2,1)}, bf16[320,2304]{1,0:T(8,128)(2,1)}) fusion(bf16[1280,2304]{1,0:T(8,128)(2,1)} %collective-permute-done.12, bf16[1280,2304]{1,0:T(8,128)(2,1)S(1)} %copy-done), kind=kLoop, calls=%fused_computation.19 | loop fusion | flops 1474560 | bytes 8847360 | tf_op jit(solution)/shard_map/add | solution.py:431
  192.1 2.1 slice_add_fusion.11
  194.1 2.0 collective-permute-start.2
  200.6 3.0 multiply_sine_fusion
  203.7 23.9 %collective-permute-done.2.refs_2_ = bf16[160,2304]{1,0:T(8,128)(2,1)} collective-permute-done((bf16[160,2304]{1,0:T(8,128)(2,1)}, bf16[160,2304]{1,0:T(8,128)(2,1)}, u32[]{:S(2)}, u32[]{:S(2)}) %collective-permute-start.2) | collective-permute-done | bytes 737312 | tf_op jit(solution)/shard_map/ppermute | solution.py:346
  227.5 4.8 %pmax.7 = s32[]{:T(128)} all-reduce(s32[]{:T(128)S(6)} %convert_element_type.29), channel_id=1, replica_groups=mesh['dp'=2,'tp'=8] {'dp'}, use_global_device_ids=true, to_apply=%region_5.6 | all-reduce | flops 1 | bytes 8 | tf_op jit(solution)/shard_map/pmax | solution.py:454
  233.1 1.4 conditional.1
  233.1 1.4 broadcast.217
  234.5 1.5 slice_add_fusion.4
  237.3 2.3 broadcast_select_fusion.head_hbm
  239.6 7.9 %collective-permute-done.16.refs_11_ = bf16[160,2304]{1,0:T(8,128)(2,1)S(1)} collective-permute-done((bf16[160,2304]{1,0:T(8,128)(2,1)S(1)}, bf16[160,2304]{1,0:T(8,128)(2,1)S(1)}, u32[]{:S(2)}, u32[]{:S(2)}) %collective-permute-start.16) | collective-permute-done | bytes 737312 | tf_op jit(solution)/shard_map/ppermute | solution.py:346
  247.5 1.3 collective-permute-done.14.refs_8_
  249.6 17.0 %finish_rows.1 = (bf16[1024,2304]{1,0:T(8,128)(2,1)}, bf16[1024,2304]{1,0:T(8,128)(2,1)}) custom-call(s32[1]{0:T(128)} %bitcast.6.more, s32[1024,1]{1,0:T(8,128)} %copy.17.cols_ref, f32[1,2304]{1,0:T(1,128)} %broadcast_in_dim.95.gain_ref, bf16[640,2304]{1,0:T(8,128)(2,1)} %broadcast_select_fusion.head_hbm, bf16[384,2304]{1,0:T(8,128)(2,1)} %get-tuple-element.96.extra_hbm, ...), custom_call_target="tpu_custom_call" | custom-call | flops 6039797760 | bytes 16000000 | tf_op jit(solution)/shard_map/finish_rows/pallas_call | solution.py:179
  266.7 97.2 %project_heads.1 = (bf16[8192,256]{1,0:T(8,128)(2,1)}, bf16[8192,256]{1,0:T(8,128)(2,1)}, bf16[8192,256]{1,0:T(8,128)(2,1)}) custom-call(bf16[1024,2304]{1,0:T(8,128)(2,1)} %get-tuple-element.57.normed_hbm, f32[1024,128]{1,0:T(8,128)} %get-tuple-element.86.cos_ref, f32[1024,128]{1,0:T(8,128)} %get-tuple-element.85.sin_ref, bf16[8,2304,256]{2,1,0:T(8,128)(2,1)} %bitcast.31, ...), custom_call_target="tpu_custom_call" | custom-call | flops 19327352832 | bytes 40000000 | tf_op jit(solution)/shard_map/project_heads/pallas_call | solution.py:317
  363.9 4.6 %copy.28 = bf16[8192,1,256]{2,0,1:T(8,128)(2,1)} copy(bf16[8192,1,256]{2,0,1:T(8,128)(2,1)} %bitcast.34) | data formatting | bytes 8388608
  368.5 2.1 copy.29
  370.6 1.6 copy-done.4
  372.2 2.0 copy.30
  (87 shorter events, 12.5 us)
Async XLA Ops:
  7.2 163.8 %all-gather.3.cloned.1.call-start = ((), (), s32[]{:S(2)}) async-start(), calls=%async_computation.2 | async-start | bytes 10616832 | tf_op jit(solution)/shard_map/all_gather | solution.py:372
  7.9 10.8 %copy-start.12 = (s32[8192]{0:T(1024)S(1)}, s32[8192]{0:T(1024)}, u32[]{:S(2)}) copy-start(s32[8192]{0:T(1024)} %param.9) | copy-start | bytes 98308
  11.0 39.2 %collective-permute-start.3 = (bf16[320,2304]{1,0:T(8,128)(2,1)}, bf16[320,2304]{1,0:T(8,128)(2,1)S(1)}, u32[]{:S(2)}, u32[]{:S(2)}) collective-permute-start(bf16[320,2304]{1,0:T(8,128)(2,1)} %get-tuple-element.65), channel_id=1, source_target_pairs={{0,2},{8,10}} | collective-permute-start | bytes 4423688 | tf_op jit(solution)/shard_map/ppermute | solution.py:349
  16.2 37.5 %collective-permute-start.8 = (bf16[320,2304]{1,0:T(8,128)(2,1)S(1)}, bf16[320,2304]{1,0:T(8,128)(2,1)}, u32[]{:S(2)}, u32[]{:S(2)}) collective-permute-start(bf16[320,2304]{1,0:T(8,128)(2,1)S(1)} %get-tuple-element.66), channel_id=1, source_target_pairs={{0,4},{8,12}} | collective-permute-start | bytes 4423688 | tf_op jit(solution)/shard_map/ppermute | solution.py:349
  18.8 22.1 %copy-start.11 = (s32[8,1024]{1,0:T(8,128)}, s32[8,1024]{1,0:T(8,128)S(1)}, u32[]{:S(2)}) copy-start(s32[8,1024]{1,0:T(8,128)S(1)} %reshape.139) | copy-start | bytes 98308
  19.5 0.6 copy-start.14
  20.1 0.6 copy-start.9
  40.9 36.5 %collective-permute-start = (bf16[1280,2304]{1,0:T(8,128)(2,1)}, bf16[1280,2304]{1,0:T(8,128)(2,1)}, u32[]{:S(2)}, u32[]{:S(2)}) collective-permute-start(bf16[1280,2304]{1,0:T(8,128)(2,1)} %gather_rows.4.rest_0_), channel_id=1, source_target_pairs={{0,1},{1,0},{2,3},{3,2},{4,5},{5,4},{6,7},{7,6},{8,9},{9,8},{10,11... | collective-permute-start | bytes 17694728 | tf_op jit(solution)/shard_map/ppermute | solution.py:346
  50.3 1.1 copy-start.8
  55.8 16.3 %collective-permute-start.4 = (bf16[320,2304]{1,0:T(8,128)(2,1)S(1)}, bf16[320,2304]{1,0:T(8,128)(2,1)}, u32[]{:S(2)}, u32[]{:S(2)}) collective-permute-start(bf16[320,2304]{1,0:T(8,128)(2,1)S(1)} %get-tuple-element.63), channel_id=1, source_target_pairs={{2,6},{10,14}} | collective-permute-start | bytes 4423688 | tf_op jit(solution)/shard_map/ppermute | solution.py:349
  57.7 17.7 %collective-permute-start.9 = (bf16[320,2304]{1,0:T(8,128)(2,1)S(1)}, bf16[320,2304]{1,0:T(8,128)(2,1)}, u32[]{:S(2)}, u32[]{:S(2)}) collective-permute-start(bf16[320,2304]{1,0:T(8,128)(2,1)S(1)} %get-tuple-element.64), channel_id=1, source_target_pairs={{4,6},{12,14}} | collective-permute-start | bytes 4423688 | tf_op jit(solution)/shard_map/ppermute | solution.py:349
  72.1 5.2 %copy-start.1 = (bf16[1280,2304]{1,0:T(8,128)(2,1)S(1)}, bf16[1280,2304]{1,0:T(8,128)(2,1)}, u32[]{:S(2)}) copy-start(bf16[1280,2304]{1,0:T(8,128)(2,1)} %gather_rows.5) | copy-start | bytes 17694724
  73.4 71.7 %collective-permute-start.5 = (bf16[320,2304]{1,0:T(8,128)(2,1)}, bf16[320,2304]{1,0:T(8,128)(2,1)}, u32[]{:S(2)}, u32[]{:S(2)}) collective-permute-start(bf16[320,2304]{1,0:T(8,128)(2,1)} %broadcast_select_fusion.4), channel_id=1, source_target_pairs={{6,4},{14,12}} | collective-permute-start | bytes 4423688 | tf_op jit(solution)/shard_map/ppermute | solution.py:349
  75.6 5.3 %copy-start.3 = (bf16[320,2304]{1,0:T(8,128)(2,1)}, bf16[320,2304]{1,0:T(8,128)(2,1)S(1)}, u32[]{:S(2)}) copy-start(bf16[320,2304]{1,0:T(8,128)(2,1)S(1)} %broadcast_select_fusion.3) | copy-start | bytes 4423684
  75.6 87.6 %collective-permute-start.10 = (bf16[320,2304]{1,0:T(8,128)(2,1)S(1)}, bf16[320,2304]{1,0:T(8,128)(2,1)}, u32[]{:S(2)}, u32[]{:S(2)}) collective-permute-start(bf16[320,2304]{1,0:T(8,128)(2,1)S(1)} %broadcast_select_fusion.3), channel_id=1, source_target_pairs={{6,2},{14,10}} | collective-permute-start | bytes 4423688 | tf_op jit(solution)/shard_map/ppermute | solution.py:349
  84.3 11.0 %copy-start.2 = (bf16[320,2304]{1,0:T(8,128)(2,1)}, bf16[320,2304]{1,0:T(8,128)(2,1)S(1)}, u32[]{:S(2)}) copy-start(bf16[320,2304]{1,0:T(8,128)(2,1)S(1)} %get-tuple-element.44.rest_1_) | copy-start | bytes 4423684
  84.3 28.4 %collective-permute-start.6 = (bf16[320,2304]{1,0:T(8,128)(2,1)S(1)}, bf16[320,2304]{1,0:T(8,128)(2,1)}, u32[]{:S(2)}, u32[]{:S(2)}) collective-permute-start(bf16[320,2304]{1,0:T(8,128)(2,1)S(1)} %get-tuple-element.44.rest_1_), channel_id=1, source_target_pairs={{0,4},{1,5},{2,6},{3,7},{4,0},{5,1},{6,2},{7,3},{8,12},{9,13},{10,... | collective-permute-start | bytes 4423688 | tf_op jit(solution)/shard_map/ppermute | solution.py:346
  107.0 75.7 %collective-permute-start.12 = (bf16[1280,2304]{1,0:T(8,128)(2,1)}, bf16[1280,2304]{1,0:T(8,128)(2,1)}, u32[]{:S(2)}, u32[]{:S(2)}) collective-permute-start(bf16[1280,2304]{1,0:T(8,128)(2,1)} %gather_rows.6.rest_0_), channel_id=1, source_target_pairs={{0,1},{1,0},{2,3},{3,2},{4,5},{5,4},{6,7},{7,6},{8,9},{9,8},{10,11... | collective-permute-start | bytes 17694728 | tf_op jit(solution)/shard_map/ppermute | solution.py:346
  114.2 48.2 %collective-permute-start.7 = (bf16[160,2304]{1,0:T(8,128)(2,1)S(1)}, bf16[160,2304]{1,0:T(8,128)(2,1)S(1)}, u32[]{:S(2)}, u32[]{:S(2)}) collective-permute-start(bf16[160,2304]{1,0:T(8,128)(2,1)S(1)} %slice_add_fusion.10), channel_id=1, source_target_pairs={{0,2},{1,3},{2,0},{3,1},{4,6},{5,7},{6,4},{7,5},{8,10},{9,11},{10,... | collective-permute-start | bytes 2211848 | tf_op jit(solution)/shard_map/ppermute | solution.py:346
  145.1 47.0 %collective-permute-start.1 = (bf16[320,2304]{1,0:T(8,128)(2,1)}, bf16[320,2304]{1,0:T(8,128)(2,1)}, u32[]{:S(2)}, u32[]{:S(2)}) collective-permute-start(bf16[320,2304]{1,0:T(8,128)(2,1)} %get-tuple-element.41.rest_0_), channel_id=1, source_target_pairs={{0,2},{1,3},{2,0},{3,1},{4,6},{5,7},{6,4},{7,5},{8,10},{9,11},{10,... | collective-permute-start | bytes 4423688 | tf_op jit(solution)/shard_map/ppermute | solution.py:346
  162.4 0.9 copy-start.18
  168.1 69.2 %collective-permute-start.11 = (bf16[640,2304]{1,0:T(8,128)(2,1)}, bf16[640,2304]{1,0:T(8,128)(2,1)}, u32[]{:S(2)}, u32[]{:S(2)}) collective-permute-start(bf16[640,2304]{1,0:T(8,128)(2,1)} %pad_maximum_fusion), channel_id=1, source_target_pairs={{0,1},{2,3},{4,5},{6,7},{8,9},{10,11},{12,13},{14,15}} | collective-permute-start | bytes 8847368 | tf_op jit(solution)/shard_map/ppermute | solution.py:366
  182.6 5.5 %copy-start = (bf16[1280,2304]{1,0:T(8,128)(2,1)S(1)}, bf16[1280,2304]{1,0:T(8,128)(2,1)}, u32[]{:S(2)}) copy-start(bf16[1280,2304]{1,0:T(8,128)(2,1)} %gather_rows.7) | copy-start | bytes 17694724
  188.1 4.0 %copy-start.7 = (bf16[160,2304]{1,0:T(8,128)(2,1)S(1)}, bf16[160,2304]{1,0:T(8,128)(2,1)}, u32[]{:S(2)}) copy-start(bf16[160,2304]{1,0:T(8,128)(2,1)} %get-tuple-element.40) | copy-start | bytes 2211844
  188.1 8.0 %copy-start.10 = (s32[8,1024]{1,0:T(8,128)S(1)}, s32[8,1024]{1,0:T(8,128)}, u32[]{:S(2)}) copy-start(s32[8,1024]{1,0:T(8,128)} %copy-done.9) | copy-start | bytes 98308
  188.1 8.0 %copy-start.15 = (pred[8,1024]{1,0:T(8,128)(4,1)S(1)}, pred[8,1024]{1,0:T(8,128)(4,1)}, u32[]{:S(2)}) copy-start(pred[8,1024]{1,0:T(8,128)(4,1)} %copy-done.14) | copy-start | bytes 24580
  188.1 8.8 %copy-start.17 = (s32[8]{0:T(128)S(1)}, s32[8]{0:T(128)}, u32[]{:S(2)}) copy-start(s32[8]{0:T(128)} %get-tuple-element.61) | copy-start | bytes 100
  192.1 7.3 %copy-start.16 = (f32[2304]{0:T(1024)S(1)}, f32[2304]{0:T(1024)}, u32[]{:S(2)}) copy-start(f32[2304]{0:T(1024)} %param.12) | copy-start | bytes 27652
  192.1 41.0 %copy-start.13 = (s32[8192]{0:T(1024)S(1)}, s32[8192]{0:T(1024)}, u32[]{:S(2)}) copy-start(s32[8192]{0:T(1024)} %param.9) | copy-start | bytes 98308
  192.1 42.5 %collective-permute-start.15 = (bf16[320,2304]{1,0:T(8,128)(2,1)}, bf16[320,2304]{1,0:T(8,128)(2,1)}, u32[]{:S(2)}, u32[]{:S(2)}) collective-permute-start(bf16[320,2304]{1,0:T(8,128)(2,1)} %get-tuple-element.54), channel_id=1, source_target_pairs={{0,4},{1,5},{2,6},{3,7},{4,0},{5,1},{6,2},{7,3},{8,12},{9,13},{10,... | collective-permute-start | bytes 4423688 | tf_op jit(solution)/shard_map/ppermute | solution.py:346
  194.1 33.4 %collective-permute-start.2 = (bf16[160,2304]{1,0:T(8,128)(2,1)}, bf16[160,2304]{1,0:T(8,128)(2,1)}, u32[]{:S(2)}, u32[]{:S(2)}) collective-permute-start(bf16[160,2304]{1,0:T(8,128)(2,1)} %slice_add_fusion.11), channel_id=1, source_target_pairs={{0,4},{1,5},{2,6},{3,7},{4,0},{5,1},{6,2},{7,3},{8,12},{9,13},{10,... | collective-permute-start | bytes 2211848 | tf_op jit(solution)/shard_map/ppermute | solution.py:346
  196.1 39.9 %collective-permute-start.13 = (bf16[320,2304]{1,0:T(8,128)(2,1)}, bf16[320,2304]{1,0:T(8,128)(2,1)}, u32[]{:S(2)}, u32[]{:S(2)}) collective-permute-start(bf16[320,2304]{1,0:T(8,128)(2,1)} %get-tuple-element.51), channel_id=1, source_target_pairs={{0,2},{1,3},{2,0},{3,1},{4,6},{5,7},{6,4},{7,5},{8,10},{9,11},{10,... | collective-permute-start | bytes 4423688 | tf_op jit(solution)/shard_map/ppermute | solution.py:346
  234.5 1.6 copy-start.6
  236.0 11.5 %collective-permute-start.16 = (bf16[160,2304]{1,0:T(8,128)(2,1)S(1)}, bf16[160,2304]{1,0:T(8,128)(2,1)S(1)}, u32[]{:S(2)}, u32[]{:S(2)}) collective-permute-start(bf16[160,2304]{1,0:T(8,128)(2,1)S(1)} %slice_add_fusion.4), channel_id=1, source_target_pairs={{0,2},{1,3},{2,0},{3,1},{4,6},{5,7},{6,4},{7,5},{8,10},{9,11},{10,... | collective-permute-start | bytes 2211848 | tf_op jit(solution)/shard_map/ppermute | solution.py:346
  237.3 11.5 %collective-permute-start.14 = (bf16[160,2304]{1,0:T(8,128)(2,1)S(1)}, bf16[160,2304]{1,0:T(8,128)(2,1)S(1)}, u32[]{:S(2)}, u32[]{:S(2)}) collective-permute-start(bf16[160,2304]{1,0:T(8,128)(2,1)S(1)} %slice_add_fusion.5), channel_id=1, source_target_pairs={{0,4},{1,5},{2,6},{3,7},{4,0},{5,1},{6,2},{7,3},{8,12},{9,13},{10,... | collective-permute-start | bytes 2211848 | tf_op jit(solution)/shard_map/ppermute | solution.py:346
  247.5 1.3 copy-start.19
  248.8 0.9 copy-start.20
  363.9 4.6 %copy-start.5 = (bf16[8192,256]{1,0:T(8,128)(2,1)S(1)}, bf16[8192,256]{1,0:T(8,128)(2,1)}, u32[]{:S(2)}) copy-start(bf16[8192,256]{1,0:T(8,128)(2,1)} %get-tuple-element.59) | copy-start | bytes 12582916
  368.5 3.7 copy-start.4
Sparse Core Ops, SparseCore 0:
  9.8 63.3 all-gather.2

commit v5 on v4

--- a/solution.py
+++ b/solution.py
@@ -120,7 +120,6 @@
         there = source.at[pl.ds(HEAD_ROWS + index // 3 * part, part), :] if index % 3 == 0 else parts.at[index // 3, index % 3 - 1]
         copies.append(pltpu.make_async_copy(ref.at[pl.ds(0, part), :], there, in_sems.at[index]))
     head_copy.start()
-    extra_copy.start()
     for copy in copies:
         copy.start()
     for copy in copies:
@@ -129,41 +128,45 @@
         span = pl.ds(HEAD_ROWS + index * part, part)
         source[span, :] = source[span, :] + parts[index, 0] + parts[index, 1]
     head_copy.wait()
-    extra_copy.wait()
+
+    @pl.when(more[0] > 0)
+    def _():
+        extra_copy.start()
+        extra_copy.wait()
 
     def results(block):
-        span = pl.ds(pl.multiple_of(block * 512, 512), 512)
+        span = pl.ds(pl.multiple_of(block * 256, 256), 256)
         return (pltpu.make_async_copy(resid.at[span, :], resid_hbm.at[span, :], out_sems.at[0]),
                 pltpu.make_async_copy(normed.at[span, :], normed_hbm.at[span, :], out_sems.at[1]))
 
-    @pl.loop(0, rows // 512)
+    @pl.loop(0, rows // 256)
     def _(block):
-        span = pl.ds(pl.multiple_of(block * 512, 512), 512)
-        lanes = lax.broadcasted_iota(jnp.int32, (512, known), 1)
+        span = pl.ds(pl.multiple_of(block * 256, 256), 256)
+        lanes = lax.broadcasted_iota(jnp.int32, (256, known), 1)
         value = jnp.where(lax.broadcasted_iota(jnp.int32, (1, known), 1) < HEAD_ROWS, normalizer, one)
-        select = jnp.where(lanes == cols_ref[span, :], jnp.broadcast_to(value, (512, known)), zero)
+        select = jnp.where(lanes == cols_ref[span, :], jnp.broadcast_to(value, (256, known)), zero)
         for piece in range(width // 256):
             cols = pl.ds(piece * 256, 256)
             resid[span, cols] = jnp.dot(select, source[:, cols], preferred_element_type=jnp.float32).astype(jnp.bfloat16)
 
         @pl.when(more[0] > 0)
         def _():
-            places = lax.broadcasted_iota(jnp.int32, (512, extra.shape[0]), 1) + known
+            places = lax.broadcasted_iota(jnp.int32, (256, extra.shape[0]), 1) + known
             from_extra = jnp.where(places == cols_ref[span, :], one, zero)
             for piece in range(width // 256):
                 cols = pl.ds(piece * 256, 256)
                 picked = jnp.dot(from_extra, extra[:, cols], preferred_element_type=jnp.float32)
                 resid[span, cols] = (resid[span, cols].astype(jnp.float32) + picked).astype(jnp.bfloat16)
 
-        for quarter in range(8):
-            rows_here = pl.ds(pl.multiple_of(block * 512 + quarter * 64, 64), 64)
+        for quarter in range(4):
+            rows_here = pl.ds(pl.multiple_of(block * 256 + quarter * 64, 64), 64)
             widened = resid[rows_here, :].astype(jnp.float32)
             inv_rms = lax.rsqrt(jnp.mean(widened * widened, axis=-1, keepdims=True) + EPSILON)
             normed[rows_here, :] = (widened * inv_rms * gain_ref[...]).astype(jnp.bfloat16)
         for result in results(block):
             result.start()
 
-    @pl.loop(0, rows // 512)
+    @pl.loop(0, rows // 256)
     def _(block):
         for result in results(block):
             result.wait()
@@ -195,7 +198,7 @@
     )(more, cols, gain, head, extra, *pieces)
 
 
-def heads_kernel(rows, normed_hbm, cos_ref, sin_ref, wq_hbm, wk_hbm, wv_hbm, q_out, k_out, v_out,
+def heads_kernel(rows, normed_hbm, cos_ref, sin_ref, wq_mine, wq_far, wq_near, wk_hbm, wv_hbm, q_out, kv_out,
                  wq, wk, wv, normed, q_stage, kv_stage, w_sem, q_send, q_recv, kv_send, kv_recv,
                  own_recv, fwd_send, fwd_recv, keep_sem):
     group = lax.axis_index("dp")
@@ -203,11 +206,16 @@
     core = lax.rem(me, 2)
     chip = me // 2
     partner = me + 1 - 2 * core
-    kv_outs = (k_out, v_out)
+    kv_outs = (kv_out.at[0], kv_out.at[1])
     tiles = rows // SEND_ROWS
     half = HEAD_DIM // 2
 
-    loads = [pltpu.make_async_copy(src, dst, w_sem.at[n]) for n, (src, dst) in enumerate(((normed_hbm, normed), (wk_hbm, wk), (wv_hbm, wv), (wq_hbm, wq)))]
+    depth = wq_mine.shape[1]
+    own_depth = pl.ds(pl.multiple_of(group * depth, depth), depth)
+    far_depth = pl.ds(pl.multiple_of((1 - group) * depth, depth), depth)
+    sources = ((normed_hbm, normed), (wk_hbm, wk), (wv_hbm, wv), (wq_mine, wq.at[:, own_depth, :]),
+               (wq_far, wq.at[pl.ds(core * CHIPS, CHIPS), far_depth, :]), (wq_near, wq.at[pl.ds((1 - core) * CHIPS, CHIPS), far_depth, :]))
+    loads = [pltpu.make_async_copy(src, dst, w_sem.at[n]) for n, (src, dst) in enumerate(sources)]
     for load in loads:
         load.start()
 
@@ -288,10 +296,7 @@
                 other = other_out.at[whole(source), :]
                 remote(other, other, fwd_send.at[offset, side], fwd_recv.at[offset, side], partner).wait_recv()
 
-    for kind in range(2):
-        @pl.when(core == kind)
-        def _():
-            forward(kv_outs[kind], kv_outs[1 - kind])
+    forward(kv_out.at[core], kv_out.at[1 - core])
 
     for keep in keeps:
         keep.wait()
@@ -306,9 +311,9 @@
     remote(q_stage.at[partner], q_out.at[whole(partner), :], q_send.at[0, 0], q_recv.at[0, 0], partner).wait()
 
 
-def project_heads(normed, cosines, sines, wq_all, w_key, w_value):
+def project_heads(normed, cosines, sines, wq_parts, w_key, w_value):
     rows, width = normed.shape
-    heads = wq_all.shape[0]
+    heads = wq_parts[0].shape[0]
     tokens = rows * heads
     tiles = rows // SEND_ROWS
     vmem = pl.BlockSpec(memory_space=pltpu.VMEM)
@@ -316,17 +321,17 @@
     dma = pltpu.SemaphoreType.DMA
     return pl.pallas_call(
         functools.partial(heads_kernel, rows),
-        out_shape=(jax.ShapeDtypeStruct((tokens, HEAD_DIM), jnp.bfloat16),) * 3,
-        in_specs=[anywhere, vmem, vmem, anywhere, anywhere, anywhere],
-        out_specs=(anywhere,) * 3,
+        out_shape=(jax.ShapeDtypeStruct((tokens, HEAD_DIM), jnp.bfloat16), jax.ShapeDtypeStruct((2, tokens, HEAD_DIM), jnp.bfloat16)),
+        in_specs=[anywhere, vmem, vmem] + [anywhere] * 5,
+        out_specs=(anywhere, anywhere),
         scratch_shapes=[
-            pltpu.VMEM(wq_all.shape, jnp.bfloat16),
+            pltpu.VMEM((heads, width, HEAD_DIM), jnp.bfloat16),
             pltpu.VMEM(w_key.shape, jnp.bfloat16),
             pltpu.VMEM(w_value.shape, jnp.bfloat16),
             pltpu.VMEM((rows, width), jnp.bfloat16),
             pltpu.VMEM((heads, rows, HEAD_DIM), jnp.bfloat16),
             pltpu.VMEM((2, CHIPS, rows, HEAD_DIM), jnp.bfloat16),
-            dma((4,)),
+            dma((6,)),
             dma((CHIPS, 2)), dma((CHIPS, 2)),
             dma((CHIPS, 2)), dma((CHIPS, 2, tiles)),
             dma((2,)),
@@ -336,7 +341,7 @@
         compiler_params=pltpu.CompilerParams(collective_id=0, has_side_effects=True, vmem_limit_bytes=67_043_328),
         cost_estimate=pl.CostEstimate(flops=2 * rows * width * 4096, bytes_accessed=40_000_000, transcendentals=0),
         name="project_heads",
-    )(normed, cosines, sines, wq_all, w_key, w_value)
+    )(normed, cosines, sines, *wq_parts, w_key, w_value)
 
 
 def solution(mesh):
@@ -369,7 +374,12 @@
     def local_body(token_ids, positions, table_rows, norm_scale, w_query, w_key, w_value):
         dev_index = lax.axis_index("tp")
         vocab_rows, model_width = table_rows.shape
-        wq_all = lax.all_gather(w_query, "tp", axis=0)
+        group = lax.axis_index("dp")
+        core = dev_index % 2
+        part_rows = w_query.shape[0] // 2
+        wq_mine = lax.all_gather(lax.dynamic_slice_in_dim(w_query, group * part_rows, part_rows, axis=0), "tp", axis=0)
+        wq_far = lax.ppermute(lax.dynamic_slice_in_dim(wq_mine, core * (group_size // 2), group_size // 2, axis=0), "dp", [(0, 1), (1, 0)])
+        wq_near = exchange(wq_far, 1)
         head_halves = share_head(table_rows[:HEAD_ROWS])
         tokens = token_ids.shape[0]
         block_rows = tokens // group_size
@@ -419,9 +429,9 @@
         pieces = []
         after, late, late_next = [], [], []
         for chunk in range(CHUNKS):
-            other = gather(chunk, 1, after + late)
+            other = gather(chunk, 1, after + late + ([wq_mine] if chunk == CHUNKS - 1 else []))
             got = exchange(other, 1)
-            mine = gather(chunk, 0, [other] + ([wq_all] if chunk == CHUNKS - 1 else []))
+            mine = gather(chunk, 0, [other])
             after, late = [], late_next
             late_next = []
             spans = []
@@ -459,8 +469,8 @@
         residual, normed = finish_rows(more.reshape(1), own_places[:, None], (1.0 + norm_scale)[None, :], head, extra, pieces)
         own = lax.dynamic_slice_in_dim(positions, dev_index * block_rows, block_rows)
         cosines, sines = rope_tables(own)
-        outs = project_heads(normed, cosines, sines, wq_all, w_key, w_value)
-        return (residual,) + tuple(out[:, None, :] for out in outs)
+        queries, keys_values = project_heads(normed, cosines, sines, (wq_mine, wq_far, wq_near), w_key, w_value)
+        return residual, queries[:, None, :], keys_values[0][:, None, :], keys_values[1][:, None, :]
 
     head_spec = P("dp", "tp", None)
     return jax.shard_map(local_body, mesh=mesh, in_specs=(P("dp"), P("dp"), P("tp", None), P(), P(None, "tp"), P(), P()), out_specs=(P(("dp", "tp"), None), head_spec, head_spec, head_spec), check_vma=False)

time: 388 us -> 382 us (0.985)
  starting transfers between devices: 62.2 us -> 50.8 us
  Pallas kernels: 163 us -> 168 us
    ppermute x10 -> x11, starting transfers between devices: 44.2 us -> 31.3 us  [exchange(): return lax.ppermute(rows, 'tp', [(i, i ^ bit) for i in range(group_size)])]
    unnamed x46, local copies, waits for them, and re-layouts: 15.2 us -> 6.78 us
    another operation x1 -> x2, local copies, waits for them, and re-layouts: 1.41 us -> 7.96 us  [the longest x1 6.6 us: local_body(): keys_values[1][:, None, :]]
    pallas_call x1, Pallas kernels: 97.2 us -> 103 us  [project_heads(): pl.pallas_call(functools.partial(heads_kernel, rows), out_shape=(jax.Shap...]
    ppermute x10 -> x11, waiting for transfers between devices: 56 us -> 55.7 us  [exchange(): return lax.ppermute(rows, 'tp', [(i, i ^ bit) for i in range(group_size)])]
  transfers between devices with their start and end apart: 18 -> 20, of which waited for: 7 -> 6; matrix products, arithmetic and copies ran while one was open for 14% -> 14% of each run, Pallas kernels for 13% -> 17%
where the time goes in v5:
time: 382 us; the launch traced here: 376 us
  Pallas kernels  168 us (44%)
  waiting for transfers between devices  67.1 us (18%)
  starting transfers between devices  50.8 us (13%)
  other arithmetic  43.9 us (11%)
  local copies, waits for them, and re-layouts  23.4 us (6%)
  between operations  15.7 us (4%)
  blocking collectives  4.78 us (1%)
    pallas_call x1, Pallas kernels, project_heads(): pl.pallas_call(functools.partial(heads_kernel, rows), out_shape=(jax.Shap...  103 us
    ppermute x11, waiting for transfers between devices, exchange(): return lax.ppermute(rows, 'tp', [(i, i ^ bit) for i in range(group_size)])  55.7 us
    pallas_call x4, Pallas kernels, gather_rows(): pl.pallas_call(functools.partial(gather_kernel, base, tiles, width), grid...  48.4 us
    ppermute x11, starting transfers between devices, exchange(): return lax.ppermute(rows, 'tp', [(i, i ^ bit) for i in range(group_size)])  31.3 us
    pallas_call x1, Pallas kernels, finish_rows(): pl.pallas_call(functools.partial(finish_kernel, len(pieces)), out_shape=(...  16.6 us
    add x4, other arithmetic, local_body(): both = lax.optimization_barrier([mine[span] + got[span] for span in spans])  15.3 us
    ppermute x6, starting transfers between devices, pass_head(): got = lax.ppermute(values, 'tp', pairs)  14.9 us
    ppermute x6, waiting for transfers between devices, pass_head(): got = lax.ppermute(values, 'tp', pairs)  11.4 us
  transfers between devices with their start and end apart: 20, of which 6 were waited for; matrix products, arithmetic and copies ran while one was open for 14% of the time, Pallas kernels for 17%

profile of v5, /device:TPU:0, one launch (start us, length us, event | category | flops | bytes accessed | tf_op | source)
XLA Modules:
  0.0 375.8 jit_solution(17318418078030804788)
XLA Ops:
  7.2 1.9 constant_dynamic-slice_fusion.1
  9.2 3.1 fusion.13
  12.3 5.2 %collective-permute-start.3 = (bf16[320,2304]{1,0:T(8,128)(2,1)}, bf16[320,2304]{1,0:T(8,128)(2,1)S(1)}, u32[]{:S(2)}, u32[]{:S(2)}) collective-permute-start(bf16[320,2304]{1,0:T(8,128)(2,1)} %get-tuple-element.63), channel_id=1, source_target_pairs={{0,2},{8,10}} | collective-permute-start | bytes 4423688 | tf_op jit(solution)/shard_map/ppermute | solution.py:354
  17.5 2.4 collective-permute-start.8
  21.8 3.0 select_reduce_fusion.1
  25.4 1.4 fusion.9
  26.8 2.6 select_reduce_fusion.2
  29.4 12.6 %gather_rows.4.rest_0_ = bf16[1280,2304]{1,0:T(8,128)(2,1)} custom-call(s32[5120]{0:T(1024)} %bitcast.38, s32[40]{0:T(128)} %get-tuple-element.83.counts, f32[40,1,128]{2,1,0:T(1,128)} %bitcast.42, bf16[32000,2304]{1,0:T(8,128)(2,1)} %table_ref.7), custom_call_target="tpu_custom_call" | custom-call | flops 25600000000 | bytes 17694720 | tf_op jit(solution)/shard_map/gather_rows/pallas_call | solution.py:98
  42.2 11.4 %collective-permute-done.3 = bf16[320,2304]{1,0:T(8,128)(2,1)S(1)} collective-permute-done((bf16[320,2304]{1,0:T(8,128)(2,1)}, bf16[320,2304]{1,0:T(8,128)(2,1)S(1)}, u32[]{:S(2)}, u32[]{:S(2)}) %collective-permute-start.3) | collective-permute-done | bytes 1474592 | tf_op jit(solution)/shard_map/ppermute | solution.py:354
  54.6 2.1 broadcast_select_fusion.2
  56.8 1.8 collective-permute-start.4
  58.6 1.8 collective-permute-start.9
  60.4 12.6 %gather_rows.5 = bf16[1280,2304]{1,0:T(8,128)(2,1)} custom-call(s32[5120]{0:T(1024)} %bitcast.39, s32[40]{0:T(128)} %get-tuple-element.83.counts, f32[40,1,128]{2,1,0:T(1,128)} %bitcast.43, bf16[32000,2304]{1,0:T(8,128)(2,1)} %table_ref.7, bf16[1280,2304]{1,0:T(8,128)(2,1)} %gather_rows.4.rest_0_), custom_call_target="tpu_custom_call" | custom-call | flops 25600000000 | bytes 17694720 | tf_op jit(solution)/shard_map/gather_rows/pallas_call | solution.py:98
  73.0 1.3 broadcast_select_fusion.4
  74.3 2.0 collective-permute-start.5
  76.4 1.8 collective-permute-start.10
  78.2 3.5 slice_add_fusion.12
  81.8 3.4 slice_add_fusion.2
  85.1 2.8 collective-permute-start.6
  87.9 11.6 %gather_rows.6.rest_0_ = bf16[1280,2304]{1,0:T(8,128)(2,1)} custom-call(s32[5120]{0:T(1024)} %bitcast.40, s32[40]{0:T(128)} %get-tuple-element.83.counts, f32[40,1,128]{2,1,0:T(1,128)} %bitcast.44, bf16[32000,2304]{1,0:T(8,128)(2,1)} %table_ref.7, bf16[320,2304]{1,0:T(8,128)(2,1)} %get-tuple-element.40.rest_0_, bf16[320,2304]{1,0:T(8,128)(2,1)} %copy-done.2, ...), custom_call_target="tpu_custom_call" | custom-call | flops 25600000000 | bytes 17694720 | tf_op jit(solution)/shard_map/gather_rows/pallas_call | solution.py:98
  99.5 6.0 %collective-permute-done.6.refs_4_ = bf16[320,2304]{1,0:T(8,128)(2,1)} collective-permute-done((bf16[320,2304]{1,0:T(8,128)(2,1)S(1)}, bf16[320,2304]{1,0:T(8,128)(2,1)}, u32[]{:S(2)}, u32[]{:S(2)}) %collective-permute-start.6) | collective-permute-done | bytes 1474592 | tf_op jit(solution)/shard_map/ppermute | solution.py:351
  105.6 1.4 slice_add_fusion.10
  107.0 26.3 %collective-permute-start.7 = (bf16[160,2304]{1,0:T(8,128)(2,1)S(1)}, bf16[160,2304]{1,0:T(8,128)(2,1)S(1)}, u32[]{:S(2)}, u32[]{:S(2)}) collective-permute-start(bf16[160,2304]{1,0:T(8,128)(2,1)S(1)} %slice_add_fusion.10), channel_id=1, source_target_pairs={{0,2},{1,3},{2,0},{3,1},{4,6},{5,7},{6,4},{7,5},{8,10},{9,11},{10,... | collective-permute-start | bytes 2211848 | tf_op jit(solution)/shard_map/ppermute | solution.py:351
  133.3 17.1 %collective-permute-done.7.refs_5_ = bf16[160,2304]{1,0:T(8,128)(2,1)S(1)} collective-permute-done((bf16[160,2304]{1,0:T(8,128)(2,1)S(1)}, bf16[160,2304]{1,0:T(8,128)(2,1)S(1)}, u32[]{:S(2)}, u32[]{:S(2)}) %collective-permute-start.7) | collective-permute-done | bytes 737312 | tf_op jit(solution)/shard_map/ppermute | solution.py:351
  151.3 1.7 broadcast_select_fusion.6
  153.0 1.6 broadcast_select_fusion.1
  154.6 1.8 pad_maximum_fusion
  156.4 2.8 collective-permute-start.11
  159.2 1.6 constant_dynamic-slice_fusion
  160.8 1.7 collective-permute-start.17
  162.5 11.6 %gather_rows.7 = bf16[1280,2304]{1,0:T(8,128)(2,1)} custom-call(s32[5120]{0:T(1024)} %bitcast.41, s32[40]{0:T(128)} %get-tuple-element.83.counts, f32[40,1,128]{2,1,0:T(1,128)} %bitcast.45, bf16[32000,2304]{1,0:T(8,128)(2,1)} %table_ref.7, bf16[1280,2304]{1,0:T(8,128)(2,1)} %gather_rows.6.rest_0_), custom_call_target="tpu_custom_call" | custom-call | flops 25600000000 | bytes 17694720 | tf_op jit(solution)/shard_map/gather_rows/pallas_call | solution.py:98
  174.2 4.8 %slice_add_fusion = (bf16[320,2304]{1,0:T(8,128)(2,1)}, bf16[320,2304]{1,0:T(8,128)(2,1)}) fusion(bf16[1280,2304]{1,0:T(8,128)(2,1)} %collective-permute-done.12, bf16[1280,2304]{1,0:T(8,128)(2,1)} %gather_rows.7), kind=kLoop, calls=%fused_computation.21 | loop fusion | flops 1474560 | bytes 8847360 | tf_op jit(solution)/shard_map/add | solution.py:441
  179.3 3.6 slice_add_fusion.6
  182.9 2.1 slice_add_fusion.11
  185.0 2.0 collective-permute-start.2
  191.4 3.0 multiply_sine_fusion
  194.4 16.0 %collective-permute-done.2.refs_2_ = bf16[160,2304]{1,0:T(8,128)(2,1)} collective-permute-done((bf16[160,2304]{1,0:T(8,128)(2,1)}, bf16[160,2304]{1,0:T(8,128)(2,1)}, u32[]{:S(2)}, u32[]{:S(2)}) %collective-permute-start.2) | collective-permute-done | bytes 737312 | tf_op jit(solution)/shard_map/ppermute | solution.py:351
  210.5 4.8 %pmax.7 = s32[]{:T(128)} all-reduce(s32[]{:T(128)S(6)} %convert_element_type.29), channel_id=1, replica_groups=mesh['dp'=2,'tp'=8] {'dp'}, use_global_device_ids=true, to_apply=%region_5.6 | all-reduce | flops 1 | bytes 8 | tf_op jit(solution)/shard_map/pmax | solution.py:464
  215.9 1.4 conditional.1
  215.9 1.4 broadcast.217
  217.3 1.5 slice_add_fusion.4
  220.1 2.3 broadcast_select_fusion.head_hbm
  222.4 15.2 %collective-permute-done.16.refs_11_ = bf16[160,2304]{1,0:T(8,128)(2,1)S(1)} collective-permute-done((bf16[160,2304]{1,0:T(8,128)(2,1)S(1)}, bf16[160,2304]{1,0:T(8,128)(2,1)S(1)}, u32[]{:S(2)}, u32[]{:S(2)}) %collective-permute-start.16) | collective-permute-done | bytes 737312 | tf_op jit(solution)/shard_map/ppermute | solution.py:351
  237.6 1.3 collective-permute-done.14.refs_8_
  239.8 16.6 %finish_rows.1 = (bf16[1024,2304]{1,0:T(8,128)(2,1)}, bf16[1024,2304]{1,0:T(8,128)(2,1)}) custom-call(s32[1]{0:T(128)} %bitcast.6.more, s32[1024,1]{1,0:T(8,128)} %copy.17.cols_ref, f32[1,2304]{1,0:T(1,128)} %broadcast_in_dim.89.gain_ref, bf16[640,2304]{1,0:T(8,128)(2,1)} %broadcast_select_fusion.head_hbm, bf16[384,2304]{1,0:T(8,128)(2,1)} %get-tuple-element.96.extra_hbm, ...), custom_call_target="tpu_custom_call" | custom-call | flops 6039797760 | bytes 16000000 | tf_op jit(solution)/shard_map/finish_rows/pallas_call | solution.py:182
  256.4 103.3 %project_heads.1 = (bf16[8192,256]{1,0:T(8,128)(2,1)}, bf16[2,8192,256]{2,1,0:T(8,128)(2,1)}) custom-call(bf16[1024,2304]{1,0:T(8,128)(2,1)} %get-tuple-element.56.normed_hbm, f32[1024,128]{1,0:T(8,128)} %get-tuple-element.86.cos_ref, f32[1024,128]{1,0:T(8,128)} %get-tuple-element.85.sin_ref, bf16[8,1152,256]{2,1,0:T(8,128)(2,1)} %bitcast.33, ...), custom_call_target="tpu_custom_call" | custom-call | flops 19327352832 | bytes 40000000 | tf_op jit(solution)/shard_map/project_heads/pallas_call | solution.py:322
  359.7 6.6 %slice_bitcast_fusion = (bf16[8192,1,256]{2,0,1:T(8,128)(2,1)}, bf16[8192,1,256]{2,0,1:T(8,128)(2,1)}) fusion(bf16[2,8192,256]{2,1,0:T(8,128)(2,1)} %get-tuple-element.58), kind=kLoop, calls=%fused_computation.13 | loop fusion | bytes 16777216 | tf_op jit(solution)/shard_map/broadcast_in_dim;squeeze | solution.py:473
  366.9 2.0 copy.26
  (95 shorter events, 11.7 us)
Async XLA Ops:
  7.2 80.7 %all-gather.3.cloned.1.call-start = ((), (), s32[]{:S(2)}) async-start(), calls=%async_computation.2 | async-start | bytes 5308416 | tf_op jit(solution)/shard_map/all_gather | solution.py:380
  9.2 10.8 %copy-start.11 = (s32[8192]{0:T(1024)S(1)}, s32[8192]{0:T(1024)}, u32[]{:S(2)}) copy-start(s32[8192]{0:T(1024)} %param.9) | copy-start | bytes 98308
  12.3 41.2 %collective-permute-start.3 = (bf16[320,2304]{1,0:T(8,128)(2,1)}, bf16[320,2304]{1,0:T(8,128)(2,1)S(1)}, u32[]{:S(2)}, u32[]{:S(2)}) collective-permute-start(bf16[320,2304]{1,0:T(8,128)(2,1)} %get-tuple-element.63), channel_id=1, source_target_pairs={{0,2},{8,10}} | collective-permute-start | bytes 4423688 | tf_op jit(solution)/shard_map/ppermute | solution.py:354
  17.5 37.2 %collective-permute-start.8 = (bf16[320,2304]{1,0:T(8,128)(2,1)S(1)}, bf16[320,2304]{1,0:T(8,128)(2,1)}, u32[]{:S(2)}, u32[]{:S(2)}) collective-permute-start(bf16[320,2304]{1,0:T(8,128)(2,1)S(1)} %get-tuple-element.64), channel_id=1, source_target_pairs={{0,4},{8,12}} | collective-permute-start | bytes 4423688 | tf_op jit(solution)/shard_map/ppermute | solution.py:354
  19.9 22.2 %copy-start.10 = (s32[8,1024]{1,0:T(8,128)}, s32[8,1024]{1,0:T(8,128)S(1)}, u32[]{:S(2)}) copy-start(s32[8,1024]{1,0:T(8,128)S(1)} %reshape.139) | copy-start | bytes 98308
  20.6 0.6 copy-start.13
  21.2 0.6 copy-start.8
  42.1 36.1 %collective-permute-start = (bf16[1280,2304]{1,0:T(8,128)(2,1)}, bf16[1280,2304]{1,0:T(8,128)(2,1)}, u32[]{:S(2)}, u32[]{:S(2)}) collective-permute-start(bf16[1280,2304]{1,0:T(8,128)(2,1)} %gather_rows.4.rest_0_), channel_id=1, source_target_pairs={{0,1},{1,0},{2,3},{3,2},{4,5},{5,4},{6,7},{7,6},{8,9},{9,8},{10,11... | collective-permute-start | bytes 17694728 | tf_op jit(solution)/shard_map/ppermute | solution.py:351
  53.5 1.1 copy-start.7
  56.8 16.3 %collective-permute-start.4 = (bf16[320,2304]{1,0:T(8,128)(2,1)S(1)}, bf16[320,2304]{1,0:T(8,128)(2,1)}, u32[]{:S(2)}, u32[]{:S(2)}) collective-permute-start(bf16[320,2304]{1,0:T(8,128)(2,1)S(1)} %get-tuple-element.61), channel_id=1, source_target_pairs={{2,6},{10,14}} | collective-permute-start | bytes 4423688 | tf_op jit(solution)/shard_map/ppermute | solution.py:354
  58.6 17.7 %collective-permute-start.9 = (bf16[320,2304]{1,0:T(8,128)(2,1)S(1)}, bf16[320,2304]{1,0:T(8,128)(2,1)}, u32[]{:S(2)}, u32[]{:S(2)}) collective-permute-start(bf16[320,2304]{1,0:T(8,128)(2,1)S(1)} %get-tuple-element.62), channel_id=1, source_target_pairs={{4,6},{12,14}} | collective-permute-start | bytes 4423688 | tf_op jit(solution)/shard_map/ppermute | solution.py:354
  73.0 5.2 %copy-start = (bf16[1280,2304]{1,0:T(8,128)(2,1)S(1)}, bf16[1280,2304]{1,0:T(8,128)(2,1)}, u32[]{:S(2)}) copy-start(bf16[1280,2304]{1,0:T(8,128)(2,1)} %gather_rows.5) | copy-start | bytes 17694724
  74.3 59.0 %collective-permute-start.5 = (bf16[320,2304]{1,0:T(8,128)(2,1)}, bf16[320,2304]{1,0:T(8,128)(2,1)}, u32[]{:S(2)}, u32[]{:S(2)}) collective-permute-start(bf16[320,2304]{1,0:T(8,128)(2,1)} %broadcast_select_fusion.4), channel_id=1, source_target_pairs={{6,4},{14,12}} | collective-permute-start | bytes 4423688 | tf_op jit(solution)/shard_map/ppermute | solution.py:354
  76.4 5.3 %copy-start.3 = (bf16[320,2304]{1,0:T(8,128)(2,1)}, bf16[320,2304]{1,0:T(8,128)(2,1)S(1)}, u32[]{:S(2)}) copy-start(bf16[320,2304]{1,0:T(8,128)(2,1)S(1)} %broadcast_select_fusion.3) | copy-start | bytes 4423684
  76.4 74.9 %collective-permute-start.10 = (bf16[320,2304]{1,0:T(8,128)(2,1)S(1)}, bf16[320,2304]{1,0:T(8,128)(2,1)}, u32[]{:S(2)}, u32[]{:S(2)}) collective-permute-start(bf16[320,2304]{1,0:T(8,128)(2,1)S(1)} %broadcast_select_fusion.3), channel_id=1, source_target_pairs={{6,2},{14,10}} | collective-permute-start | bytes 4423688 | tf_op jit(solution)/shard_map/ppermute | solution.py:354
  85.1 2.8 copy-start.2
  85.1 20.4 %collective-permute-start.6 = (bf16[320,2304]{1,0:T(8,128)(2,1)S(1)}, bf16[320,2304]{1,0:T(8,128)(2,1)}, u32[]{:S(2)}, u32[]{:S(2)}) collective-permute-start(bf16[320,2304]{1,0:T(8,128)(2,1)S(1)} %get-tuple-element.43.rest_1_), channel_id=1, source_target_pairs={{0,4},{1,5},{2,6},{3,7},{4,0},{5,1},{6,2},{7,3},{8,12},{9,13},{10,... | collective-permute-start | bytes 4423688 | tf_op jit(solution)/shard_map/ppermute | solution.py:351
  99.5 74.7 %collective-permute-start.12 = (bf16[1280,2304]{1,0:T(8,128)(2,1)}, bf16[1280,2304]{1,0:T(8,128)(2,1)}, u32[]{:S(2)}, u32[]{:S(2)}) collective-permute-start(bf16[1280,2304]{1,0:T(8,128)(2,1)} %gather_rows.6.rest_0_), channel_id=1, source_target_pairs={{0,1},{1,0},{2,3},{3,2},{4,5},{5,4},{6,7},{7,6},{8,9},{9,8},{10,11... | collective-permute-start | bytes 17694728 | tf_op jit(solution)/shard_map/ppermute | solution.py:351
  107.0 43.4 %collective-permute-start.7 = (bf16[160,2304]{1,0:T(8,128)(2,1)S(1)}, bf16[160,2304]{1,0:T(8,128)(2,1)S(1)}, u32[]{:S(2)}, u32[]{:S(2)}) collective-permute-start(bf16[160,2304]{1,0:T(8,128)(2,1)S(1)} %slice_add_fusion.10), channel_id=1, source_target_pairs={{0,2},{1,3},{2,0},{3,1},{4,6},{5,7},{6,4},{7,5},{8,10},{9,11},{10,... | collective-permute-start | bytes 2211848 | tf_op jit(solution)/shard_map/ppermute | solution.py:351
  133.2 49.7 %collective-permute-start.1 = (bf16[320,2304]{1,0:T(8,128)(2,1)}, bf16[320,2304]{1,0:T(8,128)(2,1)}, u32[]{:S(2)}, u32[]{:S(2)}) collective-permute-start(bf16[320,2304]{1,0:T(8,128)(2,1)} %get-tuple-element.40.rest_0_), channel_id=1, source_target_pairs={{0,2},{1,3},{2,0},{3,1},{4,6},{5,7},{6,4},{7,5},{8,10},{9,11},{10,... | collective-permute-start | bytes 4423688 | tf_op jit(solution)/shard_map/ppermute | solution.py:351
  150.4 0.9 copy-start.17
  151.3 7.9 %slice-start = ((s8[4718592]{0:T(1024)(128)(4,1)}), s8[4194304]{0:T(1024)(128)(4,1)S(1)}, s32[]{:S(2)}) async-start(s8[4718592]{0:T(1024)(128)(4,1)} %bitcast.34), calls=%async_computation.3 | async-start | bytes 8388608
  153.0 6.3 %slice-start.1 = ((s8[4718592]{0:T(1024)(128)(4,1)}), s8[524288]{0:T(1024)(128)(4,1)S(1)}, s32[]{:S(2)}) async-start(s8[4718592]{0:T(1024)(128)(4,1)} %bitcast.34), calls=%async_computation.4 | async-start | bytes 1048576
  156.4 63.7 %collective-permute-start.11 = (bf16[640,2304]{1,0:T(8,128)(2,1)}, bf16[640,2304]{1,0:T(8,128)(2,1)}, u32[]{:S(2)}, u32[]{:S(2)}) collective-permute-start(bf16[640,2304]{1,0:T(8,128)(2,1)} %pad_maximum_fusion), channel_id=1, source_target_pairs={{0,1},{2,3},{4,5},{6,7},{8,9},{10,11},{12,13},{14,15}} | collective-permute-start | bytes 8847368 | tf_op jit(solution)/shard_map/ppermute | solution.py:371
  160.8 56.5 %collective-permute-start.17 = (bf16[4,1152,256]{2,1,0:T(8,128)(2,1)}, bf16[4,1152,256]{2,1,0:T(8,128)(2,1)}, u32[]{:S(2)}, u32[]{:S(2)}) collective-permute-start(bf16[4,1152,256]{2,1,0:T(8,128)(2,1)} %constant_dynamic-slice_fusion), channel_id=1, source_target_pairs={{0,8},{8,0},{1,9},{9,1},{2,10},{10,2},{3,11},{11,3},{4,12},{12,4},... | collective-permute-start | bytes 7077896 | tf_op jit(solution)/shard_map/ppermute | solution.py:381
  174.1 5.2 %copy-start.1 = (bf16[1280,2304]{1,0:T(8,128)(2,1)S(1)}, bf16[1280,2304]{1,0:T(8,128)(2,1)}, u32[]{:S(2)}) copy-start(bf16[1280,2304]{1,0:T(8,128)(2,1)} %gather_rows.7) | copy-start | bytes 17694724
  179.3 3.6 copy-start.6
  179.3 7.7 %copy-start.9 = (s32[8,1024]{1,0:T(8,128)S(1)}, s32[8,1024]{1,0:T(8,128)}, u32[]{:S(2)}) copy-start(s32[8,1024]{1,0:T(8,128)} %copy-done.8) | copy-start | bytes 98308
  179.3 7.7 %copy-start.14 = (pred[8,1024]{1,0:T(8,128)(4,1)S(1)}, pred[8,1024]{1,0:T(8,128)(4,1)}, u32[]{:S(2)}) copy-start(pred[8,1024]{1,0:T(8,128)(4,1)} %copy-done.13) | copy-start | bytes 24580
  179.3 8.5 %copy-start.16 = (s32[8]{0:T(128)S(1)}, s32[8]{0:T(128)}, u32[]{:S(2)}) copy-start(s32[8]{0:T(128)} %get-tuple-element.59) | copy-start | bytes 100
  182.9 7.2 %copy-start.15 = (f32[2304]{0:T(1024)S(1)}, f32[2304]{0:T(1024)}, u32[]{:S(2)}) copy-start(f32[2304]{0:T(1024)} %param.12) | copy-start | bytes 27652
  182.9 33.0 %copy-start.12 = (s32[8192]{0:T(1024)S(1)}, s32[8192]{0:T(1024)}, u32[]{:S(2)}) copy-start(s32[8192]{0:T(1024)} %param.9) | copy-start | bytes 98308
  182.9 34.4 %collective-permute-start.15 = (bf16[320,2304]{1,0:T(8,128)(2,1)}, bf16[320,2304]{1,0:T(8,128)(2,1)}, u32[]{:S(2)}, u32[]{:S(2)}) collective-permute-start(bf16[320,2304]{1,0:T(8,128)(2,1)} %get-tuple-element.53), channel_id=1, source_target_pairs={{0,4},{1,5},{2,6},{3,7},{4,0},{5,1},{6,2},{7,3},{8,12},{9,13},{10,... | collective-permute-start | bytes 4423688 | tf_op jit(solution)/shard_map/ppermute | solution.py:351
  185.0 25.5 %collective-permute-start.2 = (bf16[160,2304]{1,0:T(8,128)(2,1)}, bf16[160,2304]{1,0:T(8,128)(2,1)}, u32[]{:S(2)}, u32[]{:S(2)}) collective-permute-start(bf16[160,2304]{1,0:T(8,128)(2,1)} %slice_add_fusion.11), channel_id=1, source_target_pairs={{0,4},{1,5},{2,6},{3,7},{4,0},{5,1},{6,2},{7,3},{8,12},{9,13},{10,... | collective-permute-start | bytes 2211848 | tf_op jit(solution)/shard_map/ppermute | solution.py:351
  187.0 31.8 %collective-permute-start.13 = (bf16[320,2304]{1,0:T(8,128)(2,1)}, bf16[320,2304]{1,0:T(8,128)(2,1)}, u32[]{:S(2)}, u32[]{:S(2)}) collective-permute-start(bf16[320,2304]{1,0:T(8,128)(2,1)} %get-tuple-element.50), channel_id=1, source_target_pairs={{0,2},{1,3},{2,0},{3,1},{4,6},{5,7},{6,4},{7,5},{8,10},{9,11},{10,... | collective-permute-start | bytes 4423688 | tf_op jit(solution)/shard_map/ppermute | solution.py:351
  217.3 1.6 copy-start.5
  217.3 39.1 %collective-permute-start.18 = (bf16[4,1152,256]{2,1,0:T(8,128)(2,1)}, bf16[4,1152,256]{2,1,0:T(8,128)(2,1)}, u32[]{:S(2)}, u32[]{:S(2)}) collective-permute-start(bf16[4,1152,256]{2,1,0:T(8,128)(2,1)} %collective-permute-done.17.wq_far), channel_id=1, source_target_pairs={{0,1},{1,0},{2,3},{3,2},{4,5},{5,4},{6,7},{7,6},{8,9},{9,8},{10,11... | collective-permute-start | bytes 7077896 | tf_op jit(solution)/shard_map/ppermute | solution.py:351
  218.8 18.9 %collective-permute-start.16 = (bf16[160,2304]{1,0:T(8,128)(2,1)S(1)}, bf16[160,2304]{1,0:T(8,128)(2,1)S(1)}, u32[]{:S(2)}, u32[]{:S(2)}) collective-permute-start(bf16[160,2304]{1,0:T(8,128)(2,1)S(1)} %slice_add_fusion.4), channel_id=1, source_target_pairs={{0,2},{1,3},{2,0},{3,1},{4,6},{5,7},{6,4},{7,5},{8,10},{9,11},{10,... | collective-permute-start | bytes 2211848 | tf_op jit(solution)/shard_map/ppermute | solution.py:351
  220.1 18.9 %collective-permute-start.14 = (bf16[160,2304]{1,0:T(8,128)(2,1)S(1)}, bf16[160,2304]{1,0:T(8,128)(2,1)S(1)}, u32[]{:S(2)}, u32[]{:S(2)}) collective-permute-start(bf16[160,2304]{1,0:T(8,128)(2,1)S(1)} %slice_add_fusion.5), channel_id=1, source_target_pairs={{0,4},{1,5},{2,6},{3,7},{4,0},{5,1},{6,2},{7,3},{8,12},{9,13},{10,... | collective-permute-start | bytes 2211848 | tf_op jit(solution)/shard_map/ppermute | solution.py:351
  237.6 1.3 copy-start.18
  238.9 0.9 copy-start.19
  359.7 7.2 %copy-start.4 = (bf16[8192,256]{1,0:T(8,128)(2,1)S(1)}, bf16[8192,256]{1,0:T(8,128)(2,1)}, u32[]{:S(2)}) copy-start(bf16[8192,256]{1,0:T(8,128)(2,1)} %get-tuple-element.57) | copy-start | bytes 12582916
Sparse Core Ops, SparseCore 0:
  9.8 42.6 all-gather.2
